TPU v7x, 512 devices: a whole 4x8x8 slice. The times are simulated.
512 devices in a mesh: section: 16 (over y, core), tensor: 32 (over x, z).
Axes of the slice: x: 4, y: 8, z: 8, core: 2. Of those that a mesh axis runs over, the one named last changes fastest.
Arguments:
- inputs: bfloat16 [2, 256, 12288], P(None, 'section', 'tensor'), may hold values from -6 to 6
- cotangent: bfloat16 [2, 256, 12288], P(None, 'section', 'tensor'), may hold values from -1.5 to 1.5
- up_weight: bfloat16 [12288, 24576], P('tensor', 'section'), may hold values from -0.04059494 to 0.067658235
- down_weight: bfloat16 [24576, 12288], P('section', 'tensor'), may hold values from -0.0390625 to 0.0390625
- norm_gain: float32 [12288], P('tensor'), may hold values from 0.25 to 2.8
Outputs:
- states: bfloat16 [2, 256, 12288], P(None, 'section', 'tensor')
- input_grads: bfloat16 [2, 256, 12288], P(None, 'section', 'tensor')
- grad_up: bfloat16 [12288, 24576], P('tensor', 'section')
- grad_down: bfloat16 [24576, 12288], P('section', 'tensor')
- grad_gain: float32 [12288], P('tensor')
All inputs are finite; a program needn't handle non-finite values.
Results may differ from a plain program's by a relative error of at most 0.03.
Values may be sent and summed in bfloat16 or wider, within the bound.
No kernel may reach another device: no remote copies, remote signals or barrier semaphores. Data moves between devices by JAX's collectives and lax.ppermute only.
A program may use at most 64 MiB of HBM per device.

v0:
```python
import jax
import jax.numpy as jnp
from jax import lax
from jax.sharding import PartitionSpec as P


D = 12288
X_COUNT = 4
Z_COUNT = 8
SECTIONS = 16
ROWS = 512
EXTRA = 128
CHUNK = ROWS // X_COUNT

norm_eps = 1e-05
gelu_c = 0.7978845608
cubic_c = 0.044715

f32 = jnp.float32
bf16 = jnp.bfloat16


Z_GROUPS = [[x * Z_COUNT + z for z in range(Z_COUNT)] for x in range(X_COUNT)]


def gelu_tanh(values):
    inner_arg = gelu_c * (values + cubic_c * values * values * values)
    return 0.5 * values * (1.0 + jnp.tanh(inner_arg))


def gelu_slope(values):
    tanh_value = jnp.tanh(gelu_c * (values + cubic_c * values * values * values))
    return 0.5 * (1.0 + tanh_value) + 0.5 * values * (1.0 - tanh_value * tanh_value) * gelu_c * (
        1.0 + 3.0 * cubic_c * values * values
    )


def shift_x(value, step):
    pairs = [
        (x * Z_COUNT + z, ((x + step) % X_COUNT) * Z_COUNT + z)
        for x in range(X_COUNT)
        for z in range(Z_COUNT)
    ]
    return lax.ppermute(value, "tensor", pairs)


def share(values, axis):
    count = lax.axis_size(axis)
    spread = jnp.broadcast_to(values[None], (count,) + values.shape)
    return added(lax.all_to_all(spread, axis, 0, 0, tiled=True))


def added(parts):
    total = parts[0].astype(f32)
    for k in range(1, parts.shape[0]):
        total = total + parts[k].astype(f32)
    return total


def split_three(values):
    high = lax.reduce_precision(values, 8, 7)
    rest = values - high
    middle = lax.reduce_precision(rest, 8, 7)
    low = rest - middle
    return high.astype(bf16), middle.astype(bf16), low.astype(bf16)


def rows_restored(chunks, x):
    total = jnp.zeros((ROWS, chunks[0].shape[1]), chunks[0].dtype)
    for k, chunk in enumerate(chunks):
        total = lax.dynamic_update_slice_in_dim(total, chunk, ((x + k) % X_COUNT) * CHUNK, axis=0)
    return total


def reduce_chunks(own, arrived):
    total = own.astype(f32)
    for part in arrived:
        total = total + part.astype(f32)
    pieces = total.astype(bf16).reshape(Z_COUNT, CHUNK // Z_COUNT, -1)
    return lax.all_to_all(pieces, "tensor", 0, 0, tiled=True, axis_index_groups=Z_GROUPS)


def per_device(inputs, cotangent, up_weight, down_weight, norm_gain):
    width = inputs.shape[2]
    hid_width = up_weight.shape[1]
    x = lax.axis_index("tensor") // Z_COUNT
    section = lax.axis_index("section")
    in_rows = inputs.reshape(32, width)
    grad_rows = cotangent.reshape(32, width)

    both = lax.all_gather(
        jnp.concatenate([in_rows, grad_rows], axis=0), "section", axis=0, tiled=True
    ).reshape(SECTIONS, 64, width)
    per_chunk = SECTIONS // X_COUNT

    def chunk_of(value, k, start):
        index = ((x + k) % X_COUNT) * per_chunk
        return lax.dynamic_slice(value, (index, start, 0), (per_chunk, 32, width)).reshape(CHUNK, width)

    g_chunks = [chunk_of(both, k, 32) for k in range(X_COUNT)]

    def grad_hidden_part(k):
        return lax.dot_general(
            g_chunks[k], down_weight, (((1,), (1,)), ((), ())), preferred_element_type=f32
        ).astype(bf16)

    dh_parts = {k: grad_hidden_part(k) for k in (2, 1, 3)}

    a_all = both[:, :32].reshape(ROWS, width)
    a_stats = a_all.astype(f32)
    gain_rows = jnp.stack(split_three(norm_gain))
    gain_up = jnp.sum(jnp.dot(gain_rows, up_weight, preferred_element_type=f32), axis=0)
    row_parts = jnp.concatenate(
        [
            jnp.sum(a_stats, axis=1).reshape(4, 128),
            jnp.sum(a_stats * a_stats, axis=1).reshape(4, 128),
            gain_up.reshape(12, 128),
        ],
        axis=0,
    )
    row_parts, dh_parts = lax.optimization_barrier((row_parts, dh_parts))
    dh_arrived = [shift_x(dh_parts[k], k) for k in (2, 1, 3)]
    summed = share(row_parts, "tensor")
    dh_own = lax.optimization_barrier(grad_hidden_part(0))
    gain_up = summed[8:].reshape(hid_width)
    mean = (summed[:4] / D).reshape(ROWS)
    scale = lax.rsqrt((summed[4:8] / D).reshape(ROWS) - mean * mean + norm_eps)
    normed = ((a_all.astype(f32) - mean[:, None]) * scale[:, None] * norm_gain).astype(bf16)
    normed_three = normed.reshape(SECTIONS, 32, width)
    normed_chunks = [chunk_of(normed_three, k, 0) for k in range(X_COUNT)]

    def pre_part(k):
        return jnp.dot(normed_chunks[k], up_weight, preferred_element_type=f32).astype(bf16)

    pre_arrived = [shift_x(pre_part(k), k) for k in (2, 1, 3)]
    pre_own = lax.optimization_barrier(pre_part(0))
    grad_hidden = reduce_chunks(dh_own, dh_arrived)
    pre = reduce_chunks(pre_own, pre_arrived)
    grad_hidden = added(grad_hidden)
    pre = added(pre)

    hidden = gelu_tanh(pre).astype(bf16)
    grad_pre = (grad_hidden * gelu_slope(pre)).astype(bf16)
    grad_pre_float = grad_pre.astype(f32)
    terms = split_three(jnp.sum(grad_pre_float * gain_up, axis=1, keepdims=True))
    terms = terms + split_three(jnp.sum(grad_pre_float * pre, axis=1, keepdims=True))
    lane = lax.broadcasted_iota(jnp.int32, (16, EXTRA), 1)
    extra = jnp.zeros((16, EXTRA), bf16)
    for k, term in enumerate(terms):
        extra = jnp.where(lane == k, term, extra)

    def gather_z(value):
        return lax.all_gather(value, "tensor", axis=0, tiled=True, axis_index_groups=Z_GROUPS)

    gathered = gather_z(jnp.concatenate([grad_pre, extra, hidden], axis=1))
    grad_pre_own = gathered[:, : hid_width + EXTRA]
    hidden_own = gathered[:, hid_width + EXTRA :]
    steps = (2, 1, 3)
    moved = {k: shift_x(grad_pre_own, (X_COUNT - k) % X_COUNT) for k in steps}
    wide_chunks = [grad_pre_own] + [moved[k] for k in (1, 2, 3)]
    moved = {k: shift_x(hidden_own, (X_COUNT - k) % X_COUNT) for k in steps}
    hidden_chunks = [hidden_own] + [moved[k] for k in (1, 2, 3)]
    grad_pre_chunks = [chunk[:, :hid_width] for chunk in wide_chunks]

    def grad_normed_part(k):
        return lax.dot_general(
            grad_pre_chunks[k], up_weight, (((1,), (1,)), ((), ())), preferred_element_type=f32
        ).astype(bf16)

    dn_part = rows_restored([grad_normed_part(k) for k in range(X_COUNT)], x)
    swapped = lax.all_to_all(dn_part.reshape(SECTIONS, 32, width), "section", 0, 0, tiled=True)
    dn_part, a_late = lax.optimization_barrier((dn_part, a_all))

    centred_all = (a_late.astype(f32) - mean[:, None]) * scale[:, None]
    gain_part = jnp.sum(dn_part.astype(f32) * centred_all, axis=0)
    gain_terms = jnp.concatenate(split_three(gain_part), axis=0).reshape(32, 36)
    gain_terms = jnp.pad(gain_terms, ((0, 0), (6, EXTRA - 42)))
    row_terms = rows_restored([chunk[:, hid_width:] for chunk in wide_chunks], x)
    beside = row_terms.reshape(SECTIONS, 32, EXTRA) + gain_terms[None]

    def out_part(k):
        return jnp.dot(hidden_chunks[k], down_weight, preferred_element_type=f32).astype(bf16)

    out_parts = rows_restored([out_part(k) for k in range(X_COUNT)], x)
    swapped_out = lax.all_to_all(
        jnp.concatenate([out_parts.reshape(SECTIONS, 32, width), beside], axis=2),
        "section",
        0,
        0,
        tiled=True,
    )

    grad_pre_rolled = jnp.concatenate(grad_pre_chunks, axis=0)
    normed_rolled = jnp.concatenate(normed_chunks, axis=0)
    grad_up = lax.dot_general(
        normed_rolled, grad_pre_rolled, (((0,), (0,)), ((), ())), preferred_element_type=f32
    ).astype(bf16)
    hidden_rolled = jnp.concatenate(hidden_chunks, axis=0)
    g_rolled = jnp.concatenate(g_chunks, axis=0)
    grad_down = lax.dot_general(
        hidden_rolled, g_rolled, (((0,), (0,)), ((), ())), preferred_element_type=f32
    ).astype(bf16)

    grad_normed = added(swapped)
    out_terms = added(swapped_out[:, :, :width])
    beside = added(swapped_out[:, :, width:])
    in_float = in_rows.astype(f32)
    states = (in_float + out_terms).astype(bf16)
    grad_gain = jnp.sum(beside[:, 6:42].reshape(3, width), axis=0)
    row_first = jnp.sum(beside[:, :3], axis=1, keepdims=True) / D
    row_second = jnp.sum(beside[:, 3:6], axis=1, keepdims=True) / D

    own_mean = lax.dynamic_slice_in_dim(mean, section * 32, 32, axis=0)[:, None]
    own_scale = lax.dynamic_slice_in_dim(scale, section * 32, 32, axis=0)[:, None]
    centred = (in_float - own_mean) * own_scale
    correction = grad_normed * norm_gain - row_first - centred * row_second
    input_grads = (grad_rows.astype(f32) + own_scale * correction).astype(bf16)
    return (
        states.reshape(inputs.shape),
        input_grads.reshape(inputs.shape),
        grad_up,
        grad_down,
        grad_gain,
    )


def solution(mesh):
    placed = (
        P(None, "section", "tensor"),
        P(None, "section", "tensor"),
        P("tensor", "section"),
        P("section", "tensor"),
        P("tensor"),
    )
    return jax.shard_map(
        per_device,
        mesh=mesh,
        in_specs=placed,
        out_specs=(
            P(None, "section", "tensor"),
            P(None, "section", "tensor"),
            P("tensor", "section"),
            P("section", "tensor"),
            P("tensor"),
        ),
        check_vma=False,
    )
```

profile of v0, /device:TPU:1, one launch (start us, length us, event | category | flops | bytes accessed | tf_op | source)
XLA Modules:
  0.0 223.2 jit_solution(3157165507122559558)
XLA Ops:
  0.8 0.8 reduce-precision_convert_fusion.3
  1.6 0.8 pad_maximum_fusion.2
  2.4 23.5 %all_gather.6 = bf16[1024,384]{1,0:T(8,128)(2,1)S(1)} all-gather(bf16[64,384]{1,0:T(8,128)(2,1)S(1)} %pad_maximum_fusion.2), channel_id=1, replica_groups=mesh['section'=16,'tensor'=32] {'section'}, dimensions={0}, use_global_device_ids=true | all-gather | bytes 835584 | tf_op jit(solution)/shard_map/all_gather | solution.py:91
  26.2 0.7 constant_dynamic-slice_fusion.7
  27.0 1.3 convolution_convert_fusion.8
  28.2 1.3 convolution_convert_fusion.7
  29.5 1.2 convolution_convert_fusion.6
  31.0 0.8 broadcast_in_dim.56
  31.8 10.5 %all-to-all-start.1 = ((f32[32,20,128]{2,1,0:T(8,128)}), f32[32,20,128]{2,1,0:T(8,128)S(1)}, u32[]{:S(2)}, u32[]{:S(2)}) async-start(f32[32,20,128]{2,1,0:T(8,128)} %broadcast_in_dim.56), calls=%async_computation.1 | async-start | bytes 786432 | tf_op jit(solution)/shard_map/all_to_all | solution.py:50
  42.3 4.4 %collective-permute-start.2 = (bf16[128,1536]{1,0:T(8,128)(2,1)}, bf16[128,1536]{1,0:T(8,128)(2,1)}, u32[]{:S(2)}, u32[]{:S(2)}) collective-permute-start(bf16[128,1536]{1,0:T(8,128)(2,1)} %convolution_convert_fusion.6), channel_id=1, source_target_pairs={{0,24},{1,25},{2,26},{3,27},{4,28},{5,29},{6,30},{7,31},{8,0},{9,1... | collective-permute-start | bytes 1179656 | tf_op jit(solution)/shard_map/ppermute | solution.py:44
  46.7 1.9 collective-permute-start.1
  48.6 3.6 %collective-permute-start = (bf16[128,1536]{1,0:T(8,128)(2,1)}, bf16[128,1536]{1,0:T(8,128)(2,1)}, u32[]{:S(2)}, u32[]{:S(2)}) collective-permute-start(bf16[128,1536]{1,0:T(8,128)(2,1)} %convolution_convert_fusion.7), channel_id=1, source_target_pairs={{0,16},{1,17},{2,18},{3,19},{4,20},{5,21},{6,22},{7,23},{8,24},{9,... | collective-permute-start | bytes 1179656 | tf_op jit(solution)/shard_map/ppermute | solution.py:44
  52.2 2.2 convolution_convert_fusion.9
  55.4 0.7 constant_dynamic-slice_fusion.3
  56.1 1.1 convolution_convert_fusion.2
  57.2 4.0 %collective-permute-start.5 = (bf16[128,1536]{1,0:T(8,128)(2,1)}, bf16[128,1536]{1,0:T(8,128)(2,1)}, u32[]{:S(2)}, u32[]{:S(2)}) collective-permute-start(bf16[128,1536]{1,0:T(8,128)(2,1)} %convolution_convert_fusion.2), channel_id=1, source_target_pairs={{0,24},{1,25},{2,26},{3,27},{4,28},{5,29},{6,30},{7,31},{8,0},{9,1... | collective-permute-start | bytes 1179656 | tf_op jit(solution)/shard_map/ppermute | solution.py:44
  61.2 1.1 convolution_convert_fusion.3
  62.3 2.0 collective-permute-start.4
  64.4 1.1 convolution_convert_fusion.4
  65.5 3.5 %collective-permute-start.3 = (bf16[128,1536]{1,0:T(8,128)(2,1)}, bf16[128,1536]{1,0:T(8,128)(2,1)}, u32[]{:S(2)}, u32[]{:S(2)}) collective-permute-start(bf16[128,1536]{1,0:T(8,128)(2,1)} %convolution_convert_fusion.4), channel_id=1, source_target_pairs={{0,16},{1,17},{2,18},{3,19},{4,20},{5,21},{6,22},{7,23},{8,24},{9,... | collective-permute-start | bytes 1179656 | tf_op jit(solution)/shard_map/ppermute | solution.py:44
  69.1 1.4 collective-permute-done
  70.5 2.2 add_convert_fusion.1
  72.7 5.1 %all-to-all-start = ((bf16[8,16,1536]{2,1,0:T(8,128)(2,1)}), bf16[8,16,1536]{2,1,0:T(8,128)(2,1)S(1)}, u32[]{:S(2)}, u32[]{:S(2)}) async-start(bf16[8,16,1536]{2,1,0:T(8,128)(2,1)} %bitcast.186), calls=%async_computation | async-start | bytes 786432 | tf_op jit(solution)/shard_map/all_to_all | solution.py:80
  77.8 1.3 convolution_convert_fusion.5
  79.4 8.0 %collective-permute-done.3 = bf16[128,1536]{1,0:T(8,128)(2,1)} collective-permute-done((bf16[128,1536]{1,0:T(8,128)(2,1)}, bf16[128,1536]{1,0:T(8,128)(2,1)}, u32[]{:S(2)}, u32[]{:S(2)}) %collective-permute-start.3) | collective-permute-done | bytes 393248 | tf_op jit(solution)/shard_map/ppermute | solution.py:44
  87.4 2.2 add_convert_fusion
  89.6 0.6 all-to-all-done
  90.2 4.6 %all-to-all-start.2 = ((bf16[8,16,1536]{2,1,0:T(8,128)(2,1)}), bf16[8,16,1536]{2,1,0:T(8,128)(2,1)}, u32[]{:S(2)}, u32[]{:S(2)}) async-start(bf16[8,16,1536]{2,1,0:T(8,128)(2,1)} %bitcast.185), calls=%async_computation.2 | async-start | bytes 786432 | tf_op jit(solution)/shard_map/all_to_all | solution.py:80
  95.2 0.8 slice.488
  96.0 0.6 fusion.82
  96.6 9.9 %all-to-all-done.2 = bf16[8,16,1536]{2,1,0:T(8,128)(2,1)} async-done(((bf16[8,16,1536]{2,1,0:T(8,128)(2,1)}), bf16[8,16,1536]{2,1,0:T(8,128)(2,1)}, u32[]{:S(2)}, u32[]{:S(2)}) %all-to-all-start.2) | async-done | bytes 393248 | tf_op jit(solution)/shard_map/all_to_all | solution.py:80
  106.5 1.3 fusion.40
  107.8 0.8 select_select_fusion
  108.6 20.9 %all_gather.7 = bf16[128,3200]{1,0:T(8,128)(2,1)S(1)} all-gather(bf16[16,3200]{1,0:T(8,128)(2,1)S(1)} %pad_maximum_fusion.1), channel_id=1, replica_groups={{0,1,2,3,4,5,6,7},{8,9,10,11,12,13,14,15},{16,17,18,19,20,21,22,23},{24..., dimensions={0}, use_global_device_ids=true | all-gather | bytes 921600 | tf_op jit(solution)/shard_map/all_gather | solution.py:153
  129.5 1.9 collective-permute-start.9
  131.5 2.5 %collective-permute-start.10 = (bf16[128,1664]{1,0:T(8,128)(2,1)S(1)}, bf16[128,1664]{1,0:T(8,128)(2,1)S(1)}, u32[]{:S(2)}, u32[]{:S(2)}) collective-permute-start(bf16[128,1664]{1,0:T(8,128)(2,1)S(1)} %slice.542), channel_id=1, source_target_pairs={{0,16},{1,17},{2,18},{3,19},{4,20},{5,21},{6,22},{7,23},{8,24},{9,... | collective-permute-start | bytes 1277960 | tf_op jit(solution)/shard_map/ppermute | solution.py:44
  133.9 2.8 %collective-permute-start.11 = (bf16[128,1664]{1,0:T(8,128)(2,1)S(1)}, bf16[128,1664]{1,0:T(8,128)(2,1)S(1)}, u32[]{:S(2)}, u32[]{:S(2)}) collective-permute-start(bf16[128,1664]{1,0:T(8,128)(2,1)S(1)} %slice.542), channel_id=1, source_target_pairs={{0,8},{1,9},{2,10},{3,11},{4,12},{5,13},{6,14},{7,15},{8,16},{9,17... | collective-permute-start | bytes 1277960 | tf_op jit(solution)/shard_map/ppermute | solution.py:44
  136.8 0.8 fusion.95
  137.6 4.3 %collective-permute-start.6 = (bf16[128,1536]{1,0:T(8,128)(2,1)S(1)}, bf16[128,1536]{1,0:T(8,128)(2,1)S(1)}, u32[]{:S(2)}, u32[]{:S(2)}) collective-permute-start(bf16[128,1536]{1,0:T(8,128)(2,1)S(1)} %get-tuple-element.26), channel_id=1, source_target_pairs={{0,24},{1,25},{2,26},{3,27},{4,28},{5,29},{6,30},{7,31},{8,0},{9,1... | collective-permute-start | bytes 1179656 | tf_op jit(solution)/shard_map/ppermute | solution.py:44
  141.9 3.1 %collective-permute-start.7 = (bf16[128,1536]{1,0:T(8,128)(2,1)S(1)}, bf16[128,1536]{1,0:T(8,128)(2,1)S(1)}, u32[]{:S(2)}, u32[]{:S(2)}) collective-permute-start(bf16[128,1536]{1,0:T(8,128)(2,1)S(1)} %get-tuple-element.26), channel_id=1, source_target_pairs={{0,16},{1,17},{2,18},{3,19},{4,20},{5,21},{6,22},{7,23},{8,24},{9,... | collective-permute-start | bytes 1179656 | tf_op jit(solution)/shard_map/ppermute | solution.py:44
  145.0 0.8 broadcast.88.clone
  145.8 1.2 fusion.17
  147.4 3.8 %collective-permute-done.6 = bf16[128,1536]{1,0:T(8,128)(2,1)S(1)} collective-permute-done((bf16[128,1536]{1,0:T(8,128)(2,1)S(1)}, bf16[128,1536]{1,0:T(8,128)(2,1)S(1)}, u32[]{:S(2)}, u32[]{:S(2)}) %collective-permute-start.6) | collective-permute-done | bytes 393248 | tf_op jit(solution)/shard_map/ppermute | solution.py:44
  151.2 3.1 %collective-permute-start.8 = (bf16[128,1536]{1,0:T(8,128)(2,1)S(1)}, bf16[128,1536]{1,0:T(8,128)(2,1)S(1)}, u32[]{:S(2)}, u32[]{:S(2)}) collective-permute-start(bf16[128,1536]{1,0:T(8,128)(2,1)S(1)} %get-tuple-element.26), channel_id=1, source_target_pairs={{0,8},{1,9},{2,10},{3,11},{4,12},{5,13},{6,14},{7,15},{8,16},{9,17... | collective-permute-start | bytes 1179656 | tf_op jit(solution)/shard_map/ppermute | solution.py:44
  154.7 1.7 collective-permute-done.7
  156.9 10.9 %collective-permute-done.8 = bf16[128,1536]{1,0:T(8,128)(2,1)S(1)} collective-permute-done((bf16[128,1536]{1,0:T(8,128)(2,1)S(1)}, bf16[128,1536]{1,0:T(8,128)(2,1)S(1)}, u32[]{:S(2)}, u32[]{:S(2)}) %collective-permute-start.8) | collective-permute-done | bytes 393248 | tf_op jit(solution)/shard_map/ppermute | solution.py:44
  168.6 0.7 copy-done.5
  169.3 1.2 fusion.16
  170.5 1.2 fusion.15
  171.6 0.7 copy-done.2
  172.4 1.2 fusion.14
  173.5 13.0 %all-to-all-start.4 = ((bf16[16,32,384]{2,1,0:T(8,128)(2,1)}), bf16[16,32,384]{2,1,0:T(8,128)(2,1)}, u32[]{:S(2)}, u32[]{:S(2)}) async-start(bf16[16,32,384]{2,1,0:T(8,128)(2,1)} %bitcast.40), calls=%async_computation.4 | async-start | bytes 786432 | tf_op jit(solution)/shard_map/all_to_all | solution.py:171
  186.6 1.3 multiply_reduce_fusion
  188.2 1.9 pad_maximum_fusion
  190.2 11.0 %all-to-all-done.4 = bf16[16,32,384]{2,1,0:T(8,128)(2,1)} async-done(((bf16[16,32,384]{2,1,0:T(8,128)(2,1)}), bf16[16,32,384]{2,1,0:T(8,128)(2,1)}, u32[]{:S(2)}, u32[]{:S(2)}) %all-to-all-start.4) | async-done | bytes 393248 | tf_op jit(solution)/shard_map/all_to_all | solution.py:171
  201.2 3.5 %all-to-all-start.3 = ((bf16[16,32,512]{2,1,0:T(8,128)(2,1)}), bf16[16,32,512]{2,1,0:T(8,128)(2,1)S(1)}, u32[]{:S(2)}, u32[]{:S(2)}) async-start(bf16[16,32,512]{2,1,0:T(8,128)(2,1)} %pad_maximum_fusion), calls=%async_computation.3 | async-start | bytes 1048576 | tf_op jit(solution)/shard_map/all_to_all | solution.py:185
  205.0 3.4 %convolution_convert_fusion = bf16[1536,384]{1,0:T(8,128)(2,1)} fusion(bf16[128,1536]{1,0:T(8,128)(2,1)} %copy-done.25, bf16[128,1536]{1,0:T(8,128)(2,1)} %copy-done.24, bf16[128,1536]{1,0:T(8,128)(2,1)} %copy-done.23, bf16[128,1536]{1,0:T(8,128)(2,1)} %copy-done.22, bf16[128,384]{1,0:T(8,128)(2,1)S(1)} %bitcast.191, bf16[128,384]{1,0:T(8,128)(2,1)S(1)} %bitcast.193, ...), kind=kOutput, calls=%fused_computation | convolution fusion | flops 612433920 | bytes 3145728 | tf_op jit(solution)/shard_map/dot_general | solution.py:200
  208.5 0.9 slice-done
  209.6 1.8 convolution_convert_fusion.1
  211.5 0.7 slice.581
  212.2 1.0 add_add_fusion.1
  213.2 8.1 %all-to-all-done.3 = bf16[16,32,512]{2,1,0:T(8,128)(2,1)S(1)} async-done(((bf16[16,32,512]{2,1,0:T(8,128)(2,1)}), bf16[16,32,512]{2,1,0:T(8,128)(2,1)S(1)}, u32[]{:S(2)}, u32[]{:S(2)}) %all-to-all-start.3) | async-done | bytes 524320 | tf_op jit(solution)/shard_map/all_to_all | solution.py:185
  221.8 0.6 reduce_sum.89
  222.5 0.7 fusion.55
  (122 shorter events, 6.2 us)
Async XLA Ops:
  0.6 30.1 %copy-start = (bf16[384,1536]{1,0:T(8,128)(2,1)S(1)}, bf16[384,1536]{1,0:T(8,128)(2,1)}, u32[]{:S(2)}) copy-start(bf16[384,1536]{1,0:T(8,128)(2,1)} %param.7) | copy-start | bytes 3538948
  0.6 26.3 %copy-start.1 = (bf16[1536,384]{1,0:T(8,128)(2,1)S(1)}, bf16[1536,384]{1,0:T(8,128)(2,1)}, u32[]{:S(2)}) copy-start(bf16[1536,384]{1,0:T(8,128)(2,1)} %param.8) | copy-start | bytes 3538948
  26.9 2.5 %copy-start.10 = (bf16[4,32,384]{2,1,0:T(8,128)(2,1)}, bf16[4,32,384]{2,1,0:T(8,128)(2,1)S(1)}, u32[]{:S(2)}) copy-start(bf16[4,32,384]{2,1,0:T(8,128)(2,1)S(1)} %get-tuple-element.29) | copy-start | bytes 294916
  26.9 2.5 %copy-start.12 = (bf16[4,32,384]{2,1,0:T(8,128)(2,1)}, bf16[4,32,384]{2,1,0:T(8,128)(2,1)S(1)}, u32[]{:S(2)}) copy-start(bf16[4,32,384]{2,1,0:T(8,128)(2,1)S(1)} %get-tuple-element.30) | copy-start | bytes 294916
  27.0 2.5 %copy-start.8 = (bf16[4,32,384]{2,1,0:T(8,128)(2,1)}, bf16[4,32,384]{2,1,0:T(8,128)(2,1)S(1)}, u32[]{:S(2)}) copy-start(bf16[4,32,384]{2,1,0:T(8,128)(2,1)S(1)} %get-tuple-element.28) | copy-start | bytes 294916
  31.8 22.6 %all-to-all-start.1 = ((f32[32,20,128]{2,1,0:T(8,128)}), f32[32,20,128]{2,1,0:T(8,128)S(1)}, u32[]{:S(2)}, u32[]{:S(2)}) async-start(f32[32,20,128]{2,1,0:T(8,128)} %broadcast_in_dim.56), calls=%async_computation.1 | async-start | bytes 786432 | tf_op jit(solution)/shard_map/all_to_all | solution.py:50
  42.3 12.9 %copy-start.28 = (f32[384]{0:T(512)S(1)}, f32[384]{0:T(512)}, u32[]{:S(2)}) copy-start(f32[384]{0:T(512)} %param.9) | copy-start | bytes 4612
  42.3 23.3 %collective-permute-start.2 = (bf16[128,1536]{1,0:T(8,128)(2,1)}, bf16[128,1536]{1,0:T(8,128)(2,1)}, u32[]{:S(2)}, u32[]{:S(2)}) collective-permute-start(bf16[128,1536]{1,0:T(8,128)(2,1)} %convolution_convert_fusion.6), channel_id=1, source_target_pairs={{0,24},{1,25},{2,26},{3,27},{4,28},{5,29},{6,30},{7,31},{8,0},{9,1... | collective-permute-start | bytes 1179656 | tf_op jit(solution)/shard_map/ppermute | solution.py:44
  46.7 22.4 %collective-permute-start.1 = (bf16[128,1536]{1,0:T(8,128)(2,1)}, bf16[128,1536]{1,0:T(8,128)(2,1)}, u32[]{:S(2)}, u32[]{:S(2)}) collective-permute-start(bf16[128,1536]{1,0:T(8,128)(2,1)} %convolution_convert_fusion.8), channel_id=1, source_target_pairs={{0,8},{1,9},{2,10},{3,11},{4,12},{5,13},{6,14},{7,15},{8,16},{9,17... | collective-permute-start | bytes 1179656 | tf_op jit(solution)/shard_map/ppermute | solution.py:44
  48.6 21.9 %collective-permute-start = (bf16[128,1536]{1,0:T(8,128)(2,1)}, bf16[128,1536]{1,0:T(8,128)(2,1)}, u32[]{:S(2)}, u32[]{:S(2)}) collective-permute-start(bf16[128,1536]{1,0:T(8,128)(2,1)} %convolution_convert_fusion.7), channel_id=1, source_target_pairs={{0,16},{1,17},{2,18},{3,19},{4,20},{5,21},{6,22},{7,23},{8,24},{9,... | collective-permute-start | bytes 1179656 | tf_op jit(solution)/shard_map/ppermute | solution.py:44
  56.1 6.2 %copy-start.15 = (bf16[4,32,384]{2,1,0:T(8,128)(2,1)}, bf16[4,32,384]{2,1,0:T(8,128)(2,1)S(1)}, u32[]{:S(2)}) copy-start(bf16[4,32,384]{2,1,0:T(8,128)(2,1)S(1)} %get-tuple-element.32) | copy-start | bytes 294916
  56.1 6.2 %copy-start.17 = (bf16[4,32,384]{2,1,0:T(8,128)(2,1)}, bf16[4,32,384]{2,1,0:T(8,128)(2,1)S(1)}, u32[]{:S(2)}) copy-start(bf16[4,32,384]{2,1,0:T(8,128)(2,1)S(1)} %get-tuple-element.33) | copy-start | bytes 294916
  56.1 8.3 %copy-start.19 = (bf16[4,32,384]{2,1,0:T(8,128)(2,1)}, bf16[4,32,384]{2,1,0:T(8,128)(2,1)S(1)}, u32[]{:S(2)}) copy-start(bf16[4,32,384]{2,1,0:T(8,128)(2,1)S(1)} %get-tuple-element.34) | copy-start | bytes 294916
  57.2 21.9 %collective-permute-start.5 = (bf16[128,1536]{1,0:T(8,128)(2,1)}, bf16[128,1536]{1,0:T(8,128)(2,1)}, u32[]{:S(2)}, u32[]{:S(2)}) collective-permute-start(bf16[128,1536]{1,0:T(8,128)(2,1)} %convolution_convert_fusion.2), channel_id=1, source_target_pairs={{0,24},{1,25},{2,26},{3,27},{4,28},{5,29},{6,30},{7,31},{8,0},{9,1... | collective-permute-start | bytes 1179656 | tf_op jit(solution)/shard_map/ppermute | solution.py:44
  62.3 8.2 %copy-start.6 = (bf16[128,1536]{1,0:T(8,128)(2,1)S(1)}, bf16[128,1536]{1,0:T(8,128)(2,1)}, u32[]{:S(2)}) copy-start(bf16[128,1536]{1,0:T(8,128)(2,1)} %convolution_convert_fusion.9) | copy-start | bytes 1179652
  62.3 17.1 %collective-permute-start.4 = (bf16[128,1536]{1,0:T(8,128)(2,1)}, bf16[128,1536]{1,0:T(8,128)(2,1)}, u32[]{:S(2)}, u32[]{:S(2)}) collective-permute-start(bf16[128,1536]{1,0:T(8,128)(2,1)} %convolution_convert_fusion.3), channel_id=1, source_target_pairs={{0,8},{1,9},{2,10},{3,11},{4,12},{5,13},{6,14},{7,15},{8,16},{9,17... | collective-permute-start | bytes 1179656 | tf_op jit(solution)/shard_map/ppermute | solution.py:44
  65.5 21.9 %collective-permute-start.3 = (bf16[128,1536]{1,0:T(8,128)(2,1)}, bf16[128,1536]{1,0:T(8,128)(2,1)}, u32[]{:S(2)}, u32[]{:S(2)}) collective-permute-start(bf16[128,1536]{1,0:T(8,128)(2,1)} %convolution_convert_fusion.4), channel_id=1, source_target_pairs={{0,16},{1,17},{2,18},{3,19},{4,20},{5,21},{6,22},{7,23},{8,24},{9,... | collective-permute-start | bytes 1179656 | tf_op jit(solution)/shard_map/ppermute | solution.py:44
  72.7 17.5 %all-to-all-start = ((bf16[8,16,1536]{2,1,0:T(8,128)(2,1)}), bf16[8,16,1536]{2,1,0:T(8,128)(2,1)S(1)}, u32[]{:S(2)}, u32[]{:S(2)}) async-start(bf16[8,16,1536]{2,1,0:T(8,128)(2,1)} %bitcast.186), calls=%async_computation | async-start | bytes 786432 | tf_op jit(solution)/shard_map/all_to_all | solution.py:80
  90.2 16.3 %all-to-all-start.2 = ((bf16[8,16,1536]{2,1,0:T(8,128)(2,1)}), bf16[8,16,1536]{2,1,0:T(8,128)(2,1)}, u32[]{:S(2)}, u32[]{:S(2)}) async-start(bf16[8,16,1536]{2,1,0:T(8,128)(2,1)} %bitcast.185), calls=%async_computation.2 | async-start | bytes 786432 | tf_op jit(solution)/shard_map/all_to_all | solution.py:80
  129.5 39.8 %collective-permute-start.9 = (bf16[128,1664]{1,0:T(8,128)(2,1)S(1)}, bf16[128,1664]{1,0:T(8,128)(2,1)S(1)}, u32[]{:S(2)}, u32[]{:S(2)}) collective-permute-start(bf16[128,1664]{1,0:T(8,128)(2,1)S(1)} %slice.542), channel_id=1, source_target_pairs={{0,24},{1,25},{2,26},{3,27},{4,28},{5,29},{6,30},{7,31},{8,0},{9,1... | collective-permute-start | bytes 1277960 | tf_op jit(solution)/shard_map/ppermute | solution.py:44
  131.5 39.0 %collective-permute-start.10 = (bf16[128,1664]{1,0:T(8,128)(2,1)S(1)}, bf16[128,1664]{1,0:T(8,128)(2,1)S(1)}, u32[]{:S(2)}, u32[]{:S(2)}) collective-permute-start(bf16[128,1664]{1,0:T(8,128)(2,1)S(1)} %slice.542), channel_id=1, source_target_pairs={{0,16},{1,17},{2,18},{3,19},{4,20},{5,21},{6,22},{7,23},{8,24},{9,... | collective-permute-start | bytes 1277960 | tf_op jit(solution)/shard_map/ppermute | solution.py:44
  133.9 37.7 %collective-permute-start.11 = (bf16[128,1664]{1,0:T(8,128)(2,1)S(1)}, bf16[128,1664]{1,0:T(8,128)(2,1)S(1)}, u32[]{:S(2)}, u32[]{:S(2)}) collective-permute-start(bf16[128,1664]{1,0:T(8,128)(2,1)S(1)} %slice.542), channel_id=1, source_target_pairs={{0,8},{1,9},{2,10},{3,11},{4,12},{5,13},{6,14},{7,15},{8,16},{9,17... | collective-permute-start | bytes 1277960 | tf_op jit(solution)/shard_map/ppermute | solution.py:44
  137.6 13.6 %copy-start.22 = (bf16[128,1536]{1,0:T(8,128)(2,1)}, bf16[128,1536]{1,0:T(8,128)(2,1)S(1)}, u32[]{:S(2)}) copy-start(bf16[128,1536]{1,0:T(8,128)(2,1)S(1)} %get-tuple-element.26) | copy-start | bytes 1179652
  137.6 13.6 %collective-permute-start.6 = (bf16[128,1536]{1,0:T(8,128)(2,1)S(1)}, bf16[128,1536]{1,0:T(8,128)(2,1)S(1)}, u32[]{:S(2)}, u32[]{:S(2)}) collective-permute-start(bf16[128,1536]{1,0:T(8,128)(2,1)S(1)} %get-tuple-element.26), channel_id=1, source_target_pairs={{0,24},{1,25},{2,26},{3,27},{4,28},{5,29},{6,30},{7,31},{8,0},{9,1... | collective-permute-start | bytes 1179656 | tf_op jit(solution)/shard_map/ppermute | solution.py:44
  141.9 14.6 %collective-permute-start.7 = (bf16[128,1536]{1,0:T(8,128)(2,1)S(1)}, bf16[128,1536]{1,0:T(8,128)(2,1)S(1)}, u32[]{:S(2)}, u32[]{:S(2)}) collective-permute-start(bf16[128,1536]{1,0:T(8,128)(2,1)S(1)} %get-tuple-element.26), channel_id=1, source_target_pairs={{0,16},{1,17},{2,18},{3,19},{4,20},{5,21},{6,22},{7,23},{8,24},{9,... | collective-permute-start | bytes 1179656 | tf_op jit(solution)/shard_map/ppermute | solution.py:44
  151.2 5.6 %copy-start.23 = (bf16[128,1536]{1,0:T(8,128)(2,1)}, bf16[128,1536]{1,0:T(8,128)(2,1)S(1)}, u32[]{:S(2)}) copy-start(bf16[128,1536]{1,0:T(8,128)(2,1)S(1)} %collective-permute-done.6) | copy-start | bytes 1179652
  151.2 16.5 %collective-permute-start.8 = (bf16[128,1536]{1,0:T(8,128)(2,1)S(1)}, bf16[128,1536]{1,0:T(8,128)(2,1)S(1)}, u32[]{:S(2)}, u32[]{:S(2)}) collective-permute-start(bf16[128,1536]{1,0:T(8,128)(2,1)S(1)} %get-tuple-element.26), channel_id=1, source_target_pairs={{0,8},{1,9},{2,10},{3,11},{4,12},{5,13},{6,14},{7,15},{8,16},{9,17... | collective-permute-start | bytes 1179656 | tf_op jit(solution)/shard_map/ppermute | solution.py:44
  156.5 11.7 %copy-start.24 = (bf16[128,1536]{1,0:T(8,128)(2,1)}, bf16[128,1536]{1,0:T(8,128)(2,1)S(1)}, u32[]{:S(2)}) copy-start(bf16[128,1536]{1,0:T(8,128)(2,1)S(1)} %collective-permute-done.7) | copy-start | bytes 1179652
  167.8 0.8 copy-start.25
  168.6 0.7 copy-start.5
  171.6 15.0 %copy-start.4 = (bf16[16,32,384]{2,1,0:T(8,128)(2,1)S(1)}, bf16[16,32,384]{2,1,0:T(8,128)(2,1)}, u32[]{:S(2)}) copy-start(bf16[16,32,384]{2,1,0:T(8,128)(2,1)} %slice.488) | copy-start | bytes 1179652
  171.6 15.0 %copy-start.29 = (f32[512]{0:T(512)S(1)}, f32[512]{0:T(512)}, u32[]{:S(2)}) copy-start(f32[512]{0:T(512)} %get-tuple-element.37) | copy-start | bytes 6148
  171.6 15.0 %copy-start.30 = (f32[512]{0:T(512)S(1)}, f32[512]{0:T(512)}, u32[]{:S(2)}) copy-start(f32[512]{0:T(512)} %fusion.82) | copy-start | bytes 6148
  171.6 0.8 copy-start.2
  173.5 14.6 %copy-start.3 = (bf16[128,1664]{1,0:T(8,128)(2,1)S(1)}, bf16[128,1664]{1,0:T(8,128)(2,1)}, u32[]{:S(2)}) copy-start(bf16[128,1664]{1,0:T(8,128)(2,1)} %copy-done.2) | copy-start | bytes 1277956
  173.5 27.6 %all-to-all-start.4 = ((bf16[16,32,384]{2,1,0:T(8,128)(2,1)}), bf16[16,32,384]{2,1,0:T(8,128)(2,1)}, u32[]{:S(2)}, u32[]{:S(2)}) async-start(bf16[16,32,384]{2,1,0:T(8,128)(2,1)} %bitcast.40), calls=%async_computation.4 | async-start | bytes 786432 | tf_op jit(solution)/shard_map/all_to_all | solution.py:171
  188.2 16.8 %copy-start.7 = (bf16[4,32,384]{2,1,0:T(8,128)(2,1)S(1)}, bf16[4,32,384]{2,1,0:T(8,128)(2,1)}, u32[]{:S(2)}) copy-start(bf16[4,32,384]{2,1,0:T(8,128)(2,1)} %get-tuple-element.27) | copy-start | bytes 294916
  188.2 16.8 %copy-start.9 = (bf16[4,32,384]{2,1,0:T(8,128)(2,1)S(1)}, bf16[4,32,384]{2,1,0:T(8,128)(2,1)}, u32[]{:S(2)}) copy-start(bf16[4,32,384]{2,1,0:T(8,128)(2,1)} %copy-done.8) | copy-start | bytes 294916
  188.2 16.8 %copy-start.11 = (bf16[4,32,384]{2,1,0:T(8,128)(2,1)S(1)}, bf16[4,32,384]{2,1,0:T(8,128)(2,1)}, u32[]{:S(2)}) copy-start(bf16[4,32,384]{2,1,0:T(8,128)(2,1)} %copy-done.10) | copy-start | bytes 294916
  188.2 16.7 %copy-start.13 = (bf16[4,32,384]{2,1,0:T(8,128)(2,1)S(1)}, bf16[4,32,384]{2,1,0:T(8,128)(2,1)}, u32[]{:S(2)}) copy-start(bf16[4,32,384]{2,1,0:T(8,128)(2,1)} %copy-done.12) | copy-start | bytes 294916
  201.2 20.1 %all-to-all-start.3 = ((bf16[16,32,512]{2,1,0:T(8,128)(2,1)}), bf16[16,32,512]{2,1,0:T(8,128)(2,1)S(1)}, u32[]{:S(2)}, u32[]{:S(2)}) async-start(bf16[16,32,512]{2,1,0:T(8,128)(2,1)} %pad_maximum_fusion), calls=%async_computation.3 | async-start | bytes 1048576 | tf_op jit(solution)/shard_map/all_to_all | solution.py:185
  208.4 1.0 slice-start
  208.4 1.0 copy-start.14
  208.4 1.1 copy-start.16
  208.4 1.1 copy-start.18
  208.4 1.1 copy-start.20
  208.4 1.2 copy-start.21
  211.5 11.0 %copy-start.26 = (bf16[2,16,384]{2,1,0:T(8,128)(2,1)S(1)}, bf16[2,16,384]{2,1,0:T(8,128)(2,1)}, u32[]{:S(2)}) copy-start(bf16[2,16,384]{2,1,0:T(8,128)(2,1)} %param.5) | copy-start | bytes 73732
  211.5 11.1 %copy-start.27 = (bf16[2,16,384]{2,1,0:T(8,128)(2,1)S(1)}, bf16[2,16,384]{2,1,0:T(8,128)(2,1)}, u32[]{:S(2)}) copy-start(bf16[2,16,384]{2,1,0:T(8,128)(2,1)} %param.6) | copy-start | bytes 73732
where the time goes:
time: 225 us; the launch traced here: 223 us
  starting transfers between devices  73.8 us (33%)
  waiting for transfers between devices  55.8 us (25%)
  blocking collectives  44.4 us (20%)
  matrix products  22.2 us (10%)
  other arithmetic  16 us (7%)
  local copies, waits for them, and re-layouts  9.83 us (4%)
    ppermute x12, starting transfers between devices, shift_x(): return lax.ppermute(value, 'tensor', pairs)  37.1 us
    ppermute x12, waiting for transfers between devices, shift_x(): return lax.ppermute(value, 'tensor', pairs)  26.2 us
    all_gather x1, blocking collectives, per_device(): lax.all_gather(jnp.concatenate([in_rows, grad_rows], axis=0), 'section',...  23.5 us
    all_gather x1, blocking collectives, gather_z(): lax.all_gather(value, 'tensor', axis=0, tiled=True, axis_index_groups=Z_G...  20.9 us
    all_to_all x1, starting transfers between devices, per_device(): lax.all_to_all(dn_part.reshape(SECTIONS, 32, width), 'section', 0, 0, til...  13 us
    all_to_all x1, waiting for transfers between devices, per_device(): lax.all_to_all(dn_part.reshape(SECTIONS, 32, width), 'section', 0, 0, til...  11 us
    all_to_all x1, starting transfers between devices, share(): return added(lax.all_to_all(spread, axis, 0, 0, tiled=True))  10.5 us
    all_to_all x2, waiting for transfers between devices, reduce_chunks(): lax.all_to_all(pieces, 'tensor', 0, 0, tiled=True, axis_index_groups=Z_GR...  10.4 us
  transfers between devices with their start and end apart: 17, of which 10 were waited for; matrix products, arithmetic and copies ran while one was open for 14% of the time, Pallas kernels for 0%

commit v1 on v0

--- a/solution.py
+++ b/solution.py
@@ -1,6 +1,8 @@
 import jax
 import jax.numpy as jnp
 from jax import lax
+from jax.experimental import pallas as pl
+from jax.experimental.pallas import tpu as pltpu
 from jax.sharding import PartitionSpec as P
 
 
@@ -65,19 +67,75 @@
     return high.astype(bf16), middle.astype(bf16), low.astype(bf16)
 
 
-def rows_restored(chunks, x):
-    total = jnp.zeros((ROWS, chunks[0].shape[1]), chunks[0].dtype)
-    for k, chunk in enumerate(chunks):
-        total = lax.dynamic_update_slice_in_dim(total, chunk, ((x + k) % X_COUNT) * CHUNK, axis=0)
-    return total
-
-
 def reduce_chunks(own, arrived):
     total = own.astype(f32)
     for part in arrived:
         total = total + part.astype(f32)
     pieces = total.astype(bf16).reshape(Z_COUNT, CHUNK // Z_COUNT, -1)
     return lax.all_to_all(pieces, "tensor", 0, 0, tiled=True, axis_index_groups=Z_GROUPS)
+
+
+def spread_z(value):
+    copies = jnp.broadcast_to(value[None], (Z_COUNT,) + value.shape)
+    rows = lax.all_to_all(copies, "tensor", 0, 0, tiled=True, axis_index_groups=Z_GROUPS)
+    return rows.reshape(CHUNK, value.shape[1])
+
+
+def input_grad_kernel(x_ref, *refs):
+    chunks = refs[:X_COUNT]
+    up_ref, a_ref, rows_ref, gain_ref, out_ref = refs[X_COUNT:]
+    hid_width = up_ref.shape[1]
+    width = up_ref.shape[0]
+    gain = gain_ref[...]
+    gain_sum = jnp.zeros((1, width), f32)
+    per_chunk = SECTIONS // X_COUNT
+    for k in range(X_COUNT):
+        chunk = lax.rem(x_ref[0] + k, X_COUNT)
+        start = pl.multiple_of(chunk * CHUNK, CHUNK)
+        part = lax.dot_general(
+            chunks[k][:, :hid_width], up_ref[...], (((1,), (1,)), ((), ())), preferred_element_type=f32
+        )
+        terms = chunks[k][:, hid_width:].astype(f32)
+        first = (terms[:, 0:1] + terms[:, 1:2] + terms[:, 2:3]) / D
+        second = (terms[:, 3:4] + terms[:, 4:5] + terms[:, 5:6]) / D
+        mean = rows_ref[pl.ds(start, CHUNK), 0:1]
+        scale = rows_ref[pl.ds(start, CHUNK), 1:2]
+        centred = (a_ref[pl.ds(start, CHUNK), :].astype(f32) - mean) * scale
+        gain_sum = gain_sum + jnp.sum(part * centred, axis=0, keepdims=True)
+        correction = part * gain - first - centred * second
+        out_ref[pl.ds(chunk * per_chunk, per_chunk), :, :width] = correction.astype(bf16).reshape(
+            per_chunk, 32, width
+        )
+    high = lax.reduce_precision(gain_sum, 8, 7)
+    middle = lax.reduce_precision(gain_sum - high, 8, 7)
+    low = gain_sum - high - middle
+    lines = [
+        part[:, c * 128 : (c + 1) * 128] for part in (high, middle, low) for c in range(width // 128)
+    ]
+    lines.append(jnp.zeros((32 - len(lines), 128), f32))
+    beside = jnp.concatenate(lines, axis=0).astype(bf16)
+    out_ref[:, :, width:] = jnp.broadcast_to(beside[None], (SECTIONS, 32, 128))
+
+
+def output_kernel(x_ref, *refs):
+    chunks = refs[:X_COUNT]
+    down_ref, out_ref = refs[X_COUNT:]
+    width = down_ref.shape[1]
+    per_chunk = SECTIONS // X_COUNT
+    for k in range(X_COUNT):
+        chunk = lax.rem(x_ref[0] + k, X_COUNT)
+        part = jnp.dot(chunks[k][...], down_ref[...], preferred_element_type=f32)
+        out_ref[pl.ds(chunk * per_chunk, per_chunk)] = part.astype(bf16).reshape(per_chunk, 32, width)
+
+
+def on_device(kernel, out_shape, x, *arrays):
+    vmem = pl.BlockSpec(memory_space=pltpu.VMEM)
+    return pl.pallas_call(
+        kernel,
+        out_shape=out_shape,
+        in_specs=[pl.BlockSpec(memory_space=pltpu.SMEM)] + [vmem] * len(arrays),
+        out_specs=vmem,
+    )(x.reshape(1).astype(jnp.int32), *arrays)
 
 
 def per_device(inputs, cotangent, up_weight, down_weight, norm_gain):
@@ -118,7 +176,6 @@
         ],
         axis=0,
     )
-    row_parts, dh_parts = lax.optimization_barrier((row_parts, dh_parts))
     dh_arrived = [shift_x(dh_parts[k], k) for k in (2, 1, 3)]
     summed = share(row_parts, "tensor")
     dh_own = lax.optimization_barrier(grad_hidden_part(0))
@@ -126,7 +183,9 @@
     mean = (summed[:4] / D).reshape(ROWS)
     scale = lax.rsqrt((summed[4:8] / D).reshape(ROWS) - mean * mean + norm_eps)
     normed = ((a_all.astype(f32) - mean[:, None]) * scale[:, None] * norm_gain).astype(bf16)
-    normed_three = normed.reshape(SECTIONS, 32, width)
+    normed_three, dh_own = lax.optimization_barrier((normed.reshape(SECTIONS, 32, width), dh_own))
+    line = lax.broadcasted_iota(jnp.int32, (ROWS, 128), 1)
+    row_info = jnp.where(line == 0, mean[:, None], scale[:, None])
     normed_chunks = [chunk_of(normed_three, k, 0) for k in range(X_COUNT)]
 
     def pre_part(k):
@@ -149,12 +208,8 @@
     for k, term in enumerate(terms):
         extra = jnp.where(lane == k, term, extra)
 
-    def gather_z(value):
-        return lax.all_gather(value, "tensor", axis=0, tiled=True, axis_index_groups=Z_GROUPS)
-
-    gathered = gather_z(jnp.concatenate([grad_pre, extra, hidden], axis=1))
-    grad_pre_own = gathered[:, : hid_width + EXTRA]
-    hidden_own = gathered[:, hid_width + EXTRA :]
+    grad_pre_own = spread_z(jnp.concatenate([grad_pre, extra], axis=1))
+    hidden_own = spread_z(hidden)
     steps = (2, 1, 3)
     moved = {k: shift_x(grad_pre_own, (X_COUNT - k) % X_COUNT) for k in steps}
     wide_chunks = [grad_pre_own] + [moved[k] for k in (1, 2, 3)]
@@ -162,59 +217,42 @@
     hidden_chunks = [hidden_own] + [moved[k] for k in (1, 2, 3)]
     grad_pre_chunks = [chunk[:, :hid_width] for chunk in wide_chunks]
 
-    def grad_normed_part(k):
-        return lax.dot_general(
-            grad_pre_chunks[k], up_weight, (((1,), (1,)), ((), ())), preferred_element_type=f32
-        ).astype(bf16)
-
-    dn_part = rows_restored([grad_normed_part(k) for k in range(X_COUNT)], x)
-    swapped = lax.all_to_all(dn_part.reshape(SECTIONS, 32, width), "section", 0, 0, tiled=True)
-    dn_part, a_late = lax.optimization_barrier((dn_part, a_all))
-
-    centred_all = (a_late.astype(f32) - mean[:, None]) * scale[:, None]
-    gain_part = jnp.sum(dn_part.astype(f32) * centred_all, axis=0)
-    gain_terms = jnp.concatenate(split_three(gain_part), axis=0).reshape(32, 36)
-    gain_terms = jnp.pad(gain_terms, ((0, 0), (6, EXTRA - 42)))
-    row_terms = rows_restored([chunk[:, hid_width:] for chunk in wide_chunks], x)
-    beside = row_terms.reshape(SECTIONS, 32, EXTRA) + gain_terms[None]
-
-    def out_part(k):
-        return jnp.dot(hidden_chunks[k], down_weight, preferred_element_type=f32).astype(bf16)
-
-    out_parts = rows_restored([out_part(k) for k in range(X_COUNT)], x)
-    swapped_out = lax.all_to_all(
-        jnp.concatenate([out_parts.reshape(SECTIONS, 32, width), beside], axis=2),
-        "section",
-        0,
-        0,
-        tiled=True,
-    )
+    dx_part = on_device(
+        input_grad_kernel,
+        jax.ShapeDtypeStruct((SECTIONS, 32, width + 128), bf16),
+        x,
+        *wide_chunks,
+        up_weight,
+        a_all,
+        row_info,
+        norm_gain.reshape(1, width),
+    )
+    swapped = lax.all_to_all(dx_part, "section", 0, 0, tiled=True)
+    out_part = on_device(
+        output_kernel,
+        jax.ShapeDtypeStruct((SECTIONS, 32, width), bf16),
+        x,
+        *hidden_chunks,
+        down_weight,
+    )
+    swapped_out = lax.all_to_all(out_part, "section", 0, 0, tiled=True)
 
     grad_pre_rolled = jnp.concatenate(grad_pre_chunks, axis=0)
     normed_rolled = jnp.concatenate(normed_chunks, axis=0)
+    hidden_rolled = jnp.concatenate(hidden_chunks, axis=0)
+    g_rolled = jnp.concatenate(g_chunks, axis=0)
     grad_up = lax.dot_general(
         normed_rolled, grad_pre_rolled, (((0,), (0,)), ((), ())), preferred_element_type=f32
     ).astype(bf16)
-    hidden_rolled = jnp.concatenate(hidden_chunks, axis=0)
-    g_rolled = jnp.concatenate(g_chunks, axis=0)
     grad_down = lax.dot_general(
         hidden_rolled, g_rolled, (((0,), (0,)), ((), ())), preferred_element_type=f32
     ).astype(bf16)
 
-    grad_normed = added(swapped)
-    out_terms = added(swapped_out[:, :, :width])
-    beside = added(swapped_out[:, :, width:])
-    in_float = in_rows.astype(f32)
-    states = (in_float + out_terms).astype(bf16)
-    grad_gain = jnp.sum(beside[:, 6:42].reshape(3, width), axis=0)
-    row_first = jnp.sum(beside[:, :3], axis=1, keepdims=True) / D
-    row_second = jnp.sum(beside[:, 3:6], axis=1, keepdims=True) / D
-
-    own_mean = lax.dynamic_slice_in_dim(mean, section * 32, 32, axis=0)[:, None]
-    own_scale = lax.dynamic_slice_in_dim(scale, section * 32, 32, axis=0)[:, None]
-    centred = (in_float - own_mean) * own_scale
-    correction = grad_normed * norm_gain - row_first - centred * row_second
-    input_grads = (grad_rows.astype(f32) + own_scale * correction).astype(bf16)
+    states = (in_rows.astype(f32) + added(swapped_out)).astype(bf16)
+    own_scale = lax.dynamic_slice(row_info, (section * 32, 1), (32, 1))
+    input_grads = (grad_rows.astype(f32) + own_scale * added(swapped[:, :, :width])).astype(bf16)
+    lines = added(swapped[:, :16, width:])[:9]
+    grad_gain = jnp.sum(lines.reshape(3, width), axis=0)
     return (
         states.reshape(inputs.shape),
         input_grads.reshape(inputs.shape),

time: 225 us -> 217 us (0.964)
  blocking collectives: 44.4 us -> 23.5 us
  waiting for transfers between devices: 55.8 us -> 69.7 us
  matrix products: 22.2 us -> 12.4 us
  starting transfers between devices: 73.8 us -> 83.1 us
  Pallas kernels: 0 us -> 7.8 us
  other arithmetic: 16 us -> 9.79 us
    all_gather x1 -> x0, blocking collectives: 20.9 us -> none  [gather_z(): lax.all_gather(value, 'tensor', axis=0, tiled=True, axis_index_groups=Z_G...]
    ppermute x12, waiting for transfers between devices: 26.2 us -> 37 us  [shift_x(): return lax.ppermute(value, 'tensor', pairs)]
    pallas_call x0 -> x2, Pallas kernels: none -> 7.8 us  [on_device(): pl.pallas_call(kernel, out_shape=out_shape, in_specs=[pl.BlockSpec(memory...]
    dot_general x8 -> x0, matrix products: 6.14 us -> none  [the longest x4 4.61 us: grad_normed_part(): lax.dot_general(grad_pre_chunks[k], up_weight, (((1,), (1,)), ((), ())),...]
    all_to_all x2 -> x4, starting transfers between devices: 16.5 us -> 22.5 us  [the longest x1 8.21 us: per_device(): swapped = lax.all_to_all(dx_part, 'section', 0, 0, tiled=True)]
    ppermute x12, starting transfers between devices: 37.1 us -> 40.5 us  [shift_x(): return lax.ppermute(value, 'tensor', pairs)]
    dot_general x4, matrix products: 4.65 us -> 2.22 us  [pre_part(): jnp.dot(normed_chunks[k], up_weight, preferred_element_type=f32)]
    all_to_all x2, waiting for transfers between devices: 10.4 us -> 12.8 us  [reduce_chunks(): lax.all_to_all(pieces, 'tensor', 0, 0, tiled=True, axis_index_groups=Z_GR...]
  transfers between devices with their start and end apart: 17 -> 19, of which waited for: 10 -> 12; matrix products, arithmetic and copies ran while one was open for 14% -> 10% of each run, Pallas kernels for 0% -> 4%
where the time goes in v1:
time: 217 us; the launch traced here: 216 us
  starting transfers between devices  83.1 us (38%)
  waiting for transfers between devices  69.7 us (32%)
  blocking collectives  23.5 us (11%)
  matrix products  12.4 us (6%)
  other arithmetic  9.79 us (5%)
  local copies, waits for them, and re-layouts  8.01 us (4%)
  Pallas kernels  7.8 us (4%)
    ppermute x12, starting transfers between devices, shift_x(): return lax.ppermute(value, 'tensor', pairs)  40.5 us
    ppermute x12, waiting for transfers between devices, shift_x(): return lax.ppermute(value, 'tensor', pairs)  37 us
    all_gather x1, blocking collectives, per_device(): lax.all_gather(jnp.concatenate([in_rows, grad_rows], axis=0), 'section',...  23.5 us
    all_to_all x2, waiting for transfers between devices, reduce_chunks(): lax.all_to_all(pieces, 'tensor', 0, 0, tiled=True, axis_index_groups=Z_GR...  12.8 us
    all_to_all x2, waiting for transfers between devices, spread_z(): lax.all_to_all(copies, 'tensor', 0, 0, tiled=True, axis_index_groups=Z_GR...  10.6 us
    all_to_all x1, starting transfers between devices, share(): return added(lax.all_to_all(spread, axis, 0, 0, tiled=True))  10.4 us
    all_to_all x2, starting transfers between devices, reduce_chunks(): lax.all_to_all(pieces, 'tensor', 0, 0, tiled=True, axis_index_groups=Z_GR...  9.69 us
    all_to_all x1, waiting for transfers between devices, per_device(): swapped = lax.all_to_all(dx_part, 'section', 0, 0, tiled=True)  9.22 us
  transfers between devices with their start and end apart: 19, of which 12 were waited for; matrix products, arithmetic and copies ran while one was open for 10% of the time, Pallas kernels for 4%

profile of v1, /device:TPU:1, one launch (start us, length us, event | category | flops | bytes accessed | tf_op | source)
XLA Modules:
  0.0 215.6 jit_solution(6939085246080699811)
XLA Ops:
  0.6 0.8 reduce-precision_convert_fusion.1
  1.4 0.8 pad_maximum_fusion.1
  2.2 23.5 %all_gather.3 = bf16[1024,384]{1,0:T(8,128)(2,1)S(1)} all-gather(bf16[64,384]{1,0:T(8,128)(2,1)S(1)} %pad_maximum_fusion.1), channel_id=1, replica_groups=mesh['section'=16,'tensor'=32] {'section'}, dimensions={0}, use_global_device_ids=true | all-gather | bytes 835584 | tf_op jit(solution)/shard_map/all_gather | solution.py:149
  25.7 0.2 convert_reduce_fusion
  26.1 0.3 convolution_reduce_fusion
  26.4 0.8 broadcast_in_dim.79
  27.2 10.4 %all-to-all-start = ((f32[32,20,128]{2,1,0:T(8,128)}), f32[32,20,128]{2,1,0:T(8,128)S(1)}, u32[]{:S(2)}, u32[]{:S(2)}) async-start(f32[32,20,128]{2,1,0:T(8,128)} %broadcast_in_dim.79), calls=%async_computation | async-start | bytes 786432 | tf_op jit(solution)/shard_map/all_to_all | solution.py:52
  37.8 1.3 convolution_convert_fusion.4
  39.1 4.6 %collective-permute-start.6 = (bf16[128,1536]{1,0:T(8,128)(2,1)}, bf16[128,1536]{1,0:T(8,128)(2,1)}, u32[]{:S(2)}, u32[]{:S(2)}) collective-permute-start(bf16[128,1536]{1,0:T(8,128)(2,1)} %convolution_convert_fusion.4), channel_id=1, source_target_pairs={{0,16},{1,17},{2,18},{3,19},{4,20},{5,21},{6,22},{7,23},{8,24},{9,... | collective-permute-start | bytes 1179656 | tf_op jit(solution)/shard_map/ppermute | solution.py:46
  43.7 1.3 convolution_convert_fusion.3
  45.0 2.2 %collective-permute-start.7 = (bf16[128,1536]{1,0:T(8,128)(2,1)}, bf16[128,1536]{1,0:T(8,128)(2,1)}, u32[]{:S(2)}, u32[]{:S(2)}) collective-permute-start(bf16[128,1536]{1,0:T(8,128)(2,1)} %convolution_convert_fusion.3), channel_id=1, source_target_pairs={{0,8},{1,9},{2,10},{3,11},{4,12},{5,13},{6,14},{7,15},{8,16},{9,17... | collective-permute-start | bytes 1179656 | tf_op jit(solution)/shard_map/ppermute | solution.py:46
  47.2 1.2 convolution_convert_fusion.2
  48.5 4.4 %collective-permute-start.8 = (bf16[128,1536]{1,0:T(8,128)(2,1)}, bf16[128,1536]{1,0:T(8,128)(2,1)}, u32[]{:S(2)}, u32[]{:S(2)}) collective-permute-start(bf16[128,1536]{1,0:T(8,128)(2,1)} %convolution_convert_fusion.2), channel_id=1, source_target_pairs={{0,24},{1,25},{2,26},{3,27},{4,28},{5,29},{6,30},{7,31},{8,0},{9,1... | collective-permute-start | bytes 1179656 | tf_op jit(solution)/shard_map/ppermute | solution.py:46
  52.9 1.2 convolution_convert_fusion.9
  54.6 0.4 convolution_convert_fusion.6
  55.0 0.4 convolution_convert_fusion.7
  55.4 2.1 collective-permute-start
  57.5 2.5 %collective-permute-start.1 = (bf16[128,1536]{1,0:T(8,128)(2,1)S(1)}, bf16[128,1536]{1,0:T(8,128)(2,1)}, u32[]{:S(2)}, u32[]{:S(2)}) collective-permute-start(bf16[128,1536]{1,0:T(8,128)(2,1)S(1)} %convolution_convert_fusion.6), channel_id=1, source_target_pairs={{0,8},{1,9},{2,10},{3,11},{4,12},{5,13},{6,14},{7,15},{8,16},{9,17... | collective-permute-start | bytes 1179656 | tf_op jit(solution)/shard_map/ppermute | solution.py:46
  60.0 1.1 convolution_convert_fusion.5
  61.1 4.0 %collective-permute-start.2 = (bf16[128,1536]{1,0:T(8,128)(2,1)}, bf16[128,1536]{1,0:T(8,128)(2,1)}, u32[]{:S(2)}, u32[]{:S(2)}) collective-permute-start(bf16[128,1536]{1,0:T(8,128)(2,1)} %convolution_convert_fusion.5), channel_id=1, source_target_pairs={{0,24},{1,25},{2,26},{3,27},{4,28},{5,29},{6,30},{7,31},{8,0},{9,1... | collective-permute-start | bytes 1179656 | tf_op jit(solution)/shard_map/ppermute | solution.py:46
  65.1 0.7 collective-permute-done.7
  65.8 2.2 %add_convert_fusion = bf16[128,1536]{1,0:T(8,128)(2,1)} fusion(bf16[128,1536]{1,0:T(8,128)(2,1)} %collective-permute-done.8, bf16[128,1536]{1,0:T(8,128)(2,1)} %collective-permute-done.7, bf16[128,1536]{1,0:T(8,128)(2,1)} %collective-permute-done.6, bf16[128,1536]{1,0:T(8,128)(2,1)S(1)} %copy-done.9), kind=kLoop, calls=%fused_computation.32 | loop fusion | flops 1572864 | bytes 1966080 | tf_op jit(solution)/shard_map/convert_element_type | solution.py:74
  67.9 5.7 %all-to-all-start.4 = ((bf16[8,16,1536]{2,1,0:T(8,128)(2,1)}), bf16[8,16,1536]{2,1,0:T(8,128)(2,1)S(1)}, u32[]{:S(2)}, u32[]{:S(2)}) async-start(bf16[8,16,1536]{2,1,0:T(8,128)(2,1)} %bitcast.36), calls=%async_computation.4 | async-start | bytes 786432 | tf_op jit(solution)/shard_map/all_to_all | solution.py:75
  73.7 0.4 convolution_convert_fusion.8
  74.0 8.0 %collective-permute-done.1 = bf16[128,1536]{1,0:T(8,128)(2,1)} collective-permute-done((bf16[128,1536]{1,0:T(8,128)(2,1)S(1)}, bf16[128,1536]{1,0:T(8,128)(2,1)}, u32[]{:S(2)}, u32[]{:S(2)}) %collective-permute-start.1) | collective-permute-done | bytes 393248 | tf_op jit(solution)/shard_map/ppermute | solution.py:46
  82.0 2.2 %add_convert_fusion.1 = bf16[128,1536]{1,0:T(8,128)(2,1)} fusion(bf16[128,1536]{1,0:T(8,128)(2,1)} %collective-permute-done.2, bf16[128,1536]{1,0:T(8,128)(2,1)} %collective-permute-done.1, bf16[128,1536]{1,0:T(8,128)(2,1)} %collective-permute-done, bf16[128,1536]{1,0:T(8,128)(2,1)S(1)} %convolution_convert_fusion.8), kind=kLoop, calls=%fused_computation.33 | loop fusion | flops 1572864 | bytes 1966080 | tf_op jit(solution)/shard_map/convert_element_type | solution.py:74
  84.2 1.6 all-to-all-done.4
  85.7 4.0 %all-to-all-start.1 = ((bf16[8,16,1536]{2,1,0:T(8,128)(2,1)}), bf16[8,16,1536]{2,1,0:T(8,128)(2,1)S(1)}, u32[]{:S(2)}, u32[]{:S(2)}) async-start(bf16[8,16,1536]{2,1,0:T(8,128)(2,1)} %bitcast.26), calls=%async_computation.1 | async-start | bytes 786432 | tf_op jit(solution)/shard_map/all_to_all | solution.py:75
  89.8 11.3 %all-to-all-done.1 = bf16[8,16,1536]{2,1,0:T(8,128)(2,1)S(1)} async-done(((bf16[8,16,1536]{2,1,0:T(8,128)(2,1)}), bf16[8,16,1536]{2,1,0:T(8,128)(2,1)S(1)}, u32[]{:S(2)}, u32[]{:S(2)}) %all-to-all-start.1) | async-done | bytes 393248 | tf_op jit(solution)/shard_map/all_to_all | solution.py:75
  101.0 0.3 fusion.32
  101.3 0.8 broadcast_in_dim.81
  102.1 3.5 %all-to-all-start.2 = ((bf16[8,16,1536]{2,1,0:T(8,128)(2,1)}), bf16[8,16,1536]{2,1,0:T(8,128)(2,1)S(1)}, u32[]{:S(2)}, u32[]{:S(2)}) async-start(bf16[8,16,1536]{2,1,0:T(8,128)(2,1)} %broadcast_in_dim.81), calls=%async_computation.2 | async-start | bytes 786432 | tf_op jit(solution)/shard_map/all_to_all | solution.py:80
  105.7 10.6 %all-to-all-done.2 = bf16[8,16,1536]{2,1,0:T(8,128)(2,1)S(1)} async-done(((bf16[8,16,1536]{2,1,0:T(8,128)(2,1)}), bf16[8,16,1536]{2,1,0:T(8,128)(2,1)S(1)}, u32[]{:S(2)}, u32[]{:S(2)}) %all-to-all-start.2) | async-done | bytes 393248 | tf_op jit(solution)/shard_map/all_to_all | solution.py:80
  116.4 0.8 broadcast_in_dim.91
  117.2 3.5 %all-to-all-start.5 = ((bf16[8,16,1664]{2,1,0:T(8,128)(2,1)}), bf16[8,16,1664]{2,1,0:T(8,128)(2,1)S(1)}, u32[]{:S(2)}, u32[]{:S(2)}) async-start(bf16[8,16,1664]{2,1,0:T(8,128)(2,1)} %broadcast_in_dim.91), calls=%async_computation.5 | async-start | bytes 851968 | tf_op jit(solution)/shard_map/all_to_all | solution.py:80
  120.7 4.3 %collective-permute-start.5 = (bf16[128,1536]{1,0:T(8,128)(2,1)S(1)}, bf16[128,1536]{1,0:T(8,128)(2,1)S(1)}, u32[]{:S(2)}, u32[]{:S(2)}) collective-permute-start(bf16[128,1536]{1,0:T(8,128)(2,1)S(1)} %bitcast.178), channel_id=1, source_target_pairs={{0,8},{1,9},{2,10},{3,11},{4,12},{5,13},{6,14},{7,15},{8,16},{9,17... | collective-permute-start | bytes 1179656 | tf_op jit(solution)/shard_map/ppermute | solution.py:46
  124.9 5.2 %collective-permute-start.4 = (bf16[128,1536]{1,0:T(8,128)(2,1)S(1)}, bf16[128,1536]{1,0:T(8,128)(2,1)S(1)}, u32[]{:S(2)}, u32[]{:S(2)}) collective-permute-start(bf16[128,1536]{1,0:T(8,128)(2,1)S(1)} %bitcast.179), channel_id=1, source_target_pairs={{0,16},{1,17},{2,18},{3,19},{4,20},{5,21},{6,22},{7,23},{8,24},{9,... | collective-permute-start | bytes 1179656 | tf_op jit(solution)/shard_map/ppermute | solution.py:46
  130.2 1.9 collective-permute-start.3
  132.1 0.6 collective-permute-done.5.refs_3_
  132.7 9.0 %collective-permute-done.4.refs_2_ = bf16[128,1536]{1,0:T(8,128)(2,1)S(1)} collective-permute-done((bf16[128,1536]{1,0:T(8,128)(2,1)S(1)}, bf16[128,1536]{1,0:T(8,128)(2,1)S(1)}, u32[]{:S(2)}, u32[]{:S(2)}) %collective-permute-start.4) | collective-permute-done | bytes 393248 | tf_op jit(solution)/shard_map/ppermute | solution.py:46
  141.7 3.3 %collective-permute-done.3.refs_1_ = bf16[128,1536]{1,0:T(8,128)(2,1)S(1)} collective-permute-done((bf16[128,1536]{1,0:T(8,128)(2,1)S(1)}, bf16[128,1536]{1,0:T(8,128)(2,1)S(1)}, u32[]{:S(2)}, u32[]{:S(2)}) %collective-permute-start.3) | collective-permute-done | bytes 393248 | tf_op jit(solution)/shard_map/ppermute | solution.py:46
  145.0 0.7 copy-done.23
  145.7 3.5 %shard_map.92 = bf16[16,32,384]{2,1,0:T(8,128)(2,1)} custom-call(s32[1]{0:T(128)} %bitcast.x_ref, bf16[128,1536]{1,0:T(8,128)(2,1)} %bitcast.181, bf16[128,1536]{1,0:T(8,128)(2,1)} %copy-done.23, bf16[128,1536]{1,0:T(8,128)(2,1)} %copy-done.22, bf16[128,1536]{1,0:T(8,128)(2,1)} %copy-done.20, bf16[1536,384]{1,0:T(8,128)(2,1)} %refs_4_.2), custom_call_target="tpu_custom_call" | custom-call | tf_op jit(solution)/shard_map/pallas_call | solution.py:133
  149.2 7.3 %all-to-all-start.3 = ((bf16[16,32,384]{2,1,0:T(8,128)(2,1)}), bf16[16,32,384]{2,1,0:T(8,128)(2,1)S(1)}, u32[]{:S(2)}, u32[]{:S(2)}) async-start(bf16[16,32,384]{2,1,0:T(8,128)(2,1)} %shard_map.92), calls=%async_computation.3 | async-start | bytes 786432 | tf_op jit(solution)/shard_map/all_to_all | solution.py:238
  156.5 0.6 broadcast_in_dim.92.refs_7_
  157.1 0.8 slice.454
  157.9 2.2 %collective-permute-start.11 = (bf16[128,1664]{1,0:T(8,128)(2,1)S(1)}, bf16[128,1664]{1,0:T(8,128)(2,1)S(1)}, u32[]{:S(2)}, u32[]{:S(2)}) collective-permute-start(bf16[128,1664]{1,0:T(8,128)(2,1)S(1)} %bitcast.172), channel_id=1, source_target_pairs={{0,8},{1,9},{2,10},{3,11},{4,12},{5,13},{6,14},{7,15},{8,16},{9,17... | collective-permute-start | bytes 1277960 | tf_op jit(solution)/shard_map/ppermute | solution.py:46
  160.1 5.2 %collective-permute-start.10 = (bf16[128,1664]{1,0:T(8,128)(2,1)S(1)}, bf16[128,1664]{1,0:T(8,128)(2,1)S(1)}, u32[]{:S(2)}, u32[]{:S(2)}) collective-permute-start(bf16[128,1664]{1,0:T(8,128)(2,1)S(1)} %bitcast.173), channel_id=1, source_target_pairs={{0,16},{1,17},{2,18},{3,19},{4,20},{5,21},{6,22},{7,23},{8,24},{9,... | collective-permute-start | bytes 1277960 | tf_op jit(solution)/shard_map/ppermute | solution.py:46
  165.3 1.9 collective-permute-start.9
  167.2 0.9 broadcast_select_fusion.refs_6_
  168.1 4.1 %collective-permute-done.11.refs_3_ = bf16[128,1664]{1,0:T(8,128)(2,1)S(1)} collective-permute-done((bf16[128,1664]{1,0:T(8,128)(2,1)S(1)}, bf16[128,1664]{1,0:T(8,128)(2,1)S(1)}, u32[]{:S(2)}, u32[]{:S(2)}) %collective-permute-start.11) | collective-permute-done | bytes 426016 | tf_op jit(solution)/shard_map/ppermute | solution.py:46
  172.2 10.0 %collective-permute-done.10.refs_2_ = bf16[128,1664]{1,0:T(8,128)(2,1)S(1)} collective-permute-done((bf16[128,1664]{1,0:T(8,128)(2,1)S(1)}, bf16[128,1664]{1,0:T(8,128)(2,1)S(1)}, u32[]{:S(2)}, u32[]{:S(2)}) %collective-permute-start.10) | collective-permute-done | bytes 426016 | tf_op jit(solution)/shard_map/ppermute | solution.py:46
  182.3 1.4 collective-permute-done.9.refs_1_
  183.6 0.7 copy-done.6
  184.4 4.3 %shard_map.93 = bf16[16,32,512]{2,1,0:T(8,128)(2,1)} custom-call(s32[1]{0:T(128)} %bitcast.x_ref, bf16[128,1664]{1,0:T(8,128)(2,1)} %bitcast.175, bf16[128,1664]{1,0:T(8,128)(2,1)} %copy-done.6, bf16[128,1664]{1,0:T(8,128)(2,1)} %copy-done.5, bf16[128,1664]{1,0:T(8,128)(2,1)} %copy-done.4, bf16[384,1536]{1,0:T(8,128)(2,1)} %refs_4_.3, ...), custom_call_target="tpu_custom_call" | custom-call | tf_op jit(solution)/shard_map/pallas_call | solution.py:133
  188.8 8.2 %all-to-all-start.6 = ((bf16[16,32,512]{2,1,0:T(8,128)(2,1)}), bf16[16,32,512]{2,1,0:T(8,128)(2,1)S(1)}, u32[]{:S(2)}, u32[]{:S(2)}) async-start(bf16[16,32,512]{2,1,0:T(8,128)(2,1)} %shard_map.93), calls=%async_computation.6 | async-start | bytes 1048576 | tf_op jit(solution)/shard_map/all_to_all | solution.py:230
  197.0 0.9 dynamic-slice_reduce_fusion
  198.0 3.1 %convolution_convert_fusion = bf16[1536,384]{1,0:T(8,128)(2,1)} fusion(bf16[128,1536]{1,0:T(8,128)(2,1)S(1)} %copy-done.21, bf16[128,1536]{1,0:T(8,128)(2,1)} %copy-done.22, bf16[128,1536]{1,0:T(8,128)(2,1)} %copy-done.23, bf16[128,1536]{1,0:T(8,128)(2,1)S(1)} %bitcast.182, bf16[128,384]{1,0:T(8,128)(2,1)S(1)} %bitcast.186, ...), kind=kOutput, calls=%fused_computation | convolution fusion | flops 612433920 | bytes 3145728 | tf_op jit(solution)/shard_map/dot_general | solution.py:247
  201.2 1.0 slice-done
  202.4 1.8 convolution_convert_fusion.1
  204.3 0.6 fusion.52
  204.9 9.2 %all-to-all-done.6 = bf16[16,32,512]{2,1,0:T(8,128)(2,1)S(1)} async-done(((bf16[16,32,512]{2,1,0:T(8,128)(2,1)}), bf16[16,32,512]{2,1,0:T(8,128)(2,1)S(1)}, u32[]{:S(2)}, u32[]{:S(2)}) %all-to-all-start.6) | async-done | bytes 524320 | tf_op jit(solution)/shard_map/all_to_all | solution.py:230
  214.2 0.6 reduce_sum.59
  214.9 0.7 fusion.50
  (98 shorter events, 1.5 us)
Async XLA Ops:
  0.6 25.5 %copy-start = (bf16[384,1536]{1,0:T(8,128)(2,1)S(1)}, bf16[384,1536]{1,0:T(8,128)(2,1)}, u32[]{:S(2)}) copy-start(bf16[384,1536]{1,0:T(8,128)(2,1)} %refs_4_.3) | copy-start | bytes 3538948
  26.4 11.5 %copy-start.1 = (bf16[1536,384]{1,0:T(8,128)(2,1)S(1)}, bf16[1536,384]{1,0:T(8,128)(2,1)}, u32[]{:S(2)}) copy-start(bf16[1536,384]{1,0:T(8,128)(2,1)} %refs_4_.2) | copy-start | bytes 3538948
  27.2 27.0 %all-to-all-start = ((f32[32,20,128]{2,1,0:T(8,128)}), f32[32,20,128]{2,1,0:T(8,128)S(1)}, u32[]{:S(2)}, u32[]{:S(2)}) async-start(f32[32,20,128]{2,1,0:T(8,128)} %broadcast_in_dim.79), calls=%async_computation | async-start | bytes 786432 | tf_op jit(solution)/shard_map/all_to_all | solution.py:52
  37.8 7.2 %copy-start.14 = (bf16[4,32,384]{2,1,0:T(8,128)(2,1)}, bf16[4,32,384]{2,1,0:T(8,128)(2,1)S(1)}, u32[]{:S(2)}) copy-start(bf16[4,32,384]{2,1,0:T(8,128)(2,1)S(1)} %get-tuple-element.17) | copy-start | bytes 294916
  37.8 7.2 %copy-start.16 = (bf16[4,32,384]{2,1,0:T(8,128)(2,1)}, bf16[4,32,384]{2,1,0:T(8,128)(2,1)S(1)}, u32[]{:S(2)}) copy-start(bf16[4,32,384]{2,1,0:T(8,128)(2,1)S(1)} %get-tuple-element.18) | copy-start | bytes 294916
  37.8 9.4 %copy-start.12 = (bf16[4,32,384]{2,1,0:T(8,128)(2,1)}, bf16[4,32,384]{2,1,0:T(8,128)(2,1)S(1)}, u32[]{:S(2)}) copy-start(bf16[4,32,384]{2,1,0:T(8,128)(2,1)S(1)} %get-tuple-element.16) | copy-start | bytes 294916
  37.8 15.1 %copy-start.10 = (bf16[4,32,384]{2,1,0:T(8,128)(2,1)}, bf16[4,32,384]{2,1,0:T(8,128)(2,1)S(1)}, u32[]{:S(2)}) copy-start(bf16[4,32,384]{2,1,0:T(8,128)(2,1)S(1)} %get-tuple-element.15) | copy-start | bytes 294916
  39.1 22.0 %collective-permute-start.6 = (bf16[128,1536]{1,0:T(8,128)(2,1)}, bf16[128,1536]{1,0:T(8,128)(2,1)}, u32[]{:S(2)}, u32[]{:S(2)}) collective-permute-start(bf16[128,1536]{1,0:T(8,128)(2,1)} %convolution_convert_fusion.4), channel_id=1, source_target_pairs={{0,16},{1,17},{2,18},{3,19},{4,20},{5,21},{6,22},{7,23},{8,24},{9,... | collective-permute-start | bytes 1179656 | tf_op jit(solution)/shard_map/ppermute | solution.py:46
  45.0 20.8 %collective-permute-start.7 = (bf16[128,1536]{1,0:T(8,128)(2,1)}, bf16[128,1536]{1,0:T(8,128)(2,1)}, u32[]{:S(2)}, u32[]{:S(2)}) collective-permute-start(bf16[128,1536]{1,0:T(8,128)(2,1)} %convolution_convert_fusion.3), channel_id=1, source_target_pairs={{0,8},{1,9},{2,10},{3,11},{4,12},{5,13},{6,14},{7,15},{8,16},{9,17... | collective-permute-start | bytes 1179656 | tf_op jit(solution)/shard_map/ppermute | solution.py:46
  48.5 5.9 %copy-start.26 = (f32[384]{0:T(512)S(1)}, f32[384]{0:T(512)}, u32[]{:S(2)}) copy-start(f32[384]{0:T(512)} %param.9) | copy-start | bytes 4612
  48.5 17.3 %collective-permute-start.8 = (bf16[128,1536]{1,0:T(8,128)(2,1)}, bf16[128,1536]{1,0:T(8,128)(2,1)}, u32[]{:S(2)}, u32[]{:S(2)}) collective-permute-start(bf16[128,1536]{1,0:T(8,128)(2,1)} %convolution_convert_fusion.2), channel_id=1, source_target_pairs={{0,24},{1,25},{2,26},{3,27},{4,28},{5,29},{6,30},{7,31},{8,0},{9,1... | collective-permute-start | bytes 1179656 | tf_op jit(solution)/shard_map/ppermute | solution.py:46
  54.6 0.8 copy-start.18
  55.4 10.4 %copy-start.9 = (bf16[128,1536]{1,0:T(8,128)(2,1)S(1)}, bf16[128,1536]{1,0:T(8,128)(2,1)}, u32[]{:S(2)}) copy-start(bf16[128,1536]{1,0:T(8,128)(2,1)} %convolution_convert_fusion.9) | copy-start | bytes 1179652
  55.4 18.6 %collective-permute-start = (bf16[128,1536]{1,0:T(8,128)(2,1)S(1)}, bf16[128,1536]{1,0:T(8,128)(2,1)}, u32[]{:S(2)}, u32[]{:S(2)}) collective-permute-start(bf16[128,1536]{1,0:T(8,128)(2,1)S(1)} %convolution_convert_fusion.7), channel_id=1, source_target_pairs={{0,16},{1,17},{2,18},{3,19},{4,20},{5,21},{6,22},{7,23},{8,24},{9,... | collective-permute-start | bytes 1179656 | tf_op jit(solution)/shard_map/ppermute | solution.py:46
  57.5 24.6 %collective-permute-start.1 = (bf16[128,1536]{1,0:T(8,128)(2,1)S(1)}, bf16[128,1536]{1,0:T(8,128)(2,1)}, u32[]{:S(2)}, u32[]{:S(2)}) collective-permute-start(bf16[128,1536]{1,0:T(8,128)(2,1)S(1)} %convolution_convert_fusion.6), channel_id=1, source_target_pairs={{0,8},{1,9},{2,10},{3,11},{4,12},{5,13},{6,14},{7,15},{8,16},{9,17... | collective-permute-start | bytes 1179656 | tf_op jit(solution)/shard_map/ppermute | solution.py:46
  61.1 20.9 %collective-permute-start.2 = (bf16[128,1536]{1,0:T(8,128)(2,1)}, bf16[128,1536]{1,0:T(8,128)(2,1)}, u32[]{:S(2)}, u32[]{:S(2)}) collective-permute-start(bf16[128,1536]{1,0:T(8,128)(2,1)} %convolution_convert_fusion.5), channel_id=1, source_target_pairs={{0,24},{1,25},{2,26},{3,27},{4,28},{5,29},{6,30},{7,31},{8,0},{9,1... | collective-permute-start | bytes 1179656 | tf_op jit(solution)/shard_map/ppermute | solution.py:46
  67.9 17.8 %all-to-all-start.4 = ((bf16[8,16,1536]{2,1,0:T(8,128)(2,1)}), bf16[8,16,1536]{2,1,0:T(8,128)(2,1)S(1)}, u32[]{:S(2)}, u32[]{:S(2)}) async-start(bf16[8,16,1536]{2,1,0:T(8,128)(2,1)} %bitcast.36), calls=%async_computation.4 | async-start | bytes 786432 | tf_op jit(solution)/shard_map/all_to_all | solution.py:75
  85.7 15.3 %all-to-all-start.1 = ((bf16[8,16,1536]{2,1,0:T(8,128)(2,1)}), bf16[8,16,1536]{2,1,0:T(8,128)(2,1)S(1)}, u32[]{:S(2)}, u32[]{:S(2)}) async-start(bf16[8,16,1536]{2,1,0:T(8,128)(2,1)} %bitcast.26), calls=%async_computation.1 | async-start | bytes 786432 | tf_op jit(solution)/shard_map/all_to_all | solution.py:75
  102.1 14.2 %all-to-all-start.2 = ((bf16[8,16,1536]{2,1,0:T(8,128)(2,1)}), bf16[8,16,1536]{2,1,0:T(8,128)(2,1)S(1)}, u32[]{:S(2)}, u32[]{:S(2)}) async-start(bf16[8,16,1536]{2,1,0:T(8,128)(2,1)} %broadcast_in_dim.81), calls=%async_computation.2 | async-start | bytes 786432 | tf_op jit(solution)/shard_map/all_to_all | solution.py:80
  116.4 28.6 %copy-start.7 = (bf16[8,16,1536]{2,1,0:T(8,128)(2,1)}, bf16[8,16,1536]{2,1,0:T(8,128)(2,1)S(1)}, u32[]{:S(2)}) copy-start(bf16[8,16,1536]{2,1,0:T(8,128)(2,1)S(1)} %all-to-all-done.2) | copy-start | bytes 1179652
  117.2 32.0 %all-to-all-start.5 = ((bf16[8,16,1664]{2,1,0:T(8,128)(2,1)}), bf16[8,16,1664]{2,1,0:T(8,128)(2,1)S(1)}, u32[]{:S(2)}, u32[]{:S(2)}) async-start(bf16[8,16,1664]{2,1,0:T(8,128)(2,1)} %broadcast_in_dim.91), calls=%async_computation.5 | async-start | bytes 851968 | tf_op jit(solution)/shard_map/all_to_all | solution.py:80
  120.7 12.0 %collective-permute-start.5 = (bf16[128,1536]{1,0:T(8,128)(2,1)S(1)}, bf16[128,1536]{1,0:T(8,128)(2,1)S(1)}, u32[]{:S(2)}, u32[]{:S(2)}) collective-permute-start(bf16[128,1536]{1,0:T(8,128)(2,1)S(1)} %bitcast.178), channel_id=1, source_target_pairs={{0,8},{1,9},{2,10},{3,11},{4,12},{5,13},{6,14},{7,15},{8,16},{9,17... | collective-permute-start | bytes 1179656 | tf_op jit(solution)/shard_map/ppermute | solution.py:46
  124.9 16.8 %collective-permute-start.4 = (bf16[128,1536]{1,0:T(8,128)(2,1)S(1)}, bf16[128,1536]{1,0:T(8,128)(2,1)S(1)}, u32[]{:S(2)}, u32[]{:S(2)}) collective-permute-start(bf16[128,1536]{1,0:T(8,128)(2,1)S(1)} %bitcast.179), channel_id=1, source_target_pairs={{0,16},{1,17},{2,18},{3,19},{4,20},{5,21},{6,22},{7,23},{8,24},{9,... | collective-permute-start | bytes 1179656 | tf_op jit(solution)/shard_map/ppermute | solution.py:46
  130.2 14.8 %collective-permute-start.3 = (bf16[128,1536]{1,0:T(8,128)(2,1)S(1)}, bf16[128,1536]{1,0:T(8,128)(2,1)S(1)}, u32[]{:S(2)}, u32[]{:S(2)}) collective-permute-start(bf16[128,1536]{1,0:T(8,128)(2,1)S(1)} %bitcast.180), channel_id=1, source_target_pairs={{0,24},{1,25},{2,26},{3,27},{4,28},{5,29},{6,30},{7,31},{8,0},{9,1... | collective-permute-start | bytes 1179656 | tf_op jit(solution)/shard_map/ppermute | solution.py:46
  132.7 12.3 %copy-start.20 = (bf16[128,1536]{1,0:T(8,128)(2,1)}, bf16[128,1536]{1,0:T(8,128)(2,1)S(1)}, u32[]{:S(2)}) copy-start(bf16[128,1536]{1,0:T(8,128)(2,1)S(1)} %collective-permute-done.5.refs_3_) | copy-start | bytes 1179652
  141.7 3.3 %copy-start.22 = (bf16[128,1536]{1,0:T(8,128)(2,1)}, bf16[128,1536]{1,0:T(8,128)(2,1)S(1)}, u32[]{:S(2)}) copy-start(bf16[128,1536]{1,0:T(8,128)(2,1)S(1)} %collective-permute-done.4.refs_2_) | copy-start | bytes 1179652
  145.0 0.7 copy-start.23
  149.2 34.4 %copy-start.2 = (bf16[8,16,1664]{2,1,0:T(8,128)(2,1)}, bf16[8,16,1664]{2,1,0:T(8,128)(2,1)S(1)}, u32[]{:S(2)}) copy-start(bf16[8,16,1664]{2,1,0:T(8,128)(2,1)S(1)} %all-to-all-done.5) | copy-start | bytes 1277956
  149.2 39.5 %all-to-all-start.3 = ((bf16[16,32,384]{2,1,0:T(8,128)(2,1)}), bf16[16,32,384]{2,1,0:T(8,128)(2,1)S(1)}, u32[]{:S(2)}, u32[]{:S(2)}) async-start(bf16[16,32,384]{2,1,0:T(8,128)(2,1)} %shard_map.92), calls=%async_computation.3 | async-start | bytes 786432 | tf_op jit(solution)/shard_map/all_to_all | solution.py:238
  157.9 14.4 %collective-permute-start.11 = (bf16[128,1664]{1,0:T(8,128)(2,1)S(1)}, bf16[128,1664]{1,0:T(8,128)(2,1)S(1)}, u32[]{:S(2)}, u32[]{:S(2)}) collective-permute-start(bf16[128,1664]{1,0:T(8,128)(2,1)S(1)} %bitcast.172), channel_id=1, source_target_pairs={{0,8},{1,9},{2,10},{3,11},{4,12},{5,13},{6,14},{7,15},{8,16},{9,17... | collective-permute-start | bytes 1277960 | tf_op jit(solution)/shard_map/ppermute | solution.py:46
  160.1 22.2 %collective-permute-start.10 = (bf16[128,1664]{1,0:T(8,128)(2,1)S(1)}, bf16[128,1664]{1,0:T(8,128)(2,1)S(1)}, u32[]{:S(2)}, u32[]{:S(2)}) collective-permute-start(bf16[128,1664]{1,0:T(8,128)(2,1)S(1)} %bitcast.173), channel_id=1, source_target_pairs={{0,16},{1,17},{2,18},{3,19},{4,20},{5,21},{6,22},{7,23},{8,24},{9,... | collective-permute-start | bytes 1277960 | tf_op jit(solution)/shard_map/ppermute | solution.py:46
  165.3 18.4 %collective-permute-start.9 = (bf16[128,1664]{1,0:T(8,128)(2,1)S(1)}, bf16[128,1664]{1,0:T(8,128)(2,1)S(1)}, u32[]{:S(2)}, u32[]{:S(2)}) collective-permute-start(bf16[128,1664]{1,0:T(8,128)(2,1)S(1)} %bitcast.174), channel_id=1, source_target_pairs={{0,24},{1,25},{2,26},{3,27},{4,28},{5,29},{6,30},{7,31},{8,0},{9,1... | collective-permute-start | bytes 1277960 | tf_op jit(solution)/shard_map/ppermute | solution.py:46
  172.2 11.4 %copy-start.4 = (bf16[128,1664]{1,0:T(8,128)(2,1)}, bf16[128,1664]{1,0:T(8,128)(2,1)S(1)}, u32[]{:S(2)}) copy-start(bf16[128,1664]{1,0:T(8,128)(2,1)S(1)} %collective-permute-done.11.refs_3_) | copy-start | bytes 1277956
  182.3 1.4 copy-start.5
  183.6 0.8 copy-start.6
  188.7 9.3 %copy-start.3 = (bf16[8,16,1664]{2,1,0:T(8,128)(2,1)S(1)}, bf16[8,16,1664]{2,1,0:T(8,128)(2,1)}, u32[]{:S(2)}) copy-start(bf16[8,16,1664]{2,1,0:T(8,128)(2,1)} %copy-done.2) | copy-start | bytes 1277956
  188.7 9.3 %copy-start.8 = (bf16[8,16,1536]{2,1,0:T(8,128)(2,1)S(1)}, bf16[8,16,1536]{2,1,0:T(8,128)(2,1)}, u32[]{:S(2)}) copy-start(bf16[8,16,1536]{2,1,0:T(8,128)(2,1)} %copy-done.7) | copy-start | bytes 1179652
  188.7 9.3 %copy-start.11 = (bf16[4,32,384]{2,1,0:T(8,128)(2,1)S(1)}, bf16[4,32,384]{2,1,0:T(8,128)(2,1)}, u32[]{:S(2)}) copy-start(bf16[4,32,384]{2,1,0:T(8,128)(2,1)} %copy-done.10) | copy-start | bytes 294916
  188.7 9.3 %copy-start.13 = (bf16[4,32,384]{2,1,0:T(8,128)(2,1)S(1)}, bf16[4,32,384]{2,1,0:T(8,128)(2,1)}, u32[]{:S(2)}) copy-start(bf16[4,32,384]{2,1,0:T(8,128)(2,1)} %copy-done.12) | copy-start | bytes 294916
  188.7 9.3 %copy-start.15 = (bf16[4,32,384]{2,1,0:T(8,128)(2,1)S(1)}, bf16[4,32,384]{2,1,0:T(8,128)(2,1)}, u32[]{:S(2)}) copy-start(bf16[4,32,384]{2,1,0:T(8,128)(2,1)} %copy-done.14) | copy-start | bytes 294916
  188.7 9.3 %copy-start.17 = (bf16[4,32,384]{2,1,0:T(8,128)(2,1)S(1)}, bf16[4,32,384]{2,1,0:T(8,128)(2,1)}, u32[]{:S(2)}) copy-start(bf16[4,32,384]{2,1,0:T(8,128)(2,1)} %copy-done.16) | copy-start | bytes 294916
  188.7 9.3 %copy-start.21 = (bf16[128,1536]{1,0:T(8,128)(2,1)S(1)}, bf16[128,1536]{1,0:T(8,128)(2,1)}, u32[]{:S(2)}) copy-start(bf16[128,1536]{1,0:T(8,128)(2,1)} %copy-done.20) | copy-start | bytes 1179652
  188.8 25.4 %all-to-all-start.6 = ((bf16[16,32,512]{2,1,0:T(8,128)(2,1)}), bf16[16,32,512]{2,1,0:T(8,128)(2,1)S(1)}, u32[]{:S(2)}, u32[]{:S(2)}) async-start(bf16[16,32,512]{2,1,0:T(8,128)(2,1)} %shard_map.93), calls=%async_computation.6 | async-start | bytes 1048576 | tf_op jit(solution)/shard_map/all_to_all | solution.py:230
  201.2 1.0 slice-start
  201.2 1.1 slice-start.1
  201.2 1.2 slice-start.2
  201.2 1.2 copy-start.19
  202.4 1.9 copy-start.24
  204.3 10.6 %copy-start.25 = (bf16[2,16,384]{2,1,0:T(8,128)(2,1)S(1)}, bf16[2,16,384]{2,1,0:T(8,128)(2,1)}, u32[]{:S(2)}) copy-start(bf16[2,16,384]{2,1,0:T(8,128)(2,1)} %param.6) | copy-start | bytes 73732

commit v2 on v1

--- a/solution.py
+++ b/solution.py
@@ -81,9 +81,17 @@
     return rows.reshape(CHUNK, value.shape[1])
 
 
+PIECES = 5
+
+
+def whole_chunks(refs):
+    own, after, upper, lower, before = (ref[...] for ref in refs)
+    return own, after, jnp.concatenate([upper, lower], axis=0), before
+
+
 def input_grad_kernel(x_ref, *refs):
-    chunks = refs[:X_COUNT]
-    up_ref, a_ref, rows_ref, gain_ref, out_ref = refs[X_COUNT:]
+    chunks = whole_chunks(refs[:PIECES])
+    up_ref, both_ref, rows_ref, gain_ref, out_ref = refs[PIECES:]
     hid_width = up_ref.shape[1]
     width = up_ref.shape[0]
     gain = gain_ref[...]
@@ -100,7 +108,8 @@
         second = (terms[:, 3:4] + terms[:, 4:5] + terms[:, 5:6]) / D
         mean = rows_ref[pl.ds(start, CHUNK), 0:1]
         scale = rows_ref[pl.ds(start, CHUNK), 1:2]
-        centred = (a_ref[pl.ds(start, CHUNK), :].astype(f32) - mean) * scale
+        rows = both_ref[pl.ds(chunk * per_chunk, per_chunk), :32, :].reshape(CHUNK, width)
+        centred = (rows.astype(f32) - mean) * scale
         gain_sum = gain_sum + jnp.sum(part * centred, axis=0, keepdims=True)
         correction = part * gain - first - centred * second
         out_ref[pl.ds(chunk * per_chunk, per_chunk), :, :width] = correction.astype(bf16).reshape(
@@ -118,14 +127,30 @@
 
 
 def output_kernel(x_ref, *refs):
-    chunks = refs[:X_COUNT]
-    down_ref, out_ref = refs[X_COUNT:]
+    chunks = whole_chunks(refs[:PIECES])
+    down_ref, out_ref = refs[PIECES:]
     width = down_ref.shape[1]
     per_chunk = SECTIONS // X_COUNT
     for k in range(X_COUNT):
         chunk = lax.rem(x_ref[0] + k, X_COUNT)
-        part = jnp.dot(chunks[k][...], down_ref[...], preferred_element_type=f32)
+        part = jnp.dot(chunks[k], down_ref[...], preferred_element_type=f32)
         out_ref[pl.ds(chunk * per_chunk, per_chunk)] = part.astype(bf16).reshape(per_chunk, 32, width)
+
+
+def weight_grads_kernel(x_ref, *refs):
+    normed = jnp.concatenate([ref[...] for ref in refs[:X_COUNT]], axis=0)
+    grads = jnp.concatenate([ref[...] for ref in refs[X_COUNT : 2 * X_COUNT]], axis=0)
+    refs = refs[2 * X_COUNT :]
+    up_ref, down_ref = refs[2 * PIECES :]
+    hid_width = up_ref.shape[1]
+    grad_pre = jnp.concatenate([c[:, :hid_width] for c in whole_chunks(refs[:PIECES])], axis=0)
+    up_ref[...] = lax.dot_general(
+        normed, grad_pre, (((0,), (0,)), ((), ())), preferred_element_type=f32
+    ).astype(bf16)
+    hidden = jnp.concatenate(whole_chunks(refs[PIECES : 2 * PIECES]), axis=0)
+    down_ref[...] = lax.dot_general(
+        hidden, grads, (((0,), (0,)), ((), ())), preferred_element_type=f32
+    ).astype(bf16)
 
 
 def on_device(kernel, out_shape, x, *arrays):
@@ -134,7 +159,7 @@
         kernel,
         out_shape=out_shape,
         in_specs=[pl.BlockSpec(memory_space=pltpu.SMEM)] + [vmem] * len(arrays),
-        out_specs=vmem,
+        out_specs=jax.tree.map(lambda _: vmem, out_shape),
     )(x.reshape(1).astype(jnp.int32), *arrays)
 
 
@@ -195,6 +220,7 @@
     pre_own = lax.optimization_barrier(pre_part(0))
     grad_hidden = reduce_chunks(dh_own, dh_arrived)
     pre = reduce_chunks(pre_own, pre_arrived)
+    pre, row_info = lax.optimization_barrier((pre, row_info))
     grad_hidden = added(grad_hidden)
     pre = added(pre)
 
@@ -210,12 +236,16 @@
 
     grad_pre_own = spread_z(jnp.concatenate([grad_pre, extra], axis=1))
     hidden_own = spread_z(hidden)
-    steps = (2, 1, 3)
-    moved = {k: shift_x(grad_pre_own, (X_COUNT - k) % X_COUNT) for k in steps}
-    wide_chunks = [grad_pre_own] + [moved[k] for k in (1, 2, 3)]
-    moved = {k: shift_x(hidden_own, (X_COUNT - k) % X_COUNT) for k in steps}
-    hidden_chunks = [hidden_own] + [moved[k] for k in (1, 2, 3)]
-    grad_pre_chunks = [chunk[:, :hid_width] for chunk in wide_chunks]
+
+    def gather_x(own):
+        after = shift_x(own, -1)
+        before = shift_x(own, 1)
+        upper = shift_x(before[: CHUNK // 2], 1)
+        lower = shift_x(after[CHUNK // 2 :], -1)
+        return [own, after, upper, lower, before]
+
+    wide_chunks = gather_x(grad_pre_own)
+    hidden_chunks = gather_x(hidden_own)
 
     dx_part = on_device(
         input_grad_kernel,
@@ -223,7 +253,7 @@
         x,
         *wide_chunks,
         up_weight,
-        a_all,
+        both,
         row_info,
         norm_gain.reshape(1, width),
     )
@@ -237,16 +267,18 @@
     )
     swapped_out = lax.all_to_all(out_part, "section", 0, 0, tiled=True)
 
-    grad_pre_rolled = jnp.concatenate(grad_pre_chunks, axis=0)
-    normed_rolled = jnp.concatenate(normed_chunks, axis=0)
-    hidden_rolled = jnp.concatenate(hidden_chunks, axis=0)
-    g_rolled = jnp.concatenate(g_chunks, axis=0)
-    grad_up = lax.dot_general(
-        normed_rolled, grad_pre_rolled, (((0,), (0,)), ((), ())), preferred_element_type=f32
-    ).astype(bf16)
-    grad_down = lax.dot_general(
-        hidden_rolled, g_rolled, (((0,), (0,)), ((), ())), preferred_element_type=f32
-    ).astype(bf16)
+    grad_up, grad_down = on_device(
+        weight_grads_kernel,
+        (
+            jax.ShapeDtypeStruct((width, hid_width), bf16),
+            jax.ShapeDtypeStruct((hid_width, width), bf16),
+        ),
+        x,
+        *normed_chunks,
+        *g_chunks,
+        *wide_chunks,
+        *hidden_chunks,
+    )
 
     states = (in_rows.astype(f32) + added(swapped_out)).astype(bf16)
     own_scale = lax.dynamic_slice(row_info, (section * 32, 1), (32, 1))

time: 217 us -> 239 us (1.10)
  waiting for transfers between devices: 69.7 us -> 91.3 us
  matrix products: 12.4 us -> 6 us
  Pallas kernels: 7.8 us -> 12.8 us
  starting transfers between devices: 83.1 us -> 87.5 us
    all_to_all x2, waiting for transfers between devices: 12.8 us -> 27.2 us  [reduce_chunks(): lax.all_to_all(pieces, 'tensor', 0, 0, tiled=True, axis_index_groups=Z_GR...]
    ppermute x12 -> x14, starting transfers between devices: 40.5 us -> 46.2 us  [shift_x(): return lax.ppermute(value, 'tensor', pairs)]
    pallas_call x2 -> x3, Pallas kernels: 7.8 us -> 12.8 us  [on_device(): pl.pallas_call(kernel, out_shape=out_shape, in_specs=[pl.BlockSpec(memory...]
    dot_general x2 -> x0, matrix products: 4.96 us -> none  [the longest x1 3.14 us: per_device(): lax.dot_general(hidden_rolled, g_rolled, (((0,), (0,)), ((), ())), prefer...]
    all_to_all x2, waiting for transfers between devices: 10.6 us -> 14.9 us  [spread_z(): lax.all_to_all(copies, 'tensor', 0, 0, tiled=True, axis_index_groups=Z_GR...]
    ppermute x12 -> x14, waiting for transfers between devices: 37 us -> 38 us  [shift_x(): return lax.ppermute(value, 'tensor', pairs)]
  transfers between devices with their start and end apart: 19 -> 21, of which waited for: 12 -> 13; matrix products, arithmetic and copies ran while one was open for 10% -> 6% of each run, Pallas kernels for 4% -> 5%
where the time goes in v2:
time: 239 us; the launch traced here: 237 us
  waiting for transfers between devices  91.3 us (38%)
  starting transfers between devices  87.5 us (37%)
  blocking collectives  23.5 us (10%)
  Pallas kernels  12.8 us (5%)
  other arithmetic  8.42 us (4%)
  local copies, waits for them, and re-layouts  6.51 us (3%)
  matrix products  6 us (3%)
    ppermute x14, starting transfers between devices, shift_x(): return lax.ppermute(value, 'tensor', pairs)  46.2 us
    ppermute x14, waiting for transfers between devices, shift_x(): return lax.ppermute(value, 'tensor', pairs)  38 us
    all_to_all x2, waiting for transfers between devices, reduce_chunks(): lax.all_to_all(pieces, 'tensor', 0, 0, tiled=True, axis_index_groups=Z_GR...  27.2 us
    all_gather x1, blocking collectives, per_device(): lax.all_gather(jnp.concatenate([in_rows, grad_rows], axis=0), 'section',...  23.5 us
    all_to_all x2, waiting for transfers between devices, spread_z(): lax.all_to_all(copies, 'tensor', 0, 0, tiled=True, axis_index_groups=Z_GR...  14.9 us
    pallas_call x3, Pallas kernels, on_device(): pl.pallas_call(kernel, out_shape=out_shape, in_specs=[pl.BlockSpec(memory...  12.8 us
    all_to_all x1, waiting for transfers between devices, per_device(): swapped = lax.all_to_all(dx_part, 'section', 0, 0, tiled=True)  10.7 us
    all_to_all x1, starting transfers between devices, share(): return added(lax.all_to_all(spread, axis, 0, 0, tiled=True))  10.5 us
  transfers between devices with their start and end apart: 21, of which 13 were waited for; matrix products, arithmetic and copies ran while one was open for 6% of the time, Pallas kernels for 5%

profile of v2, /device:TPU:1, one launch (start us, length us, event | category | flops | bytes accessed | tf_op | source)
XLA Modules:
  0.0 237.4 jit_solution(15700771004229246534)
XLA Ops:
  0.6 0.8 reduce-precision_convert_fusion.1
  1.4 0.8 pad_maximum_fusion.1
  2.2 23.5 %all_gather.3 = bf16[1024,384]{1,0:T(8,128)(2,1)S(1)} all-gather(bf16[64,384]{1,0:T(8,128)(2,1)S(1)} %pad_maximum_fusion.1), channel_id=1, replica_groups=mesh['section'=16,'tensor'=32] {'section'}, dimensions={0}, use_global_device_ids=true | all-gather | bytes 835584 | tf_op jit(solution)/shard_map/all_gather | solution.py:174
  26.1 0.3 convolution_reduce_fusion
  26.4 0.8 broadcast_in_dim.79
  27.2 10.5 %all-to-all-start = ((f32[32,20,128]{2,1,0:T(8,128)}), f32[32,20,128]{2,1,0:T(8,128)S(1)}, u32[]{:S(2)}, u32[]{:S(2)}) async-start(f32[32,20,128]{2,1,0:T(8,128)} %broadcast_in_dim.79), calls=%async_computation | async-start | bytes 786432 | tf_op jit(solution)/shard_map/all_to_all | solution.py:52
  37.7 0.7 constant_dynamic-slice_fusion.7
  38.4 1.3 convolution_convert_fusion.2
  39.7 4.6 %collective-permute-start.7 = (bf16[128,1536]{1,0:T(8,128)(2,1)}, bf16[128,1536]{1,0:T(8,128)(2,1)}, u32[]{:S(2)}, u32[]{:S(2)}) collective-permute-start(bf16[128,1536]{1,0:T(8,128)(2,1)} %convolution_convert_fusion.2), channel_id=1, source_target_pairs={{0,16},{1,17},{2,18},{3,19},{4,20},{5,21},{6,22},{7,23},{8,24},{9,... | collective-permute-start | bytes 1179656 | tf_op jit(solution)/shard_map/ppermute | solution.py:46
  44.3 1.3 convolution_convert_fusion.1
  45.6 2.4 collective-permute-start.8
  48.0 1.3 convolution_convert_fusion.7
  49.2 0.5 all-to-all-done
  50.3 0.4 convolution_convert_fusion.3
  50.7 0.4 convolution_convert_fusion.4
  51.1 0.4 convolution_convert_fusion.5
  51.5 4.1 %collective-permute-start = (bf16[128,1536]{1,0:T(8,128)(2,1)S(1)}, bf16[128,1536]{1,0:T(8,128)(2,1)S(1)}, u32[]{:S(2)}, u32[]{:S(2)}) collective-permute-start(bf16[128,1536]{1,0:T(8,128)(2,1)S(1)} %convolution_convert_fusion.5), channel_id=1, source_target_pairs={{0,16},{1,17},{2,18},{3,19},{4,20},{5,21},{6,22},{7,23},{8,24},{9,... | collective-permute-start | bytes 1179656 | tf_op jit(solution)/shard_map/ppermute | solution.py:46
  55.6 2.3 collective-permute-start.1
  57.9 4.2 %collective-permute-start.2 = (bf16[128,1536]{1,0:T(8,128)(2,1)S(1)}, bf16[128,1536]{1,0:T(8,128)(2,1)S(1)}, u32[]{:S(2)}, u32[]{:S(2)}) collective-permute-start(bf16[128,1536]{1,0:T(8,128)(2,1)S(1)} %convolution_convert_fusion.3), channel_id=1, source_target_pairs={{0,24},{1,25},{2,26},{3,27},{4,28},{5,29},{6,30},{7,31},{8,0},{9,1... | collective-permute-start | bytes 1179656 | tf_op jit(solution)/shard_map/ppermute | solution.py:46
  62.1 0.5 convolution_convert_fusion
  62.6 0.4 convolution_convert_fusion.6
  63.0 10.5 %collective-permute-done = bf16[128,1536]{1,0:T(8,128)(2,1)S(1)} collective-permute-done((bf16[128,1536]{1,0:T(8,128)(2,1)S(1)}, bf16[128,1536]{1,0:T(8,128)(2,1)S(1)}, u32[]{:S(2)}, u32[]{:S(2)}) %collective-permute-start) | collective-permute-done | bytes 393248 | tf_op jit(solution)/shard_map/ppermute | solution.py:46
  73.5 1.9 collective-permute-start.9
  75.4 7.0 %collective-permute-done.1 = bf16[128,1536]{1,0:T(8,128)(2,1)S(1)} collective-permute-done((bf16[128,1536]{1,0:T(8,128)(2,1)S(1)}, bf16[128,1536]{1,0:T(8,128)(2,1)S(1)}, u32[]{:S(2)}, u32[]{:S(2)}) %collective-permute-start.1) | collective-permute-done | bytes 393248 | tf_op jit(solution)/shard_map/ppermute | solution.py:46
  82.4 0.9 add_convert_fusion.1
  83.3 5.3 %all-to-all-start.1 = ((bf16[8,16,1536]{2,1,0:T(8,128)(2,1)}), bf16[8,16,1536]{2,1,0:T(8,128)(2,1)S(1)}, u32[]{:S(2)}, u32[]{:S(2)}) async-start(bf16[8,16,1536]{2,1,0:T(8,128)(2,1)} %bitcast.26), calls=%async_computation.1 | async-start | bytes 786432 | tf_op jit(solution)/shard_map/all_to_all | solution.py:75
  88.7 2.1 add_convert_fusion
  90.7 13.0 %all-to-all-done.1 = bf16[8,16,1536]{2,1,0:T(8,128)(2,1)S(1)} async-done(((bf16[8,16,1536]{2,1,0:T(8,128)(2,1)}), bf16[8,16,1536]{2,1,0:T(8,128)(2,1)S(1)}, u32[]{:S(2)}, u32[]{:S(2)}) %all-to-all-start.1) | async-done | bytes 393248 | tf_op jit(solution)/shard_map/all_to_all | solution.py:75
  103.7 3.5 %all-to-all-start.4 = ((bf16[8,16,1536]{2,1,0:T(8,128)(2,1)}), bf16[8,16,1536]{2,1,0:T(8,128)(2,1)S(1)}, u32[]{:S(2)}, u32[]{:S(2)}) async-start(bf16[8,16,1536]{2,1,0:T(8,128)(2,1)} %bitcast.36), calls=%async_computation.4 | async-start | bytes 786432 | tf_op jit(solution)/shard_map/all_to_all | solution.py:75
  107.2 0.9 broadcast_select_fusion.refs_7_
  108.1 14.1 %all-to-all-done.4 = bf16[8,16,1536]{2,1,0:T(8,128)(2,1)S(1)} async-done(((bf16[8,16,1536]{2,1,0:T(8,128)(2,1)}), bf16[8,16,1536]{2,1,0:T(8,128)(2,1)S(1)}, u32[]{:S(2)}, u32[]{:S(2)}) %all-to-all-start.4) | async-done | bytes 393248 | tf_op jit(solution)/shard_map/all_to_all | solution.py:75
  122.3 0.3 fusion.4
  122.6 0.8 broadcast_in_dim.83
  123.4 3.5 %all-to-all-start.2 = ((bf16[8,16,1536]{2,1,0:T(8,128)(2,1)}), bf16[8,16,1536]{2,1,0:T(8,128)(2,1)S(1)}, u32[]{:S(2)}, u32[]{:S(2)}) async-start(bf16[8,16,1536]{2,1,0:T(8,128)(2,1)} %broadcast_in_dim.83), calls=%async_computation.2 | async-start | bytes 786432 | tf_op jit(solution)/shard_map/all_to_all | solution.py:80
  127.0 14.9 %all-to-all-done.2 = bf16[8,16,1536]{2,1,0:T(8,128)(2,1)S(1)} async-done(((bf16[8,16,1536]{2,1,0:T(8,128)(2,1)}), bf16[8,16,1536]{2,1,0:T(8,128)(2,1)S(1)}, u32[]{:S(2)}, u32[]{:S(2)}) %all-to-all-start.2) | async-done | bytes 393248 | tf_op jit(solution)/shard_map/all_to_all | solution.py:80
  141.9 0.8 broadcast_in_dim.91
  142.7 3.5 %all-to-all-start.5 = ((bf16[8,16,1664]{2,1,0:T(8,128)(2,1)}), bf16[8,16,1664]{2,1,0:T(8,128)(2,1)S(1)}, u32[]{:S(2)}, u32[]{:S(2)}) async-start(bf16[8,16,1664]{2,1,0:T(8,128)(2,1)} %broadcast_in_dim.91), calls=%async_computation.5 | async-start | bytes 851968 | tf_op jit(solution)/shard_map/all_to_all | solution.py:80
  146.2 1.9 collective-permute-start.4
  148.1 4.6 %collective-permute-start.3 = (bf16[128,1536]{1,0:T(8,128)(2,1)S(1)}, bf16[128,1536]{1,0:T(8,128)(2,1)S(1)}, u32[]{:S(2)}, u32[]{:S(2)}) collective-permute-start(bf16[128,1536]{1,0:T(8,128)(2,1)S(1)} %bitcast.176), channel_id=1, source_target_pairs={{0,24},{1,25},{2,26},{3,27},{4,28},{5,29},{6,30},{7,31},{8,0},{9,1... | collective-permute-start | bytes 1179656 | tf_op jit(solution)/shard_map/ppermute | solution.py:46
  152.7 6.8 %collective-permute-done.4.refs_4_.refs_17_ = bf16[128,1536]{1,0:T(8,128)(2,1)S(1)} collective-permute-done((bf16[128,1536]{1,0:T(8,128)(2,1)S(1)}, bf16[128,1536]{1,0:T(8,128)(2,1)S(1)}, u32[]{:S(2)}, u32[]{:S(2)}) %collective-permute-start.4) | collective-permute-done | bytes 393248 | tf_op jit(solution)/shard_map/ppermute | solution.py:46
  159.5 1.9 collective-permute-start.5
  161.5 4.6 %collective-permute-start.6 = (bf16[64,1536]{1,0:T(8,128)(2,1)S(1)}, bf16[64,1536]{1,0:T(8,128)(2,1)S(1)}, u32[]{:S(2)}, u32[]{:S(2)}) collective-permute-start(bf16[64,1536]{1,0:T(8,128)(2,1)S(1)} %slice.490), channel_id=1, source_target_pairs={{0,24},{1,25},{2,26},{3,27},{4,28},{5,29},{6,30},{7,31},{8,0},{9,1... | collective-permute-start | bytes 589832 | tf_op jit(solution)/shard_map/ppermute | solution.py:46
  166.1 1.7 collective-permute-done.5.refs_2_.refs_15_
  167.7 0.9 collective-permute-done.6.refs_3_.refs_16_
  168.7 0.7 copy-done.21
  169.4 3.5 %shard_map.92 = bf16[16,32,384]{2,1,0:T(8,128)(2,1)} custom-call(s32[1]{0:T(128)} %bitcast.x_ref, bf16[128,1536]{1,0:T(8,128)(2,1)} %bitcast.177, bf16[128,1536]{1,0:T(8,128)(2,1)} %copy-done.8, bf16[64,1536]{1,0:T(8,128)(2,1)} %copy-done.20, bf16[64,1536]{1,0:T(8,128)(2,1)} %copy-done.21, bf16[128,1536]{1,0:T(8,128)(2,1)} %copy-done.7, ...), custom_call_target="tpu_custom_call" | custom-call | tf_op jit(solution)/shard_map/pallas_call | solution.py:158
  172.9 6.8 %all-to-all-start.3 = ((bf16[16,32,384]{2,1,0:T(8,128)(2,1)}), bf16[16,32,384]{2,1,0:T(8,128)(2,1)S(1)}, u32[]{:S(2)}, u32[]{:S(2)}) async-start(bf16[16,32,384]{2,1,0:T(8,128)(2,1)} %shard_map.92), calls=%async_computation.3 | async-start | bytes 786432 | tf_op jit(solution)/shard_map/all_to_all | solution.py:268
  179.7 1.9 collective-permute-start.11
  181.6 5.3 %collective-permute-start.10 = (bf16[128,1664]{1,0:T(8,128)(2,1)S(1)}, bf16[128,1664]{1,0:T(8,128)(2,1)S(1)}, u32[]{:S(2)}, u32[]{:S(2)}) collective-permute-start(bf16[128,1664]{1,0:T(8,128)(2,1)S(1)} %bitcast.172), channel_id=1, source_target_pairs={{0,24},{1,25},{2,26},{3,27},{4,28},{5,29},{6,30},{7,31},{8,0},{9,1... | collective-permute-start | bytes 1277960 | tf_op jit(solution)/shard_map/ppermute | solution.py:46
  186.9 8.1 %collective-permute-done.11.refs_4_.refs_12_ = bf16[128,1664]{1,0:T(8,128)(2,1)S(1)} collective-permute-done((bf16[128,1664]{1,0:T(8,128)(2,1)S(1)}, bf16[128,1664]{1,0:T(8,128)(2,1)S(1)}, u32[]{:S(2)}, u32[]{:S(2)}) %collective-permute-start.11) | collective-permute-done | bytes 426016 | tf_op jit(solution)/shard_map/ppermute | solution.py:46
  195.1 1.9 collective-permute-start.12
  197.1 4.6 %collective-permute-start.13 = (bf16[64,1664]{1,0:T(8,128)(2,1)S(1)}, bf16[64,1664]{1,0:T(8,128)(2,1)S(1)}, u32[]{:S(2)}, u32[]{:S(2)}) collective-permute-start(bf16[64,1664]{1,0:T(8,128)(2,1)S(1)} %slice.517), channel_id=1, source_target_pairs={{0,24},{1,25},{2,26},{3,27},{4,28},{5,29},{6,30},{7,31},{8,0},{9,1... | collective-permute-start | bytes 638984 | tf_op jit(solution)/shard_map/ppermute | solution.py:46
  201.7 0.6 broadcast_in_dim.92.refs_8_
  202.2 2.1 collective-permute-done.12.refs_2_.refs_10_
  204.3 0.9 collective-permute-done.13.refs_3_.refs_11_
  205.3 0.7 copy-done.19
  206.0 4.5 %shard_map.93 = bf16[16,32,512]{2,1,0:T(8,128)(2,1)} custom-call(s32[1]{0:T(128)} %bitcast.x_ref, bf16[128,1664]{1,0:T(8,128)(2,1)} %bitcast.173, bf16[128,1664]{1,0:T(8,128)(2,1)} %copy-done.6, bf16[64,1664]{1,0:T(8,128)(2,1)} %copy-done.18, bf16[64,1664]{1,0:T(8,128)(2,1)} %copy-done.19, bf16[128,1664]{1,0:T(8,128)(2,1)} %copy-done.5, ...), custom_call_target="tpu_custom_call" | custom-call | tf_op jit(solution)/shard_map/pallas_call | solution.py:158
  210.5 8.4 %all-to-all-start.6 = ((bf16[16,32,512]{2,1,0:T(8,128)(2,1)}), bf16[16,32,512]{2,1,0:T(8,128)(2,1)S(1)}, u32[]{:S(2)}, u32[]{:S(2)}) async-start(bf16[16,32,512]{2,1,0:T(8,128)(2,1)} %shard_map.93), calls=%async_computation.6 | async-start | bytes 1048576 | tf_op jit(solution)/shard_map/all_to_all | solution.py:260
  218.8 0.9 dynamic-slice_reduce_fusion
  219.8 4.8 %shard_map.94 = (bf16[384,1536]{1,0:T(8,128)(2,1)}, bf16[1536,384]{1,0:T(8,128)(2,1)}) custom-call(s32[1]{0:T(128)} %bitcast.x_ref, bf16[128,384]{1,0:T(8,128)(2,1)} %bitcast.188, bf16[128,384]{1,0:T(8,128)(2,1)} %bitcast.192, bf16[128,384]{1,0:T(8,128)(2,1)} %bitcast.194, bf16[128,384]{1,0:T(8,128)(2,1)} %bitcast.190, bf16[128,384]{1,0:T(8,128)(2,1)} %bitcast.180, ...), custom_call_target="tpu_custom_call" | custom-call | tf_op jit(solution)/shard_map/pallas_call | solution.py:158
  224.7 0.6 fusion.24
  225.4 10.7 %all-to-all-done.6 = bf16[16,32,512]{2,1,0:T(8,128)(2,1)S(1)} async-done(((bf16[16,32,512]{2,1,0:T(8,128)(2,1)}), bf16[16,32,512]{2,1,0:T(8,128)(2,1)S(1)}, u32[]{:S(2)}, u32[]{:S(2)}) %all-to-all-start.6) | async-done | bytes 524320 | tf_op jit(solution)/shard_map/all_to_all | solution.py:260
  236.1 0.6 reduce_sum.59
  236.8 0.7 fusion.22
  (93 shorter events, 1.4 us)
Async XLA Ops:
  0.6 25.5 %copy-start = (bf16[384,1536]{1,0:T(8,128)(2,1)S(1)}, bf16[384,1536]{1,0:T(8,128)(2,1)}, u32[]{:S(2)}) copy-start(bf16[384,1536]{1,0:T(8,128)(2,1)} %refs_5_.3) | copy-start | bytes 3538948
  25.7 24.3 %copy-start.2 = (bf16[1024,384]{1,0:T(8,128)(2,1)}, bf16[1024,384]{1,0:T(8,128)(2,1)S(1)}, u32[]{:S(2)}) copy-start(bf16[1024,384]{1,0:T(8,128)(2,1)S(1)} %all_gather.3) | copy-start | bytes 2359300
  26.4 12.1 %copy-start.1 = (bf16[1536,384]{1,0:T(8,128)(2,1)S(1)}, bf16[1536,384]{1,0:T(8,128)(2,1)}, u32[]{:S(2)}) copy-start(bf16[1536,384]{1,0:T(8,128)(2,1)} %refs_5_.2) | copy-start | bytes 3538948
  27.2 22.6 %all-to-all-start = ((f32[32,20,128]{2,1,0:T(8,128)}), f32[32,20,128]{2,1,0:T(8,128)S(1)}, u32[]{:S(2)}, u32[]{:S(2)}) async-start(f32[32,20,128]{2,1,0:T(8,128)} %broadcast_in_dim.79), calls=%async_computation | async-start | bytes 786432 | tf_op jit(solution)/shard_map/all_to_all | solution.py:52
  38.4 7.2 %copy-start.12 = (bf16[4,32,384]{2,1,0:T(8,128)(2,1)}, bf16[4,32,384]{2,1,0:T(8,128)(2,1)S(1)}, u32[]{:S(2)}) copy-start(bf16[4,32,384]{2,1,0:T(8,128)(2,1)S(1)} %get-tuple-element.25) | copy-start | bytes 294916
  38.4 7.2 %copy-start.13 = (bf16[4,32,384]{2,1,0:T(8,128)(2,1)}, bf16[4,32,384]{2,1,0:T(8,128)(2,1)S(1)}, u32[]{:S(2)}) copy-start(bf16[4,32,384]{2,1,0:T(8,128)(2,1)S(1)} %get-tuple-element.26) | copy-start | bytes 294916
  38.4 9.5 %copy-start.10 = (bf16[4,32,384]{2,1,0:T(8,128)(2,1)}, bf16[4,32,384]{2,1,0:T(8,128)(2,1)S(1)}, u32[]{:S(2)}) copy-start(bf16[4,32,384]{2,1,0:T(8,128)(2,1)S(1)} %get-tuple-element.23) | copy-start | bytes 294916
  39.7 49.0 %collective-permute-start.7 = (bf16[128,1536]{1,0:T(8,128)(2,1)}, bf16[128,1536]{1,0:T(8,128)(2,1)}, u32[]{:S(2)}, u32[]{:S(2)}) collective-permute-start(bf16[128,1536]{1,0:T(8,128)(2,1)} %convolution_convert_fusion.2), channel_id=1, source_target_pairs={{0,16},{1,17},{2,18},{3,19},{4,20},{5,21},{6,22},{7,23},{8,24},{9,... | collective-permute-start | bytes 1179656 | tf_op jit(solution)/shard_map/ppermute | solution.py:46
  45.6 4.4 %copy-start.24 = (f32[384]{0:T(512)S(1)}, f32[384]{0:T(512)}, u32[]{:S(2)}) copy-start(f32[384]{0:T(512)} %param.9) | copy-start | bytes 4612
  45.6 43.0 %collective-permute-start.8 = (bf16[128,1536]{1,0:T(8,128)(2,1)}, bf16[128,1536]{1,0:T(8,128)(2,1)}, u32[]{:S(2)}, u32[]{:S(2)}) collective-permute-start(bf16[128,1536]{1,0:T(8,128)(2,1)} %convolution_convert_fusion.1), channel_id=1, source_target_pairs={{0,8},{1,9},{2,10},{3,11},{4,12},{5,13},{6,14},{7,15},{8,16},{9,17... | collective-permute-start | bytes 1179656 | tf_op jit(solution)/shard_map/ppermute | solution.py:46
  50.3 0.8 copy-start.15
  50.3 0.8 copy-start.16
  50.3 0.8 copy-start.17
  50.3 12.3 %copy-start.14 = (bf16[4,32,384]{2,1,0:T(8,128)(2,1)}, bf16[4,32,384]{2,1,0:T(8,128)(2,1)S(1)}, u32[]{:S(2)}) copy-start(bf16[4,32,384]{2,1,0:T(8,128)(2,1)S(1)} %get-tuple-element.27) | copy-start | bytes 294916
  51.1 11.0 %copy-start.11 = (bf16[4,32,384]{2,1,0:T(8,128)(2,1)S(1)}, bf16[4,32,384]{2,1,0:T(8,128)(2,1)}, u32[]{:S(2)}) copy-start(bf16[4,32,384]{2,1,0:T(8,128)(2,1)} %get-tuple-element.24) | copy-start | bytes 294916
  51.5 22.0 %collective-permute-start = (bf16[128,1536]{1,0:T(8,128)(2,1)S(1)}, bf16[128,1536]{1,0:T(8,128)(2,1)S(1)}, u32[]{:S(2)}, u32[]{:S(2)}) collective-permute-start(bf16[128,1536]{1,0:T(8,128)(2,1)S(1)} %convolution_convert_fusion.5), channel_id=1, source_target_pairs={{0,16},{1,17},{2,18},{3,19},{4,20},{5,21},{6,22},{7,23},{8,24},{9,... | collective-permute-start | bytes 1179656 | tf_op jit(solution)/shard_map/ppermute | solution.py:46
  55.6 26.8 %collective-permute-start.1 = (bf16[128,1536]{1,0:T(8,128)(2,1)S(1)}, bf16[128,1536]{1,0:T(8,128)(2,1)S(1)}, u32[]{:S(2)}, u32[]{:S(2)}) collective-permute-start(bf16[128,1536]{1,0:T(8,128)(2,1)S(1)} %convolution_convert_fusion.4), channel_id=1, source_target_pairs={{0,8},{1,9},{2,10},{3,11},{4,12},{5,13},{6,14},{7,15},{8,16},{9,17... | collective-permute-start | bytes 1179656 | tf_op jit(solution)/shard_map/ppermute | solution.py:46
  57.9 24.4 %collective-permute-start.2 = (bf16[128,1536]{1,0:T(8,128)(2,1)S(1)}, bf16[128,1536]{1,0:T(8,128)(2,1)S(1)}, u32[]{:S(2)}, u32[]{:S(2)}) collective-permute-start(bf16[128,1536]{1,0:T(8,128)(2,1)S(1)} %convolution_convert_fusion.3), channel_id=1, source_target_pairs={{0,24},{1,25},{2,26},{3,27},{4,28},{5,29},{6,30},{7,31},{8,0},{9,1... | collective-permute-start | bytes 1179656 | tf_op jit(solution)/shard_map/ppermute | solution.py:46
  63.0 25.6 %copy-start.9 = (bf16[128,1536]{1,0:T(8,128)(2,1)S(1)}, bf16[128,1536]{1,0:T(8,128)(2,1)}, u32[]{:S(2)}) copy-start(bf16[128,1536]{1,0:T(8,128)(2,1)} %convolution_convert_fusion.7) | copy-start | bytes 1179652
  73.5 15.2 %collective-permute-start.9 = (bf16[128,1536]{1,0:T(8,128)(2,1)S(1)}, bf16[128,1536]{1,0:T(8,128)(2,1)S(1)}, u32[]{:S(2)}, u32[]{:S(2)}) collective-permute-start(bf16[128,1536]{1,0:T(8,128)(2,1)S(1)} %convolution_convert_fusion), channel_id=1, source_target_pairs={{0,24},{1,25},{2,26},{3,27},{4,28},{5,29},{6,30},{7,31},{8,0},{9,1... | collective-permute-start | bytes 1179656 | tf_op jit(solution)/shard_map/ppermute | solution.py:46
  83.3 20.4 %all-to-all-start.1 = ((bf16[8,16,1536]{2,1,0:T(8,128)(2,1)}), bf16[8,16,1536]{2,1,0:T(8,128)(2,1)S(1)}, u32[]{:S(2)}, u32[]{:S(2)}) async-start(bf16[8,16,1536]{2,1,0:T(8,128)(2,1)} %bitcast.26), calls=%async_computation.1 | async-start | bytes 786432 | tf_op jit(solution)/shard_map/all_to_all | solution.py:75
  103.7 18.5 %all-to-all-start.4 = ((bf16[8,16,1536]{2,1,0:T(8,128)(2,1)}), bf16[8,16,1536]{2,1,0:T(8,128)(2,1)S(1)}, u32[]{:S(2)}, u32[]{:S(2)}) async-start(bf16[8,16,1536]{2,1,0:T(8,128)(2,1)} %bitcast.36), calls=%async_computation.4 | async-start | bytes 786432 | tf_op jit(solution)/shard_map/all_to_all | solution.py:75
  123.4 18.5 %all-to-all-start.2 = ((bf16[8,16,1536]{2,1,0:T(8,128)(2,1)}), bf16[8,16,1536]{2,1,0:T(8,128)(2,1)S(1)}, u32[]{:S(2)}, u32[]{:S(2)}) async-start(bf16[8,16,1536]{2,1,0:T(8,128)(2,1)} %broadcast_in_dim.83), calls=%async_computation.2 | async-start | bytes 786432 | tf_op jit(solution)/shard_map/all_to_all | solution.py:80
  141.9 26.8 %copy-start.4 = (bf16[8,16,1536]{2,1,0:T(8,128)(2,1)}, bf16[8,16,1536]{2,1,0:T(8,128)(2,1)S(1)}, u32[]{:S(2)}) copy-start(bf16[8,16,1536]{2,1,0:T(8,128)(2,1)S(1)} %all-to-all-done.2) | copy-start | bytes 1179652
  142.7 30.1 %all-to-all-start.5 = ((bf16[8,16,1664]{2,1,0:T(8,128)(2,1)}), bf16[8,16,1664]{2,1,0:T(8,128)(2,1)S(1)}, u32[]{:S(2)}, u32[]{:S(2)}) async-start(bf16[8,16,1664]{2,1,0:T(8,128)(2,1)} %broadcast_in_dim.91), calls=%async_computation.5 | async-start | bytes 851968 | tf_op jit(solution)/shard_map/all_to_all | solution.py:80
  146.2 13.3 %collective-permute-start.4 = (bf16[128,1536]{1,0:T(8,128)(2,1)S(1)}, bf16[128,1536]{1,0:T(8,128)(2,1)S(1)}, u32[]{:S(2)}, u32[]{:S(2)}) collective-permute-start(bf16[128,1536]{1,0:T(8,128)(2,1)S(1)} %bitcast.175), channel_id=1, source_target_pairs={{0,8},{1,9},{2,10},{3,11},{4,12},{5,13},{6,14},{7,15},{8,16},{9,17... | collective-permute-start | bytes 1179656 | tf_op jit(solution)/shard_map/ppermute | solution.py:46
  148.1 13.3 %collective-permute-start.3 = (bf16[128,1536]{1,0:T(8,128)(2,1)S(1)}, bf16[128,1536]{1,0:T(8,128)(2,1)S(1)}, u32[]{:S(2)}, u32[]{:S(2)}) collective-permute-start(bf16[128,1536]{1,0:T(8,128)(2,1)S(1)} %bitcast.176), channel_id=1, source_target_pairs={{0,24},{1,25},{2,26},{3,27},{4,28},{5,29},{6,30},{7,31},{8,0},{9,1... | collective-permute-start | bytes 1179656 | tf_op jit(solution)/shard_map/ppermute | solution.py:46
  159.5 9.2 %copy-start.7 = (bf16[128,1536]{1,0:T(8,128)(2,1)}, bf16[128,1536]{1,0:T(8,128)(2,1)S(1)}, u32[]{:S(2)}) copy-start(bf16[128,1536]{1,0:T(8,128)(2,1)S(1)} %collective-permute-done.4.refs_4_.refs_17_) | copy-start | bytes 1179652
  159.5 8.2 %collective-permute-start.5 = (bf16[64,1536]{1,0:T(8,128)(2,1)S(1)}, bf16[64,1536]{1,0:T(8,128)(2,1)S(1)}, u32[]{:S(2)}, u32[]{:S(2)}) collective-permute-start(bf16[64,1536]{1,0:T(8,128)(2,1)S(1)} %slice.489), channel_id=1, source_target_pairs={{0,8},{1,9},{2,10},{3,11},{4,12},{5,13},{6,14},{7,15},{8,16},{9,17... | collective-permute-start | bytes 589832 | tf_op jit(solution)/shard_map/ppermute | solution.py:46
  161.5 7.2 %copy-start.8 = (bf16[128,1536]{1,0:T(8,128)(2,1)}, bf16[128,1536]{1,0:T(8,128)(2,1)S(1)}, u32[]{:S(2)}) copy-start(bf16[128,1536]{1,0:T(8,128)(2,1)S(1)} %collective-permute-done.3.refs_1_.refs_14_) | copy-start | bytes 1179652
  161.5 7.2 %collective-permute-start.6 = (bf16[64,1536]{1,0:T(8,128)(2,1)S(1)}, bf16[64,1536]{1,0:T(8,128)(2,1)S(1)}, u32[]{:S(2)}, u32[]{:S(2)}) collective-permute-start(bf16[64,1536]{1,0:T(8,128)(2,1)S(1)} %slice.490), channel_id=1, source_target_pairs={{0,24},{1,25},{2,26},{3,27},{4,28},{5,29},{6,30},{7,31},{8,0},{9,1... | collective-permute-start | bytes 589832 | tf_op jit(solution)/shard_map/ppermute | solution.py:46
  167.7 0.9 copy-start.20
  168.7 0.7 copy-start.21
  172.9 32.4 %copy-start.3 = (bf16[8,16,1664]{2,1,0:T(8,128)(2,1)}, bf16[8,16,1664]{2,1,0:T(8,128)(2,1)S(1)}, u32[]{:S(2)}) copy-start(bf16[8,16,1664]{2,1,0:T(8,128)(2,1)S(1)} %all-to-all-done.5) | copy-start | bytes 1277956
  172.9 37.6 %all-to-all-start.3 = ((bf16[16,32,384]{2,1,0:T(8,128)(2,1)}), bf16[16,32,384]{2,1,0:T(8,128)(2,1)S(1)}, u32[]{:S(2)}, u32[]{:S(2)}) async-start(bf16[16,32,384]{2,1,0:T(8,128)(2,1)} %shard_map.92), calls=%async_computation.3 | async-start | bytes 786432 | tf_op jit(solution)/shard_map/all_to_all | solution.py:268
  179.7 15.4 %collective-permute-start.11 = (bf16[128,1664]{1,0:T(8,128)(2,1)S(1)}, bf16[128,1664]{1,0:T(8,128)(2,1)S(1)}, u32[]{:S(2)}, u32[]{:S(2)}) collective-permute-start(bf16[128,1664]{1,0:T(8,128)(2,1)S(1)} %bitcast.171), channel_id=1, source_target_pairs={{0,8},{1,9},{2,10},{3,11},{4,12},{5,13},{6,14},{7,15},{8,16},{9,17... | collective-permute-start | bytes 1277960 | tf_op jit(solution)/shard_map/ppermute | solution.py:46
  181.6 15.4 %collective-permute-start.10 = (bf16[128,1664]{1,0:T(8,128)(2,1)S(1)}, bf16[128,1664]{1,0:T(8,128)(2,1)S(1)}, u32[]{:S(2)}, u32[]{:S(2)}) collective-permute-start(bf16[128,1664]{1,0:T(8,128)(2,1)S(1)} %bitcast.172), channel_id=1, source_target_pairs={{0,24},{1,25},{2,26},{3,27},{4,28},{5,29},{6,30},{7,31},{8,0},{9,1... | collective-permute-start | bytes 1277960 | tf_op jit(solution)/shard_map/ppermute | solution.py:46
  195.1 10.2 %copy-start.5 = (bf16[128,1664]{1,0:T(8,128)(2,1)}, bf16[128,1664]{1,0:T(8,128)(2,1)S(1)}, u32[]{:S(2)}) copy-start(bf16[128,1664]{1,0:T(8,128)(2,1)S(1)} %collective-permute-done.11.refs_4_.refs_12_) | copy-start | bytes 1277956
  195.1 9.2 %collective-permute-start.12 = (bf16[64,1664]{1,0:T(8,128)(2,1)S(1)}, bf16[64,1664]{1,0:T(8,128)(2,1)S(1)}, u32[]{:S(2)}, u32[]{:S(2)}) collective-permute-start(bf16[64,1664]{1,0:T(8,128)(2,1)S(1)} %slice.516), channel_id=1, source_target_pairs={{0,8},{1,9},{2,10},{3,11},{4,12},{5,13},{6,14},{7,15},{8,16},{9,17... | collective-permute-start | bytes 638984 | tf_op jit(solution)/shard_map/ppermute | solution.py:46
  197.0 8.2 %copy-start.6 = (bf16[128,1664]{1,0:T(8,128)(2,1)}, bf16[128,1664]{1,0:T(8,128)(2,1)S(1)}, u32[]{:S(2)}) copy-start(bf16[128,1664]{1,0:T(8,128)(2,1)S(1)} %collective-permute-done.10.refs_1_.refs_9_) | copy-start | bytes 1277956
  197.1 8.2 %collective-permute-start.13 = (bf16[64,1664]{1,0:T(8,128)(2,1)S(1)}, bf16[64,1664]{1,0:T(8,128)(2,1)S(1)}, u32[]{:S(2)}, u32[]{:S(2)}) collective-permute-start(bf16[64,1664]{1,0:T(8,128)(2,1)S(1)} %slice.517), channel_id=1, source_target_pairs={{0,24},{1,25},{2,26},{3,27},{4,28},{5,29},{6,30},{7,31},{8,0},{9,1... | collective-permute-start | bytes 638984 | tf_op jit(solution)/shard_map/ppermute | solution.py:46
  204.3 1.0 copy-start.18
  205.3 0.7 copy-start.19
  210.5 25.6 %all-to-all-start.6 = ((bf16[16,32,512]{2,1,0:T(8,128)(2,1)}), bf16[16,32,512]{2,1,0:T(8,128)(2,1)S(1)}, u32[]{:S(2)}, u32[]{:S(2)}) async-start(bf16[16,32,512]{2,1,0:T(8,128)(2,1)} %shard_map.93), calls=%async_computation.6 | async-start | bytes 1048576 | tf_op jit(solution)/shard_map/all_to_all | solution.py:260
  219.8 4.9 %copy-start.22 = (bf16[2,16,384]{2,1,0:T(8,128)(2,1)S(1)}, bf16[2,16,384]{2,1,0:T(8,128)(2,1)}, u32[]{:S(2)}) copy-start(bf16[2,16,384]{2,1,0:T(8,128)(2,1)} %param.5) | copy-start | bytes 73732
  224.7 12.1 %copy-start.23 = (bf16[2,16,384]{2,1,0:T(8,128)(2,1)S(1)}, bf16[2,16,384]{2,1,0:T(8,128)(2,1)}, u32[]{:S(2)}) copy-start(bf16[2,16,384]{2,1,0:T(8,128)(2,1)} %param.6) | copy-start | bytes 73732

commit v3 on v2

--- a/solution.py
+++ b/solution.py
@@ -22,6 +22,7 @@
 bf16 = jnp.bfloat16
 
 
+X_GROUPS = [[x * Z_COUNT + z for x in range(X_COUNT)] for z in range(Z_COUNT)]
 Z_GROUPS = [[x * Z_COUNT + z for z in range(Z_COUNT)] for x in range(X_COUNT)]
 
 
@@ -81,40 +82,22 @@
     return rows.reshape(CHUNK, value.shape[1])
 
 
-PIECES = 5
-
-
-def whole_chunks(refs):
-    own, after, upper, lower, before = (ref[...] for ref in refs)
-    return own, after, jnp.concatenate([upper, lower], axis=0), before
-
-
-def input_grad_kernel(x_ref, *refs):
-    chunks = whole_chunks(refs[:PIECES])
-    up_ref, both_ref, rows_ref, gain_ref, out_ref = refs[PIECES:]
-    hid_width = up_ref.shape[1]
-    width = up_ref.shape[0]
-    gain = gain_ref[...]
-    gain_sum = jnp.zeros((1, width), f32)
-    per_chunk = SECTIONS // X_COUNT
-    for k in range(X_COUNT):
-        chunk = lax.rem(x_ref[0] + k, X_COUNT)
-        start = pl.multiple_of(chunk * CHUNK, CHUNK)
-        part = lax.dot_general(
-            chunks[k][:, :hid_width], up_ref[...], (((1,), (1,)), ((), ())), preferred_element_type=f32
-        )
-        terms = chunks[k][:, hid_width:].astype(f32)
-        first = (terms[:, 0:1] + terms[:, 1:2] + terms[:, 2:3]) / D
-        second = (terms[:, 3:4] + terms[:, 4:5] + terms[:, 5:6]) / D
-        mean = rows_ref[pl.ds(start, CHUNK), 0:1]
-        scale = rows_ref[pl.ds(start, CHUNK), 1:2]
-        rows = both_ref[pl.ds(chunk * per_chunk, per_chunk), :32, :].reshape(CHUNK, width)
-        centred = (rows.astype(f32) - mean) * scale
-        gain_sum = gain_sum + jnp.sum(part * centred, axis=0, keepdims=True)
-        correction = part * gain - first - centred * second
-        out_ref[pl.ds(chunk * per_chunk, per_chunk), :, :width] = correction.astype(bf16).reshape(
-            per_chunk, 32, width
-        )
+def input_grad_kernel(left_ref, right_ref, up_ref, both_ref, rows_ref, gain_ref, out_ref):
+    width, hid_width = up_ref.shape
+    cut = left_ref.shape[1]
+    part = lax.dot_general(
+        left_ref[...], up_ref[:, :cut], (((1,), (1,)), ((), ())), preferred_element_type=f32
+    ) + lax.dot_general(
+        right_ref[:, : hid_width - cut], up_ref[:, cut:], (((1,), (1,)), ((), ())), preferred_element_type=f32
+    )
+    terms = right_ref[:, hid_width - cut :].astype(f32)
+    first = (terms[:, 0:1] + terms[:, 1:2] + terms[:, 2:3]) / D
+    second = (terms[:, 3:4] + terms[:, 4:5] + terms[:, 5:6]) / D
+    rows = both_ref[:, :32, :].reshape(ROWS, width)
+    centred = (rows.astype(f32) - rows_ref[:, 0:1]) * rows_ref[:, 1:2]
+    gain_sum = jnp.sum(part * centred, axis=0, keepdims=True)
+    correction = part * gain_ref[...] - first - centred * second
+    out_ref[:, :, :width] = correction.astype(bf16).reshape(SECTIONS, 32, width)
     high = lax.reduce_precision(gain_sum, 8, 7)
     middle = lax.reduce_precision(gain_sum - high, 8, 7)
     low = gain_sum - high - middle
@@ -126,41 +109,45 @@
     out_ref[:, :, width:] = jnp.broadcast_to(beside[None], (SECTIONS, 32, 128))
 
 
-def output_kernel(x_ref, *refs):
-    chunks = whole_chunks(refs[:PIECES])
-    down_ref, out_ref = refs[PIECES:]
-    width = down_ref.shape[1]
-    per_chunk = SECTIONS // X_COUNT
-    for k in range(X_COUNT):
-        chunk = lax.rem(x_ref[0] + k, X_COUNT)
-        part = jnp.dot(chunks[k], down_ref[...], preferred_element_type=f32)
-        out_ref[pl.ds(chunk * per_chunk, per_chunk)] = part.astype(bf16).reshape(per_chunk, 32, width)
-
-
-def weight_grads_kernel(x_ref, *refs):
-    normed = jnp.concatenate([ref[...] for ref in refs[:X_COUNT]], axis=0)
-    grads = jnp.concatenate([ref[...] for ref in refs[X_COUNT : 2 * X_COUNT]], axis=0)
-    refs = refs[2 * X_COUNT :]
-    up_ref, down_ref = refs[2 * PIECES :]
-    hid_width = up_ref.shape[1]
-    grad_pre = jnp.concatenate([c[:, :hid_width] for c in whole_chunks(refs[:PIECES])], axis=0)
-    up_ref[...] = lax.dot_general(
-        normed, grad_pre, (((0,), (0,)), ((), ())), preferred_element_type=f32
-    ).astype(bf16)
-    hidden = jnp.concatenate(whole_chunks(refs[PIECES : 2 * PIECES]), axis=0)
-    down_ref[...] = lax.dot_general(
-        hidden, grads, (((0,), (0,)), ((), ())), preferred_element_type=f32
-    ).astype(bf16)
-
-
-def on_device(kernel, out_shape, x, *arrays):
+def output_kernel(left_ref, right_ref, down_ref, out_ref):
+    cut = left_ref.shape[1]
+    part = jnp.dot(left_ref[...], down_ref[:cut], preferred_element_type=f32) + jnp.dot(
+        right_ref[...], down_ref[cut:], preferred_element_type=f32
+    )
+    out_ref[...] = part.astype(bf16).reshape(out_ref.shape)
+
+
+def weight_grads_kernel(
+    normed_ref, both_ref, pre_left_ref, pre_right_ref, hid_left_ref, hid_right_ref, up_ref, down_ref
+):
+    width, hid_width = up_ref.shape
+    normed = normed_ref[...].reshape(ROWS, width)
+    grads = both_ref[:, 32:, :].reshape(ROWS, width)
+    rows_in = (((0,), (0,)), ((), ()))
+    cut = pre_left_ref.shape[1]
+    up_ref[:, :cut] = lax.dot_general(
+        normed, pre_left_ref[...], rows_in, preferred_element_type=f32
+    ).astype(bf16)
+    up_ref[:, cut:] = lax.dot_general(
+        normed, pre_right_ref[:, : hid_width - cut], rows_in, preferred_element_type=f32
+    ).astype(bf16)
+    cut = hid_left_ref.shape[1]
+    down_ref[:cut] = lax.dot_general(
+        hid_left_ref[...], grads, rows_in, preferred_element_type=f32
+    ).astype(bf16)
+    down_ref[cut:] = lax.dot_general(
+        hid_right_ref[...], grads, rows_in, preferred_element_type=f32
+    ).astype(bf16)
+
+
+def on_device(kernel, out_shape, *arrays):
     vmem = pl.BlockSpec(memory_space=pltpu.VMEM)
     return pl.pallas_call(
         kernel,
         out_shape=out_shape,
-        in_specs=[pl.BlockSpec(memory_space=pltpu.SMEM)] + [vmem] * len(arrays),
+        in_specs=[vmem] * len(arrays),
         out_specs=jax.tree.map(lambda _: vmem, out_shape),
-    )(x.reshape(1).astype(jnp.int32), *arrays)
+    )(*arrays)
 
 
 def per_device(inputs, cotangent, up_weight, down_weight, norm_gain):
@@ -237,33 +224,27 @@
     grad_pre_own = spread_z(jnp.concatenate([grad_pre, extra], axis=1))
     hidden_own = spread_z(hidden)
 
-    def gather_x(own):
-        after = shift_x(own, -1)
-        before = shift_x(own, 1)
-        upper = shift_x(before[: CHUNK // 2], 1)
-        lower = shift_x(after[CHUNK // 2 :], -1)
-        return [own, after, upper, lower, before]
-
-    wide_chunks = gather_x(grad_pre_own)
-    hidden_chunks = gather_x(hidden_own)
-
+    def gather_x(own, cut):
+        parts = (own[:, :cut], own[:, cut:])
+        return [
+            lax.all_gather(part, "tensor", axis=0, tiled=True, axis_index_groups=X_GROUPS)
+            for part in parts
+        ]
+
+    wide_parts = gather_x(grad_pre_own, hid_width // 2)
     dx_part = on_device(
         input_grad_kernel,
         jax.ShapeDtypeStruct((SECTIONS, 32, width + 128), bf16),
-        x,
-        *wide_chunks,
+        *wide_parts,
         up_weight,
         both,
         row_info,
         norm_gain.reshape(1, width),
     )
     swapped = lax.all_to_all(dx_part, "section", 0, 0, tiled=True)
+    hidden_parts = gather_x(hidden_own, hid_width // 2)
     out_part = on_device(
-        output_kernel,
-        jax.ShapeDtypeStruct((SECTIONS, 32, width), bf16),
-        x,
-        *hidden_chunks,
-        down_weight,
+        output_kernel, jax.ShapeDtypeStruct((SECTIONS, 32, width), bf16), *hidden_parts, down_weight
     )
     swapped_out = lax.all_to_all(out_part, "section", 0, 0, tiled=True)
 
@@ -273,11 +254,10 @@
             jax.ShapeDtypeStruct((width, hid_width), bf16),
             jax.ShapeDtypeStruct((hid_width, width), bf16),
         ),
-        x,
-        *normed_chunks,
-        *g_chunks,
-        *wide_chunks,
-        *hidden_chunks,
+        normed_three,
+        both,
+        *wide_parts,
+        *hidden_parts,
     )
 
     states = (in_rows.astype(f32) + added(swapped_out)).astype(bf16)

time: 239 us -> 244 us (1.021)
  blocking collectives: 23.5 us -> 73.1 us
  starting transfers between devices: 87.5 us -> 66 us
  waiting for transfers between devices: 91.3 us -> 70.5 us
    all_gather x0 -> x4, blocking collectives: none -> 49.6 us  [gather_x(): lax.all_gather(part, 'tensor', axis=0, tiled=True, axis_index_groups=X_GR...]
    ppermute x14 -> x6, starting transfers between devices: 46.2 us -> 19.5 us  [shift_x(): return lax.ppermute(value, 'tensor', pairs)]
    ppermute x14 -> x6, waiting for transfers between devices: 38 us -> 17.2 us  [shift_x(): return lax.ppermute(value, 'tensor', pairs)]
    all_to_all x1, starting transfers between devices: 8.37 us -> 11 us  [per_device(): swapped = lax.all_to_all(dx_part, 'section', 0, 0, tiled=True)]
    all_to_all x1, starting transfers between devices: 6.83 us -> 9.33 us  [per_device(): swapped_out = lax.all_to_all(out_part, 'section', 0, 0, tiled=True)]
  transfers between devices with their start and end apart: 21 -> 13, of which waited for: 13 -> 7; matrix products, arithmetic and copies ran while one was open for 6% -> 5% of each run, Pallas kernels for 5% -> 5%
where the time goes in v3:
time: 244 us; the launch traced here: 243 us
  blocking collectives  73.1 us (30%)
  waiting for transfers between devices  70.5 us (29%)
  starting transfers between devices  66 us (27%)
  Pallas kernels  12.3 us (5%)
  other arithmetic  8.44 us (3%)
  matrix products  6.04 us (2%)
  local copies, waits for them, and re-layouts  5.37 us (2%)
    all_gather x4, blocking collectives, gather_x(): lax.all_gather(part, 'tensor', axis=0, tiled=True, axis_index_groups=X_GR...  49.6 us
    all_to_all x2, waiting for transfers between devices, reduce_chunks(): lax.all_to_all(pieces, 'tensor', 0, 0, tiled=True, axis_index_groups=Z_GR...  27.2 us
    all_gather x1, blocking collectives, per_device(): lax.all_gather(jnp.concatenate([in_rows, grad_rows], axis=0), 'section',...  23.5 us
    ppermute x6, starting transfers between devices, shift_x(): return lax.ppermute(value, 'tensor', pairs)  19.5 us
    ppermute x6, waiting for transfers between devices, shift_x(): return lax.ppermute(value, 'tensor', pairs)  17.2 us
    all_to_all x2, waiting for transfers between devices, spread_z(): lax.all_to_all(copies, 'tensor', 0, 0, tiled=True, axis_index_groups=Z_GR...  14.9 us
    pallas_call x3, Pallas kernels, on_device(): pl.pallas_call(kernel, out_shape=out_shape, in_specs=[vmem] * len(arrays)...  12.3 us
    all_to_all x1, starting transfers between devices, per_device(): swapped = lax.all_to_all(dx_part, 'section', 0, 0, tiled=True)  11 us
  transfers between devices with their start and end apart: 13, of which 7 were waited for; matrix products, arithmetic and copies ran while one was open for 5% of the time, Pallas kernels for 5%

profile of v3, /device:TPU:1, one launch (start us, length us, event | category | flops | bytes accessed | tf_op | source)
XLA Modules:
  0.0 242.9 jit_solution(8947996063410935691)
XLA Ops:
  0.6 0.8 reduce-precision_convert_fusion.1
  1.4 0.8 pad_maximum_fusion.1
  2.2 23.5 %all_gather.15 = bf16[1024,384]{1,0:T(8,128)(2,1)S(1)} all-gather(bf16[64,384]{1,0:T(8,128)(2,1)S(1)} %pad_maximum_fusion.1), channel_id=1, replica_groups=mesh['section'=16,'tensor'=32] {'section'}, dimensions={0}, use_global_device_ids=true | all-gather | bytes 835584 | tf_op jit(solution)/shard_map/all_gather | solution.py:161
  25.7 0.2 convert_reduce_fusion
  25.9 0.1 reshape.323
  26.0 0.1 reshape.324
  26.1 0.3 convolution_reduce_fusion
  26.4 0.8 broadcast_in_dim.79
  27.2 10.5 %all-to-all-start = ((f32[32,20,128]{2,1,0:T(8,128)}), f32[32,20,128]{2,1,0:T(8,128)S(1)}, u32[]{:S(2)}, u32[]{:S(2)}) async-start(f32[32,20,128]{2,1,0:T(8,128)} %broadcast_in_dim.79), calls=%async_computation | async-start | bytes 786432 | tf_op jit(solution)/shard_map/all_to_all | solution.py:53
  37.7 0.7 constant_dynamic-slice_fusion.7
  38.4 1.3 convolution_convert_fusion.2
  39.7 4.6 %collective-permute-start.3 = (bf16[128,1536]{1,0:T(8,128)(2,1)}, bf16[128,1536]{1,0:T(8,128)(2,1)}, u32[]{:S(2)}, u32[]{:S(2)}) collective-permute-start(bf16[128,1536]{1,0:T(8,128)(2,1)} %convolution_convert_fusion.2), channel_id=1, source_target_pairs={{0,16},{1,17},{2,18},{3,19},{4,20},{5,21},{6,22},{7,23},{8,24},{9,... | collective-permute-start | bytes 1179656 | tf_op jit(solution)/shard_map/ppermute | solution.py:47
  44.3 1.2 convolution_convert_fusion.1
  45.6 2.3 collective-permute-start.4
  48.0 1.2 convolution_convert_fusion.7
  49.2 0.6 all-to-all-done
  49.8 0.1 sub.76
  49.9 0.1 reshape.326
  50.0 0.2 fusion.3.normed_ref
  50.2 0.1 constant_dynamic-slice_fusion.6
  50.3 0.4 convolution_convert_fusion.3
  50.7 0.3 copy-done.3
  51.0 0.4 convolution_convert_fusion.4
  51.4 0.4 convolution_convert_fusion.5
  51.7 4.1 %collective-permute-start = (bf16[128,1536]{1,0:T(8,128)(2,1)S(1)}, bf16[128,1536]{1,0:T(8,128)(2,1)S(1)}, u32[]{:S(2)}, u32[]{:S(2)}) collective-permute-start(bf16[128,1536]{1,0:T(8,128)(2,1)S(1)} %convolution_convert_fusion.5), channel_id=1, source_target_pairs={{0,16},{1,17},{2,18},{3,19},{4,20},{5,21},{6,22},{7,23},{8,24},{9,... | collective-permute-start | bytes 1179656 | tf_op jit(solution)/shard_map/ppermute | solution.py:47
  55.9 2.3 collective-permute-start.1
  58.2 4.2 %collective-permute-start.2 = (bf16[128,1536]{1,0:T(8,128)(2,1)S(1)}, bf16[128,1536]{1,0:T(8,128)(2,1)S(1)}, u32[]{:S(2)}, u32[]{:S(2)}) collective-permute-start(bf16[128,1536]{1,0:T(8,128)(2,1)S(1)} %convolution_convert_fusion.3), channel_id=1, source_target_pairs={{0,24},{1,25},{2,26},{3,27},{4,28},{5,29},{6,30},{7,31},{8,0},{9,1... | collective-permute-start | bytes 1179656 | tf_op jit(solution)/shard_map/ppermute | solution.py:47
  62.4 0.5 convolution_convert_fusion
  62.9 0.4 convolution_convert_fusion.6
  63.3 10.2 %collective-permute-done = bf16[128,1536]{1,0:T(8,128)(2,1)S(1)} collective-permute-done((bf16[128,1536]{1,0:T(8,128)(2,1)S(1)}, bf16[128,1536]{1,0:T(8,128)(2,1)S(1)}, u32[]{:S(2)}, u32[]{:S(2)}) %collective-permute-start) | collective-permute-done | bytes 393248 | tf_op jit(solution)/shard_map/ppermute | solution.py:47
  73.5 1.9 collective-permute-start.5
  75.4 7.0 %collective-permute-done.1 = bf16[128,1536]{1,0:T(8,128)(2,1)S(1)} collective-permute-done((bf16[128,1536]{1,0:T(8,128)(2,1)S(1)}, bf16[128,1536]{1,0:T(8,128)(2,1)S(1)}, u32[]{:S(2)}, u32[]{:S(2)}) %collective-permute-start.1) | collective-permute-done | bytes 393248 | tf_op jit(solution)/shard_map/ppermute | solution.py:47
  82.4 1.0 add_convert_fusion.1
  83.3 5.3 %all-to-all-start.1 = ((bf16[8,16,1536]{2,1,0:T(8,128)(2,1)}), bf16[8,16,1536]{2,1,0:T(8,128)(2,1)S(1)}, u32[]{:S(2)}, u32[]{:S(2)}) async-start(bf16[8,16,1536]{2,1,0:T(8,128)(2,1)} %bitcast.25), calls=%async_computation.1 | async-start | bytes 786432 | tf_op jit(solution)/shard_map/all_to_all | solution.py:76
  88.7 2.1 add_convert_fusion
  90.7 13.0 %all-to-all-done.1 = bf16[8,16,1536]{2,1,0:T(8,128)(2,1)S(1)} async-done(((bf16[8,16,1536]{2,1,0:T(8,128)(2,1)}), bf16[8,16,1536]{2,1,0:T(8,128)(2,1)S(1)}, u32[]{:S(2)}, u32[]{:S(2)}) %all-to-all-start.1) | async-done | bytes 393248 | tf_op jit(solution)/shard_map/all_to_all | solution.py:76
  103.8 3.5 %all-to-all-start.4 = ((bf16[8,16,1536]{2,1,0:T(8,128)(2,1)}), bf16[8,16,1536]{2,1,0:T(8,128)(2,1)S(1)}, u32[]{:S(2)}, u32[]{:S(2)}) async-start(bf16[8,16,1536]{2,1,0:T(8,128)(2,1)} %bitcast.35), calls=%async_computation.4 | async-start | bytes 786432 | tf_op jit(solution)/shard_map/all_to_all | solution.py:76
  107.3 0.9 broadcast_select_fusion.rows_ref
  108.2 14.1 %all-to-all-done.4 = bf16[8,16,1536]{2,1,0:T(8,128)(2,1)S(1)} async-done(((bf16[8,16,1536]{2,1,0:T(8,128)(2,1)}), bf16[8,16,1536]{2,1,0:T(8,128)(2,1)S(1)}, u32[]{:S(2)}, u32[]{:S(2)}) %all-to-all-start.4) | async-done | bytes 393248 | tf_op jit(solution)/shard_map/all_to_all | solution.py:76
  122.3 0.3 fusion.4
  122.6 0.8 broadcast_in_dim.83
  123.4 3.5 %all-to-all-start.2 = ((bf16[8,16,1536]{2,1,0:T(8,128)(2,1)}), bf16[8,16,1536]{2,1,0:T(8,128)(2,1)S(1)}, u32[]{:S(2)}, u32[]{:S(2)}) async-start(bf16[8,16,1536]{2,1,0:T(8,128)(2,1)} %broadcast_in_dim.83), calls=%async_computation.2 | async-start | bytes 786432 | tf_op jit(solution)/shard_map/all_to_all | solution.py:81
  126.9 0.1 select_select_fusion
  127.0 14.9 %all-to-all-done.2 = bf16[8,16,1536]{2,1,0:T(8,128)(2,1)S(1)} async-done(((bf16[8,16,1536]{2,1,0:T(8,128)(2,1)}), bf16[8,16,1536]{2,1,0:T(8,128)(2,1)S(1)}, u32[]{:S(2)}, u32[]{:S(2)}) %all-to-all-start.2) | async-done | bytes 393248 | tf_op jit(solution)/shard_map/all_to_all | solution.py:81
  141.9 0.8 broadcast_in_dim.91
  142.7 3.5 %all-to-all-start.5 = ((bf16[8,16,1664]{2,1,0:T(8,128)(2,1)}), bf16[8,16,1664]{2,1,0:T(8,128)(2,1)S(1)}, u32[]{:S(2)}, u32[]{:S(2)}) async-start(bf16[8,16,1664]{2,1,0:T(8,128)(2,1)} %broadcast_in_dim.91), calls=%async_computation.5 | async-start | bytes 851968 | tf_op jit(solution)/shard_map/all_to_all | solution.py:81
  146.2 11.6 %all_gather.17.right_ref.hid_right_ref = bf16[512,768]{1,0:T(8,128)(2,1)} all-gather(bf16[128,768]{1,0:T(8,128)(2,1)S(1)} %get-tuple-element.27), channel_id=1, replica_groups={{0,8,16,24},{1,9,17,25},{2,10,18,26},{3,11,19,27},{4,12,20,28},{5,13,21..., dimensions={0}, use_global_device_ids=true | all-gather | bytes 983040 | tf_op jit(solution)/shard_map/all_gather | solution.py:230
  157.8 13.0 %all_gather.16.left_ref.hid_left_ref = bf16[512,768]{1,0:T(8,128)(2,1)} all-gather(bf16[128,768]{1,0:T(8,128)(2,1)S(1)} %get-tuple-element.28), channel_id=1, replica_groups={{0,8,16,24},{1,9,17,25},{2,10,18,26},{3,11,19,27},{4,12,20,28},{5,13,21..., dimensions={0}, use_global_device_ids=true | all-gather | bytes 983040 | tf_op jit(solution)/shard_map/all_gather | solution.py:230
  170.8 3.5 %shard_map.92 = bf16[16,32,384]{2,1,0:T(8,128)(2,1)} custom-call(bf16[512,768]{1,0:T(8,128)(2,1)} %all_gather.16.left_ref.hid_left_ref, bf16[512,768]{1,0:T(8,128)(2,1)} %all_gather.17.right_ref.hid_right_ref, bf16[1536,384]{1,0:T(8,128)(2,1)} %down_ref.1), custom_call_target="tpu_custom_call" | custom-call | tf_op jit(solution)/shard_map/pallas_call | solution.py:145
  174.2 9.3 %all-to-all-start.3 = ((bf16[16,32,384]{2,1,0:T(8,128)(2,1)}), bf16[16,32,384]{2,1,0:T(8,128)(2,1)S(1)}, u32[]{:S(2)}, u32[]{:S(2)}) async-start(bf16[16,32,384]{2,1,0:T(8,128)(2,1)} %shard_map.92), calls=%async_computation.3 | async-start | bytes 786432 | tf_op jit(solution)/shard_map/all_to_all | solution.py:249
  183.6 0.6 broadcast_in_dim.92.gain_ref
  184.2 12.6 %all_gather.18.left_ref.pre_left_ref = bf16[512,768]{1,0:T(8,128)(2,1)} all-gather(bf16[128,768]{1,0:T(8,128)(2,1)S(1)} %slice.516), channel_id=1, replica_groups={{0,8,16,24},{1,9,17,25},{2,10,18,26},{3,11,19,27},{4,12,20,28},{5,13,21..., dimensions={0}, use_global_device_ids=true | all-gather | bytes 983040 | tf_op jit(solution)/shard_map/all_gather | solution.py:230
  196.8 12.5 %all_gather.19.right_ref.pre_right_ref = bf16[512,896]{1,0:T(8,128)(2,1)} all-gather(bf16[128,896]{1,0:T(8,128)(2,1)S(1)} %slice.517), channel_id=1, replica_groups={{0,8,16,24},{1,9,17,25},{2,10,18,26},{3,11,19,27},{4,12,20,28},{5,13,21..., dimensions={0}, use_global_device_ids=true | all-gather | bytes 1146880 | tf_op jit(solution)/shard_map/all_gather | solution.py:230
  209.3 3.9 %shard_map.93 = bf16[16,32,512]{2,1,0:T(8,128)(2,1)} custom-call(bf16[512,768]{1,0:T(8,128)(2,1)} %all_gather.18.left_ref.pre_left_ref, bf16[512,896]{1,0:T(8,128)(2,1)} %all_gather.19.right_ref.pre_right_ref, bf16[384,1536]{1,0:T(8,128)(2,1)} %up_ref.1, bf16[16,64,384]{2,1,0:T(8,128)(2,1)} %bitcast.169, f32[512,128]{1,0:T(8,128)} %broadcast_select_fusion.rows_ref, ...), custom_call_target="tpu_custom_call" | custom-call | tf_op jit(solution)/shard_map/pallas_call | solution.py:145
  213.2 11.0 %all-to-all-start.6 = ((bf16[16,32,512]{2,1,0:T(8,128)(2,1)}), bf16[16,32,512]{2,1,0:T(8,128)(2,1)S(1)}, u32[]{:S(2)}, u32[]{:S(2)}) async-start(bf16[16,32,512]{2,1,0:T(8,128)(2,1)} %shard_map.93), calls=%async_computation.6 | async-start | bytes 1048576 | tf_op jit(solution)/shard_map/all_to_all | solution.py:244
  224.3 0.9 dynamic-slice_reduce_fusion
  225.2 0.1 mul.159
  225.2 4.9 %shard_map.94 = (bf16[384,1536]{1,0:T(8,128)(2,1)}, bf16[1536,384]{1,0:T(8,128)(2,1)}) custom-call(bf16[16,32,384]{2,1,0:T(8,128)(2,1)} %copy-done.3, bf16[16,64,384]{2,1,0:T(8,128)(2,1)} %bitcast.170, bf16[512,768]{1,0:T(8,128)(2,1)} %all_gather.18.left_ref.pre_left_ref, bf16[512,896]{1,0:T(8,128)(2,1)} %all_gather.19.right_ref.pre_right_ref, ...), custom_call_target="tpu_custom_call" | custom-call | tf_op jit(solution)/shard_map/pallas_call | solution.py:145
  230.1 0.1 add_add_fusion.1
  230.2 0.6 fusion.24
  230.8 10.6 %all-to-all-done.6 = bf16[16,32,512]{2,1,0:T(8,128)(2,1)S(1)} async-done(((bf16[16,32,512]{2,1,0:T(8,128)(2,1)}), bf16[16,32,512]{2,1,0:T(8,128)(2,1)S(1)}, u32[]{:S(2)}, u32[]{:S(2)}) %all-to-all-start.6) | async-done | bytes 524320 | tf_op jit(solution)/shard_map/all_to_all | solution.py:244
  241.5 0.6 reduce_sum.59
  242.1 0.1 add_add_fusion
  242.2 0.7 fusion.22
  (48 shorter events, 0.3 us)
Async XLA Ops:
  0.6 25.5 %copy-start = (bf16[384,1536]{1,0:T(8,128)(2,1)S(1)}, bf16[384,1536]{1,0:T(8,128)(2,1)}, u32[]{:S(2)}) copy-start(bf16[384,1536]{1,0:T(8,128)(2,1)} %up_ref.1) | copy-start | bytes 3538948
  25.7 24.3 %copy-start.2 = (bf16[1024,384]{1,0:T(8,128)(2,1)}, bf16[1024,384]{1,0:T(8,128)(2,1)S(1)}, u32[]{:S(2)}) copy-start(bf16[1024,384]{1,0:T(8,128)(2,1)S(1)} %all_gather.15) | copy-start | bytes 2359300
  26.4 12.0 %copy-start.1 = (bf16[1536,384]{1,0:T(8,128)(2,1)S(1)}, bf16[1536,384]{1,0:T(8,128)(2,1)}, u32[]{:S(2)}) copy-start(bf16[1536,384]{1,0:T(8,128)(2,1)} %down_ref.1) | copy-start | bytes 3538948
  27.2 22.6 %all-to-all-start = ((f32[32,20,128]{2,1,0:T(8,128)}), f32[32,20,128]{2,1,0:T(8,128)S(1)}, u32[]{:S(2)}, u32[]{:S(2)}) async-start(f32[32,20,128]{2,1,0:T(8,128)} %broadcast_in_dim.79), calls=%async_computation | async-start | bytes 786432 | tf_op jit(solution)/shard_map/all_to_all | solution.py:53
  39.7 48.9 %collective-permute-start.3 = (bf16[128,1536]{1,0:T(8,128)(2,1)}, bf16[128,1536]{1,0:T(8,128)(2,1)}, u32[]{:S(2)}, u32[]{:S(2)}) collective-permute-start(bf16[128,1536]{1,0:T(8,128)(2,1)} %convolution_convert_fusion.2), channel_id=1, source_target_pairs={{0,16},{1,17},{2,18},{3,19},{4,20},{5,21},{6,22},{7,23},{8,24},{9,... | collective-permute-start | bytes 1179656 | tf_op jit(solution)/shard_map/ppermute | solution.py:47
  45.6 4.4 %copy-start.8 = (f32[384]{0:T(512)S(1)}, f32[384]{0:T(512)}, u32[]{:S(2)}) copy-start(f32[384]{0:T(512)} %param.9) | copy-start | bytes 4612
  45.6 43.1 %collective-permute-start.4 = (bf16[128,1536]{1,0:T(8,128)(2,1)}, bf16[128,1536]{1,0:T(8,128)(2,1)}, u32[]{:S(2)}, u32[]{:S(2)}) collective-permute-start(bf16[128,1536]{1,0:T(8,128)(2,1)} %convolution_convert_fusion.1), channel_id=1, source_target_pairs={{0,8},{1,9},{2,10},{3,11},{4,12},{5,13},{6,14},{7,15},{8,16},{9,17... | collective-permute-start | bytes 1179656 | tf_op jit(solution)/shard_map/ppermute | solution.py:47
  50.2 0.8 copy-start.3
  51.3 11.0 %copy-start.5 = (bf16[4,32,384]{2,1,0:T(8,128)(2,1)S(1)}, bf16[4,32,384]{2,1,0:T(8,128)(2,1)}, u32[]{:S(2)}) copy-start(bf16[4,32,384]{2,1,0:T(8,128)(2,1)} %get-tuple-element.24) | copy-start | bytes 294916
  51.7 21.8 %collective-permute-start = (bf16[128,1536]{1,0:T(8,128)(2,1)S(1)}, bf16[128,1536]{1,0:T(8,128)(2,1)S(1)}, u32[]{:S(2)}, u32[]{:S(2)}) collective-permute-start(bf16[128,1536]{1,0:T(8,128)(2,1)S(1)} %convolution_convert_fusion.5), channel_id=1, source_target_pairs={{0,16},{1,17},{2,18},{3,19},{4,20},{5,21},{6,22},{7,23},{8,24},{9,... | collective-permute-start | bytes 1179656 | tf_op jit(solution)/shard_map/ppermute | solution.py:47
  55.9 26.5 %collective-permute-start.1 = (bf16[128,1536]{1,0:T(8,128)(2,1)S(1)}, bf16[128,1536]{1,0:T(8,128)(2,1)S(1)}, u32[]{:S(2)}, u32[]{:S(2)}) collective-permute-start(bf16[128,1536]{1,0:T(8,128)(2,1)S(1)} %convolution_convert_fusion.4), channel_id=1, source_target_pairs={{0,8},{1,9},{2,10},{3,11},{4,12},{5,13},{6,14},{7,15},{8,16},{9,17... | collective-permute-start | bytes 1179656 | tf_op jit(solution)/shard_map/ppermute | solution.py:47
  58.2 24.2 %collective-permute-start.2 = (bf16[128,1536]{1,0:T(8,128)(2,1)S(1)}, bf16[128,1536]{1,0:T(8,128)(2,1)S(1)}, u32[]{:S(2)}, u32[]{:S(2)}) collective-permute-start(bf16[128,1536]{1,0:T(8,128)(2,1)S(1)} %convolution_convert_fusion.3), channel_id=1, source_target_pairs={{0,24},{1,25},{2,26},{3,27},{4,28},{5,29},{6,30},{7,31},{8,0},{9,1... | collective-permute-start | bytes 1179656 | tf_op jit(solution)/shard_map/ppermute | solution.py:47
  63.3 25.4 %copy-start.4 = (bf16[128,1536]{1,0:T(8,128)(2,1)S(1)}, bf16[128,1536]{1,0:T(8,128)(2,1)}, u32[]{:S(2)}) copy-start(bf16[128,1536]{1,0:T(8,128)(2,1)} %convolution_convert_fusion.7) | copy-start | bytes 1179652
  73.5 15.2 %collective-permute-start.5 = (bf16[128,1536]{1,0:T(8,128)(2,1)S(1)}, bf16[128,1536]{1,0:T(8,128)(2,1)S(1)}, u32[]{:S(2)}, u32[]{:S(2)}) collective-permute-start(bf16[128,1536]{1,0:T(8,128)(2,1)S(1)} %convolution_convert_fusion), channel_id=1, source_target_pairs={{0,24},{1,25},{2,26},{3,27},{4,28},{5,29},{6,30},{7,31},{8,0},{9,1... | collective-permute-start | bytes 1179656 | tf_op jit(solution)/shard_map/ppermute | solution.py:47
  83.3 20.4 %all-to-all-start.1 = ((bf16[8,16,1536]{2,1,0:T(8,128)(2,1)}), bf16[8,16,1536]{2,1,0:T(8,128)(2,1)S(1)}, u32[]{:S(2)}, u32[]{:S(2)}) async-start(bf16[8,16,1536]{2,1,0:T(8,128)(2,1)} %bitcast.25), calls=%async_computation.1 | async-start | bytes 786432 | tf_op jit(solution)/shard_map/all_to_all | solution.py:76
  103.8 18.5 %all-to-all-start.4 = ((bf16[8,16,1536]{2,1,0:T(8,128)(2,1)}), bf16[8,16,1536]{2,1,0:T(8,128)(2,1)S(1)}, u32[]{:S(2)}, u32[]{:S(2)}) async-start(bf16[8,16,1536]{2,1,0:T(8,128)(2,1)} %bitcast.35), calls=%async_computation.4 | async-start | bytes 786432 | tf_op jit(solution)/shard_map/all_to_all | solution.py:76
  123.4 18.5 %all-to-all-start.2 = ((bf16[8,16,1536]{2,1,0:T(8,128)(2,1)}), bf16[8,16,1536]{2,1,0:T(8,128)(2,1)S(1)}, u32[]{:S(2)}, u32[]{:S(2)}) async-start(bf16[8,16,1536]{2,1,0:T(8,128)(2,1)} %broadcast_in_dim.83), calls=%async_computation.2 | async-start | bytes 786432 | tf_op jit(solution)/shard_map/all_to_all | solution.py:81
  142.7 31.5 %all-to-all-start.5 = ((bf16[8,16,1664]{2,1,0:T(8,128)(2,1)}), bf16[8,16,1664]{2,1,0:T(8,128)(2,1)S(1)}, u32[]{:S(2)}, u32[]{:S(2)}) async-start(bf16[8,16,1664]{2,1,0:T(8,128)(2,1)} %broadcast_in_dim.91), calls=%async_computation.5 | async-start | bytes 851968 | tf_op jit(solution)/shard_map/all_to_all | solution.py:81
  174.2 39.0 %all-to-all-start.3 = ((bf16[16,32,384]{2,1,0:T(8,128)(2,1)}), bf16[16,32,384]{2,1,0:T(8,128)(2,1)S(1)}, u32[]{:S(2)}, u32[]{:S(2)}) async-start(bf16[16,32,384]{2,1,0:T(8,128)(2,1)} %shard_map.92), calls=%async_computation.3 | async-start | bytes 786432 | tf_op jit(solution)/shard_map/all_to_all | solution.py:249
  213.2 28.2 %all-to-all-start.6 = ((bf16[16,32,512]{2,1,0:T(8,128)(2,1)}), bf16[16,32,512]{2,1,0:T(8,128)(2,1)S(1)}, u32[]{:S(2)}, u32[]{:S(2)}) async-start(bf16[16,32,512]{2,1,0:T(8,128)(2,1)} %shard_map.93), calls=%async_computation.6 | async-start | bytes 1048576 | tf_op jit(solution)/shard_map/all_to_all | solution.py:244
  225.2 5.0 %copy-start.6 = (bf16[2,16,384]{2,1,0:T(8,128)(2,1)S(1)}, bf16[2,16,384]{2,1,0:T(8,128)(2,1)}, u32[]{:S(2)}) copy-start(bf16[2,16,384]{2,1,0:T(8,128)(2,1)} %param.5) | copy-start | bytes 73732
  230.1 12.0 %copy-start.7 = (bf16[2,16,384]{2,1,0:T(8,128)(2,1)S(1)}, bf16[2,16,384]{2,1,0:T(8,128)(2,1)}, u32[]{:S(2)}) copy-start(bf16[2,16,384]{2,1,0:T(8,128)(2,1)} %param.6) | copy-start | bytes 73732

commit v4 on v2

--- a/solution.py
+++ b/solution.py
@@ -126,15 +126,25 @@
     out_ref[:, :, width:] = jnp.broadcast_to(beside[None], (SECTIONS, 32, 128))
 
 
-def output_kernel(x_ref, *refs):
-    chunks = whole_chunks(refs[:PIECES])
-    down_ref, out_ref = refs[PIECES:]
-    width = down_ref.shape[1]
+def place_output(out_ref, chunk, part):
     per_chunk = SECTIONS // X_COUNT
-    for k in range(X_COUNT):
-        chunk = lax.rem(x_ref[0] + k, X_COUNT)
-        part = jnp.dot(chunks[k], down_ref[...], preferred_element_type=f32)
-        out_ref[pl.ds(chunk * per_chunk, per_chunk)] = part.astype(bf16).reshape(per_chunk, 32, width)
+    out_ref[pl.ds(chunk * per_chunk, per_chunk)] = part.astype(bf16).reshape(per_chunk, 32, part.shape[1])
+
+
+def near_output_kernel(x_ref, own_ref, after_ref, before_ref, down_ref, out_ref):
+    for k, ref in ((0, own_ref), (1, after_ref), (3, before_ref)):
+        part = jnp.dot(ref[...], down_ref[...], preferred_element_type=f32)
+        place_output(out_ref, lax.rem(x_ref[0] + k, X_COUNT), part)
+
+
+def far_output_kernel(x_ref, upper_ref, lower_ref, near_ref, down_ref, out_ref):
+    for k in (0, 1, 3):
+        per_chunk = SECTIONS // X_COUNT
+        there = pl.ds(lax.rem(x_ref[0] + k, X_COUNT) * per_chunk, per_chunk)
+        out_ref[there] = near_ref[there]
+    rows = jnp.concatenate([upper_ref[...], lower_ref[...]], axis=0)
+    part = jnp.dot(rows, down_ref[...], preferred_element_type=f32)
+    place_output(out_ref, lax.rem(x_ref[0] + 2, X_COUNT), part)
 
 
 def weight_grads_kernel(x_ref, *refs):
@@ -258,13 +268,10 @@
         norm_gain.reshape(1, width),
     )
     swapped = lax.all_to_all(dx_part, "section", 0, 0, tiled=True)
-    out_part = on_device(
-        output_kernel,
-        jax.ShapeDtypeStruct((SECTIONS, 32, width), bf16),
-        x,
-        *hidden_chunks,
-        down_weight,
-    )
+    own, after, upper, lower, before = hidden_chunks
+    out_shape = jax.ShapeDtypeStruct((SECTIONS, 32, width), bf16)
+    near = on_device(near_output_kernel, out_shape, x, own, after, before, down_weight)
+    out_part = on_device(far_output_kernel, out_shape, x, upper, lower, near, down_weight)
     swapped_out = lax.all_to_all(out_part, "section", 0, 0, tiled=True)
 
     grad_up, grad_down = on_device(

time: 239 us -> 238 us (level)
  starting transfers between devices: 87.5 us -> 84.4 us
  Pallas kernels: 12.8 us -> 15.2 us
    ppermute x14, starting transfers between devices: 46.2 us -> 43.1 us  [shift_x(): return lax.ppermute(value, 'tensor', pairs)]
    pallas_call x3 -> x4, Pallas kernels: 12.8 us -> 15.2 us  [on_device(): pl.pallas_call(kernel, out_shape=out_shape, in_specs=[pl.BlockSpec(memory...]
  transfers between devices with their start and end apart: 21 -> 21, of which waited for: 13 -> 12; matrix products, arithmetic and copies ran while one was open for 6% -> 6% of each run, Pallas kernels for 5% -> 6%
where the time goes in v4:
time: 238 us; the launch traced here: 237 us
  waiting for transfers between devices  91.3 us (38%)
  starting transfers between devices  84.4 us (35%)
  blocking collectives  23.5 us (10%)
  Pallas kernels  15.2 us (6%)
  other arithmetic  8.42 us (4%)
  local copies, waits for them, and re-layouts  6.52 us (3%)
  matrix products  6 us (3%)
    ppermute x14, starting transfers between devices, shift_x(): return lax.ppermute(value, 'tensor', pairs)  43.1 us
    ppermute x14, waiting for transfers between devices, shift_x(): return lax.ppermute(value, 'tensor', pairs)  37.9 us
    all_to_all x2, waiting for transfers between devices, reduce_chunks(): lax.all_to_all(pieces, 'tensor', 0, 0, tiled=True, axis_index_groups=Z_GR...  27.2 us
    all_gather x1, blocking collectives, per_device(): lax.all_gather(jnp.concatenate([in_rows, grad_rows], axis=0), 'section',...  23.5 us
    pallas_call x4, Pallas kernels, on_device(): pl.pallas_call(kernel, out_shape=out_shape, in_specs=[pl.BlockSpec(memory...  15.2 us
    all_to_all x2, waiting for transfers between devices, spread_z(): lax.all_to_all(copies, 'tensor', 0, 0, tiled=True, axis_index_groups=Z_GR...  14.9 us
    all_to_all x1, waiting for transfers between devices, per_device(): swapped = lax.all_to_all(dx_part, 'section', 0, 0, tiled=True)  10.7 us
    all_to_all x1, starting transfers between devices, share(): return added(lax.all_to_all(spread, axis, 0, 0, tiled=True))  10.5 us
  transfers between devices with their start and end apart: 21, of which 12 were waited for; matrix products, arithmetic and copies ran while one was open for 6% of the time, Pallas kernels for 6%

profile of v4, /device:TPU:1, one launch (start us, length us, event | category | flops | bytes accessed | tf_op | source)
XLA Modules:
  0.0 236.6 jit_solution(14562302049783851084)
XLA Ops:
  0.6 0.8 reduce-precision_convert_fusion.1
  1.4 0.8 pad_maximum_fusion.1
  2.2 23.5 %all_gather.3 = bf16[1024,384]{1,0:T(8,128)(2,1)S(1)} all-gather(bf16[64,384]{1,0:T(8,128)(2,1)S(1)} %pad_maximum_fusion.1), channel_id=1, replica_groups=mesh['section'=16,'tensor'=32] {'section'}, dimensions={0}, use_global_device_ids=true | all-gather | bytes 835584 | tf_op jit(solution)/shard_map/all_gather | solution.py:184
  26.1 0.3 convolution_reduce_fusion
  26.4 0.8 broadcast_in_dim.79
  27.2 10.5 %all-to-all-start = ((f32[32,20,128]{2,1,0:T(8,128)}), f32[32,20,128]{2,1,0:T(8,128)S(1)}, u32[]{:S(2)}, u32[]{:S(2)}) async-start(f32[32,20,128]{2,1,0:T(8,128)} %broadcast_in_dim.79), calls=%async_computation | async-start | bytes 786432 | tf_op jit(solution)/shard_map/all_to_all | solution.py:52
  37.7 0.7 constant_dynamic-slice_fusion.7
  38.4 1.3 convolution_convert_fusion.2
  39.7 4.6 %collective-permute-start.7 = (bf16[128,1536]{1,0:T(8,128)(2,1)}, bf16[128,1536]{1,0:T(8,128)(2,1)}, u32[]{:S(2)}, u32[]{:S(2)}) collective-permute-start(bf16[128,1536]{1,0:T(8,128)(2,1)} %convolution_convert_fusion.2), channel_id=1, source_target_pairs={{0,16},{1,17},{2,18},{3,19},{4,20},{5,21},{6,22},{7,23},{8,24},{9,... | collective-permute-start | bytes 1179656 | tf_op jit(solution)/shard_map/ppermute | solution.py:46
  44.3 1.3 convolution_convert_fusion.1
  45.6 2.4 collective-permute-start.8
  48.0 1.3 convolution_convert_fusion.7
  49.2 0.5 all-to-all-done
  50.3 0.4 convolution_convert_fusion.3
  50.7 0.4 convolution_convert_fusion.4
  51.1 0.4 convolution_convert_fusion.5
  51.5 4.1 %collective-permute-start = (bf16[128,1536]{1,0:T(8,128)(2,1)S(1)}, bf16[128,1536]{1,0:T(8,128)(2,1)S(1)}, u32[]{:S(2)}, u32[]{:S(2)}) collective-permute-start(bf16[128,1536]{1,0:T(8,128)(2,1)S(1)} %convolution_convert_fusion.5), channel_id=1, source_target_pairs={{0,16},{1,17},{2,18},{3,19},{4,20},{5,21},{6,22},{7,23},{8,24},{9,... | collective-permute-start | bytes 1179656 | tf_op jit(solution)/shard_map/ppermute | solution.py:46
  55.6 2.3 collective-permute-start.1
  57.9 4.2 %collective-permute-start.2 = (bf16[128,1536]{1,0:T(8,128)(2,1)S(1)}, bf16[128,1536]{1,0:T(8,128)(2,1)S(1)}, u32[]{:S(2)}, u32[]{:S(2)}) collective-permute-start(bf16[128,1536]{1,0:T(8,128)(2,1)S(1)} %convolution_convert_fusion.3), channel_id=1, source_target_pairs={{0,24},{1,25},{2,26},{3,27},{4,28},{5,29},{6,30},{7,31},{8,0},{9,1... | collective-permute-start | bytes 1179656 | tf_op jit(solution)/shard_map/ppermute | solution.py:46
  62.1 0.5 convolution_convert_fusion
  62.6 0.4 convolution_convert_fusion.6
  63.0 10.5 %collective-permute-done = bf16[128,1536]{1,0:T(8,128)(2,1)S(1)} collective-permute-done((bf16[128,1536]{1,0:T(8,128)(2,1)S(1)}, bf16[128,1536]{1,0:T(8,128)(2,1)S(1)}, u32[]{:S(2)}, u32[]{:S(2)}) %collective-permute-start) | collective-permute-done | bytes 393248 | tf_op jit(solution)/shard_map/ppermute | solution.py:46
  73.5 1.9 collective-permute-start.9
  75.4 7.0 %collective-permute-done.1 = bf16[128,1536]{1,0:T(8,128)(2,1)S(1)} collective-permute-done((bf16[128,1536]{1,0:T(8,128)(2,1)S(1)}, bf16[128,1536]{1,0:T(8,128)(2,1)S(1)}, u32[]{:S(2)}, u32[]{:S(2)}) %collective-permute-start.1) | collective-permute-done | bytes 393248 | tf_op jit(solution)/shard_map/ppermute | solution.py:46
  82.4 0.9 add_convert_fusion.1
  83.3 5.3 %all-to-all-start.1 = ((bf16[8,16,1536]{2,1,0:T(8,128)(2,1)}), bf16[8,16,1536]{2,1,0:T(8,128)(2,1)S(1)}, u32[]{:S(2)}, u32[]{:S(2)}) async-start(bf16[8,16,1536]{2,1,0:T(8,128)(2,1)} %bitcast.26), calls=%async_computation.1 | async-start | bytes 786432 | tf_op jit(solution)/shard_map/all_to_all | solution.py:75
  88.7 2.1 add_convert_fusion
  90.7 13.0 %all-to-all-done.1 = bf16[8,16,1536]{2,1,0:T(8,128)(2,1)S(1)} async-done(((bf16[8,16,1536]{2,1,0:T(8,128)(2,1)}), bf16[8,16,1536]{2,1,0:T(8,128)(2,1)S(1)}, u32[]{:S(2)}, u32[]{:S(2)}) %all-to-all-start.1) | async-done | bytes 393248 | tf_op jit(solution)/shard_map/all_to_all | solution.py:75
  103.7 3.5 %all-to-all-start.4 = ((bf16[8,16,1536]{2,1,0:T(8,128)(2,1)}), bf16[8,16,1536]{2,1,0:T(8,128)(2,1)S(1)}, u32[]{:S(2)}, u32[]{:S(2)}) async-start(bf16[8,16,1536]{2,1,0:T(8,128)(2,1)} %bitcast.36), calls=%async_computation.4 | async-start | bytes 786432 | tf_op jit(solution)/shard_map/all_to_all | solution.py:75
  107.2 0.9 broadcast_select_fusion.refs_7_
  108.1 14.1 %all-to-all-done.4 = bf16[8,16,1536]{2,1,0:T(8,128)(2,1)S(1)} async-done(((bf16[8,16,1536]{2,1,0:T(8,128)(2,1)}), bf16[8,16,1536]{2,1,0:T(8,128)(2,1)S(1)}, u32[]{:S(2)}, u32[]{:S(2)}) %all-to-all-start.4) | async-done | bytes 393248 | tf_op jit(solution)/shard_map/all_to_all | solution.py:75
  122.3 0.3 fusion.4
  122.6 0.8 broadcast_in_dim.83
  123.4 3.5 %all-to-all-start.2 = ((bf16[8,16,1536]{2,1,0:T(8,128)(2,1)}), bf16[8,16,1536]{2,1,0:T(8,128)(2,1)S(1)}, u32[]{:S(2)}, u32[]{:S(2)}) async-start(bf16[8,16,1536]{2,1,0:T(8,128)(2,1)} %broadcast_in_dim.83), calls=%async_computation.2 | async-start | bytes 786432 | tf_op jit(solution)/shard_map/all_to_all | solution.py:80
  127.0 14.9 %all-to-all-done.2 = bf16[8,16,1536]{2,1,0:T(8,128)(2,1)S(1)} async-done(((bf16[8,16,1536]{2,1,0:T(8,128)(2,1)}), bf16[8,16,1536]{2,1,0:T(8,128)(2,1)S(1)}, u32[]{:S(2)}, u32[]{:S(2)}) %all-to-all-start.2) | async-done | bytes 393248 | tf_op jit(solution)/shard_map/all_to_all | solution.py:80
  141.9 0.8 broadcast_in_dim.91
  142.7 3.5 %all-to-all-start.5 = ((bf16[8,16,1664]{2,1,0:T(8,128)(2,1)}), bf16[8,16,1664]{2,1,0:T(8,128)(2,1)S(1)}, u32[]{:S(2)}, u32[]{:S(2)}) async-start(bf16[8,16,1664]{2,1,0:T(8,128)(2,1)} %broadcast_in_dim.91), calls=%async_computation.5 | async-start | bytes 851968 | tf_op jit(solution)/shard_map/all_to_all | solution.py:80
  146.2 1.9 collective-permute-start.5
  148.1 3.4 %collective-permute-start.3 = (bf16[128,1536]{1,0:T(8,128)(2,1)S(1)}, bf16[128,1536]{1,0:T(8,128)(2,1)S(1)}, u32[]{:S(2)}, u32[]{:S(2)}) collective-permute-start(bf16[128,1536]{1,0:T(8,128)(2,1)S(1)} %bitcast.176), channel_id=1, source_target_pairs={{0,8},{1,9},{2,10},{3,11},{4,12},{5,13},{6,14},{7,15},{8,16},{9,17... | collective-permute-start | bytes 1179656 | tf_op jit(solution)/shard_map/ppermute | solution.py:46
  151.5 6.8 %collective-permute-done.5.after_ref.refs_14_ = bf16[128,1536]{1,0:T(8,128)(2,1)S(1)} collective-permute-done((bf16[128,1536]{1,0:T(8,128)(2,1)S(1)}, bf16[128,1536]{1,0:T(8,128)(2,1)S(1)}, u32[]{:S(2)}, u32[]{:S(2)}) %collective-permute-start.5) | collective-permute-done | bytes 393248 | tf_op jit(solution)/shard_map/ppermute | solution.py:46
  158.3 3.4 %collective-permute-start.6 = (bf16[64,1536]{1,0:T(8,128)(2,1)S(1)}, bf16[64,1536]{1,0:T(8,128)(2,1)S(1)}, u32[]{:S(2)}, u32[]{:S(2)}) collective-permute-start(bf16[64,1536]{1,0:T(8,128)(2,1)S(1)} %slice.490), channel_id=1, source_target_pairs={{0,24},{1,25},{2,26},{3,27},{4,28},{5,29},{6,30},{7,31},{8,0},{9,1... | collective-permute-start | bytes 589832 | tf_op jit(solution)/shard_map/ppermute | solution.py:46
  161.8 1.9 collective-permute-start.4
  163.7 3.2 %shard_map.92.near_ref = bf16[16,32,384]{2,1,0:T(8,128)(2,1)} custom-call(s32[1]{0:T(128)} %bitcast.x_ref, bf16[128,1536]{1,0:T(8,128)(2,1)} %bitcast.177, bf16[128,1536]{1,0:T(8,128)(2,1)} %copy-done.7, bf16[128,1536]{1,0:T(8,128)(2,1)} %copy-done.8, bf16[1536,384]{1,0:T(8,128)(2,1)} %down_ref.3), custom_call_target="tpu_custom_call" | custom-call | tf_op jit(solution)/shard_map/pallas_call | solution.py:168
  166.9 3.1 %collective-permute-done.4.upper_ref.refs_15_ = bf16[64,1536]{1,0:T(8,128)(2,1)S(1)} collective-permute-done((bf16[64,1536]{1,0:T(8,128)(2,1)S(1)}, bf16[64,1536]{1,0:T(8,128)(2,1)S(1)}, u32[]{:S(2)}, u32[]{:S(2)}) %collective-permute-start.4) | collective-permute-done | bytes 196640 | tf_op jit(solution)/shard_map/ppermute | solution.py:46
  170.0 0.7 copy-done.21
  170.7 2.7 %shard_map.93 = bf16[16,32,384]{2,1,0:T(8,128)(2,1)} custom-call(s32[1]{0:T(128)} %bitcast.x_ref, bf16[64,1536]{1,0:T(8,128)(2,1)} %copy-done.21, bf16[64,1536]{1,0:T(8,128)(2,1)} %copy-done.20, bf16[16,32,384]{2,1,0:T(8,128)(2,1)} %shard_map.92.near_ref, bf16[1536,384]{1,0:T(8,128)(2,1)} %down_ref.3), custom_call_target="tpu_custom_call" | custom-call | tf_op jit(solution)/shard_map/pallas_call | solution.py:168
  173.4 6.5 %all-to-all-start.3 = ((bf16[16,32,384]{2,1,0:T(8,128)(2,1)}), bf16[16,32,384]{2,1,0:T(8,128)(2,1)S(1)}, u32[]{:S(2)}, u32[]{:S(2)}) async-start(bf16[16,32,384]{2,1,0:T(8,128)(2,1)} %shard_map.93), calls=%async_computation.3 | async-start | bytes 786432 | tf_op jit(solution)/shard_map/all_to_all | solution.py:275
  179.9 1.9 collective-permute-start.11
  181.8 4.6 %collective-permute-start.10 = (bf16[128,1664]{1,0:T(8,128)(2,1)S(1)}, bf16[128,1664]{1,0:T(8,128)(2,1)S(1)}, u32[]{:S(2)}, u32[]{:S(2)}) collective-permute-start(bf16[128,1664]{1,0:T(8,128)(2,1)S(1)} %bitcast.172), channel_id=1, source_target_pairs={{0,24},{1,25},{2,26},{3,27},{4,28},{5,29},{6,30},{7,31},{8,0},{9,1... | collective-permute-start | bytes 1277960 | tf_op jit(solution)/shard_map/ppermute | solution.py:46
  186.4 7.9 %collective-permute-done.11.refs_4_.refs_12_ = bf16[128,1664]{1,0:T(8,128)(2,1)S(1)} collective-permute-done((bf16[128,1664]{1,0:T(8,128)(2,1)S(1)}, bf16[128,1664]{1,0:T(8,128)(2,1)S(1)}, u32[]{:S(2)}, u32[]{:S(2)}) %collective-permute-start.11) | collective-permute-done | bytes 426016 | tf_op jit(solution)/shard_map/ppermute | solution.py:46
  194.3 1.9 collective-permute-start.12
  196.3 4.6 %collective-permute-start.13 = (bf16[64,1664]{1,0:T(8,128)(2,1)S(1)}, bf16[64,1664]{1,0:T(8,128)(2,1)S(1)}, u32[]{:S(2)}, u32[]{:S(2)}) collective-permute-start(bf16[64,1664]{1,0:T(8,128)(2,1)S(1)} %slice.517), channel_id=1, source_target_pairs={{0,24},{1,25},{2,26},{3,27},{4,28},{5,29},{6,30},{7,31},{8,0},{9,1... | collective-permute-start | bytes 638984 | tf_op jit(solution)/shard_map/ppermute | solution.py:46
  200.8 0.6 broadcast_in_dim.92.refs_8_
  201.4 1.8 collective-permute-done.12.refs_2_.refs_10_
  203.2 0.9 collective-permute-done.13.refs_3_.refs_11_
  204.2 0.7 copy-done.19
  204.9 4.5 %shard_map.94 = bf16[16,32,512]{2,1,0:T(8,128)(2,1)} custom-call(s32[1]{0:T(128)} %bitcast.x_ref, bf16[128,1664]{1,0:T(8,128)(2,1)} %bitcast.173, bf16[128,1664]{1,0:T(8,128)(2,1)} %copy-done.6, bf16[64,1664]{1,0:T(8,128)(2,1)} %copy-done.18, bf16[64,1664]{1,0:T(8,128)(2,1)} %copy-done.19, bf16[128,1664]{1,0:T(8,128)(2,1)} %copy-done.5, ...), custom_call_target="tpu_custom_call" | custom-call | tf_op jit(solution)/shard_map/pallas_call | solution.py:168
  209.4 8.7 %all-to-all-start.6 = ((bf16[16,32,512]{2,1,0:T(8,128)(2,1)}), bf16[16,32,512]{2,1,0:T(8,128)(2,1)S(1)}, u32[]{:S(2)}, u32[]{:S(2)}) async-start(bf16[16,32,512]{2,1,0:T(8,128)(2,1)} %shard_map.94), calls=%async_computation.6 | async-start | bytes 1048576 | tf_op jit(solution)/shard_map/all_to_all | solution.py:270
  218.0 0.9 dynamic-slice_reduce_fusion
  219.0 4.8 %shard_map.95 = (bf16[384,1536]{1,0:T(8,128)(2,1)}, bf16[1536,384]{1,0:T(8,128)(2,1)}) custom-call(s32[1]{0:T(128)} %bitcast.x_ref, bf16[128,384]{1,0:T(8,128)(2,1)} %bitcast.188, bf16[128,384]{1,0:T(8,128)(2,1)} %bitcast.192, bf16[128,384]{1,0:T(8,128)(2,1)} %bitcast.194, bf16[128,384]{1,0:T(8,128)(2,1)} %bitcast.190, bf16[128,384]{1,0:T(8,128)(2,1)} %bitcast.180, ...), custom_call_target="tpu_custom_call" | custom-call | tf_op jit(solution)/shard_map/pallas_call | solution.py:168
  223.9 0.6 fusion.24
  224.5 10.7 %all-to-all-done.6 = bf16[16,32,512]{2,1,0:T(8,128)(2,1)S(1)} async-done(((bf16[16,32,512]{2,1,0:T(8,128)(2,1)}), bf16[16,32,512]{2,1,0:T(8,128)(2,1)S(1)}, u32[]{:S(2)}, u32[]{:S(2)}) %all-to-all-start.6) | async-done | bytes 524320 | tf_op jit(solution)/shard_map/all_to_all | solution.py:270
  235.3 0.6 reduce_sum.59
  235.9 0.7 fusion.22
  (94 shorter events, 1.4 us)
Async XLA Ops:
  0.6 25.5 %copy-start.1 = (bf16[384,1536]{1,0:T(8,128)(2,1)S(1)}, bf16[384,1536]{1,0:T(8,128)(2,1)}, u32[]{:S(2)}) copy-start(bf16[384,1536]{1,0:T(8,128)(2,1)} %refs_5_.1) | copy-start | bytes 3538948
  25.7 24.3 %copy-start.2 = (bf16[1024,384]{1,0:T(8,128)(2,1)}, bf16[1024,384]{1,0:T(8,128)(2,1)S(1)}, u32[]{:S(2)}) copy-start(bf16[1024,384]{1,0:T(8,128)(2,1)S(1)} %all_gather.3) | copy-start | bytes 2359300
  26.4 12.1 %copy-start = (bf16[1536,384]{1,0:T(8,128)(2,1)S(1)}, bf16[1536,384]{1,0:T(8,128)(2,1)}, u32[]{:S(2)}) copy-start(bf16[1536,384]{1,0:T(8,128)(2,1)} %down_ref.3) | copy-start | bytes 3538948
  27.2 22.6 %all-to-all-start = ((f32[32,20,128]{2,1,0:T(8,128)}), f32[32,20,128]{2,1,0:T(8,128)S(1)}, u32[]{:S(2)}, u32[]{:S(2)}) async-start(f32[32,20,128]{2,1,0:T(8,128)} %broadcast_in_dim.79), calls=%async_computation | async-start | bytes 786432 | tf_op jit(solution)/shard_map/all_to_all | solution.py:52
  38.4 7.2 %copy-start.12 = (bf16[4,32,384]{2,1,0:T(8,128)(2,1)}, bf16[4,32,384]{2,1,0:T(8,128)(2,1)S(1)}, u32[]{:S(2)}) copy-start(bf16[4,32,384]{2,1,0:T(8,128)(2,1)S(1)} %get-tuple-element.25) | copy-start | bytes 294916
  38.4 7.2 %copy-start.13 = (bf16[4,32,384]{2,1,0:T(8,128)(2,1)}, bf16[4,32,384]{2,1,0:T(8,128)(2,1)S(1)}, u32[]{:S(2)}) copy-start(bf16[4,32,384]{2,1,0:T(8,128)(2,1)S(1)} %get-tuple-element.26) | copy-start | bytes 294916
  38.4 9.5 %copy-start.10 = (bf16[4,32,384]{2,1,0:T(8,128)(2,1)}, bf16[4,32,384]{2,1,0:T(8,128)(2,1)S(1)}, u32[]{:S(2)}) copy-start(bf16[4,32,384]{2,1,0:T(8,128)(2,1)S(1)} %get-tuple-element.23) | copy-start | bytes 294916
  39.7 49.0 %collective-permute-start.7 = (bf16[128,1536]{1,0:T(8,128)(2,1)}, bf16[128,1536]{1,0:T(8,128)(2,1)}, u32[]{:S(2)}, u32[]{:S(2)}) collective-permute-start(bf16[128,1536]{1,0:T(8,128)(2,1)} %convolution_convert_fusion.2), channel_id=1, source_target_pairs={{0,16},{1,17},{2,18},{3,19},{4,20},{5,21},{6,22},{7,23},{8,24},{9,... | collective-permute-start | bytes 1179656 | tf_op jit(solution)/shard_map/ppermute | solution.py:46
  45.6 4.4 %copy-start.24 = (f32[384]{0:T(512)S(1)}, f32[384]{0:T(512)}, u32[]{:S(2)}) copy-start(f32[384]{0:T(512)} %param.9) | copy-start | bytes 4612
  45.6 43.0 %collective-permute-start.8 = (bf16[128,1536]{1,0:T(8,128)(2,1)}, bf16[128,1536]{1,0:T(8,128)(2,1)}, u32[]{:S(2)}, u32[]{:S(2)}) collective-permute-start(bf16[128,1536]{1,0:T(8,128)(2,1)} %convolution_convert_fusion.1), channel_id=1, source_target_pairs={{0,8},{1,9},{2,10},{3,11},{4,12},{5,13},{6,14},{7,15},{8,16},{9,17... | collective-permute-start | bytes 1179656 | tf_op jit(solution)/shard_map/ppermute | solution.py:46
  50.3 0.8 copy-start.15
  50.3 0.8 copy-start.16
  50.3 0.8 copy-start.17
  50.3 12.3 %copy-start.14 = (bf16[4,32,384]{2,1,0:T(8,128)(2,1)}, bf16[4,32,384]{2,1,0:T(8,128)(2,1)S(1)}, u32[]{:S(2)}) copy-start(bf16[4,32,384]{2,1,0:T(8,128)(2,1)S(1)} %get-tuple-element.27) | copy-start | bytes 294916
  51.1 11.0 %copy-start.11 = (bf16[4,32,384]{2,1,0:T(8,128)(2,1)S(1)}, bf16[4,32,384]{2,1,0:T(8,128)(2,1)}, u32[]{:S(2)}) copy-start(bf16[4,32,384]{2,1,0:T(8,128)(2,1)} %get-tuple-element.24) | copy-start | bytes 294916
  51.5 22.0 %collective-permute-start = (bf16[128,1536]{1,0:T(8,128)(2,1)S(1)}, bf16[128,1536]{1,0:T(8,128)(2,1)S(1)}, u32[]{:S(2)}, u32[]{:S(2)}) collective-permute-start(bf16[128,1536]{1,0:T(8,128)(2,1)S(1)} %convolution_convert_fusion.5), channel_id=1, source_target_pairs={{0,16},{1,17},{2,18},{3,19},{4,20},{5,21},{6,22},{7,23},{8,24},{9,... | collective-permute-start | bytes 1179656 | tf_op jit(solution)/shard_map/ppermute | solution.py:46
  55.6 26.8 %collective-permute-start.1 = (bf16[128,1536]{1,0:T(8,128)(2,1)S(1)}, bf16[128,1536]{1,0:T(8,128)(2,1)S(1)}, u32[]{:S(2)}, u32[]{:S(2)}) collective-permute-start(bf16[128,1536]{1,0:T(8,128)(2,1)S(1)} %convolution_convert_fusion.4), channel_id=1, source_target_pairs={{0,8},{1,9},{2,10},{3,11},{4,12},{5,13},{6,14},{7,15},{8,16},{9,17... | collective-permute-start | bytes 1179656 | tf_op jit(solution)/shard_map/ppermute | solution.py:46
  57.9 24.4 %collective-permute-start.2 = (bf16[128,1536]{1,0:T(8,128)(2,1)S(1)}, bf16[128,1536]{1,0:T(8,128)(2,1)S(1)}, u32[]{:S(2)}, u32[]{:S(2)}) collective-permute-start(bf16[128,1536]{1,0:T(8,128)(2,1)S(1)} %convolution_convert_fusion.3), channel_id=1, source_target_pairs={{0,24},{1,25},{2,26},{3,27},{4,28},{5,29},{6,30},{7,31},{8,0},{9,1... | collective-permute-start | bytes 1179656 | tf_op jit(solution)/shard_map/ppermute | solution.py:46
  63.0 25.6 %copy-start.9 = (bf16[128,1536]{1,0:T(8,128)(2,1)S(1)}, bf16[128,1536]{1,0:T(8,128)(2,1)}, u32[]{:S(2)}) copy-start(bf16[128,1536]{1,0:T(8,128)(2,1)} %convolution_convert_fusion.7) | copy-start | bytes 1179652
  73.5 15.2 %collective-permute-start.9 = (bf16[128,1536]{1,0:T(8,128)(2,1)S(1)}, bf16[128,1536]{1,0:T(8,128)(2,1)S(1)}, u32[]{:S(2)}, u32[]{:S(2)}) collective-permute-start(bf16[128,1536]{1,0:T(8,128)(2,1)S(1)} %convolution_convert_fusion), channel_id=1, source_target_pairs={{0,24},{1,25},{2,26},{3,27},{4,28},{5,29},{6,30},{7,31},{8,0},{9,1... | collective-permute-start | bytes 1179656 | tf_op jit(solution)/shard_map/ppermute | solution.py:46
  83.3 20.4 %all-to-all-start.1 = ((bf16[8,16,1536]{2,1,0:T(8,128)(2,1)}), bf16[8,16,1536]{2,1,0:T(8,128)(2,1)S(1)}, u32[]{:S(2)}, u32[]{:S(2)}) async-start(bf16[8,16,1536]{2,1,0:T(8,128)(2,1)} %bitcast.26), calls=%async_computation.1 | async-start | bytes 786432 | tf_op jit(solution)/shard_map/all_to_all | solution.py:75
  103.7 18.5 %all-to-all-start.4 = ((bf16[8,16,1536]{2,1,0:T(8,128)(2,1)}), bf16[8,16,1536]{2,1,0:T(8,128)(2,1)S(1)}, u32[]{:S(2)}, u32[]{:S(2)}) async-start(bf16[8,16,1536]{2,1,0:T(8,128)(2,1)} %bitcast.36), calls=%async_computation.4 | async-start | bytes 786432 | tf_op jit(solution)/shard_map/all_to_all | solution.py:75
  123.4 18.5 %all-to-all-start.2 = ((bf16[8,16,1536]{2,1,0:T(8,128)(2,1)}), bf16[8,16,1536]{2,1,0:T(8,128)(2,1)S(1)}, u32[]{:S(2)}, u32[]{:S(2)}) async-start(bf16[8,16,1536]{2,1,0:T(8,128)(2,1)} %broadcast_in_dim.83), calls=%async_computation.2 | async-start | bytes 786432 | tf_op jit(solution)/shard_map/all_to_all | solution.py:80
  141.9 21.8 %copy-start.4 = (bf16[8,16,1536]{2,1,0:T(8,128)(2,1)}, bf16[8,16,1536]{2,1,0:T(8,128)(2,1)S(1)}, u32[]{:S(2)}) copy-start(bf16[8,16,1536]{2,1,0:T(8,128)(2,1)S(1)} %all-to-all-done.2) | copy-start | bytes 1179652
  142.7 30.6 %all-to-all-start.5 = ((bf16[8,16,1664]{2,1,0:T(8,128)(2,1)}), bf16[8,16,1664]{2,1,0:T(8,128)(2,1)S(1)}, u32[]{:S(2)}, u32[]{:S(2)}) async-start(bf16[8,16,1664]{2,1,0:T(8,128)(2,1)} %broadcast_in_dim.91), calls=%async_computation.5 | async-start | bytes 851968 | tf_op jit(solution)/shard_map/all_to_all | solution.py:80
  146.2 12.1 %collective-permute-start.5 = (bf16[128,1536]{1,0:T(8,128)(2,1)S(1)}, bf16[128,1536]{1,0:T(8,128)(2,1)S(1)}, u32[]{:S(2)}, u32[]{:S(2)}) collective-permute-start(bf16[128,1536]{1,0:T(8,128)(2,1)S(1)} %bitcast.175), channel_id=1, source_target_pairs={{0,24},{1,25},{2,26},{3,27},{4,28},{5,29},{6,30},{7,31},{8,0},{9,1... | collective-permute-start | bytes 1179656 | tf_op jit(solution)/shard_map/ppermute | solution.py:46
  148.1 13.6 %collective-permute-start.3 = (bf16[128,1536]{1,0:T(8,128)(2,1)S(1)}, bf16[128,1536]{1,0:T(8,128)(2,1)S(1)}, u32[]{:S(2)}, u32[]{:S(2)}) collective-permute-start(bf16[128,1536]{1,0:T(8,128)(2,1)S(1)} %bitcast.176), channel_id=1, source_target_pairs={{0,8},{1,9},{2,10},{3,11},{4,12},{5,13},{6,14},{7,15},{8,16},{9,17... | collective-permute-start | bytes 1179656 | tf_op jit(solution)/shard_map/ppermute | solution.py:46
  158.3 5.4 %copy-start.7 = (bf16[128,1536]{1,0:T(8,128)(2,1)}, bf16[128,1536]{1,0:T(8,128)(2,1)S(1)}, u32[]{:S(2)}) copy-start(bf16[128,1536]{1,0:T(8,128)(2,1)S(1)} %collective-permute-done.5.after_ref.refs_14_) | copy-start | bytes 1179652
  158.3 8.6 %collective-permute-start.6 = (bf16[64,1536]{1,0:T(8,128)(2,1)S(1)}, bf16[64,1536]{1,0:T(8,128)(2,1)S(1)}, u32[]{:S(2)}, u32[]{:S(2)}) collective-permute-start(bf16[64,1536]{1,0:T(8,128)(2,1)S(1)} %slice.490), channel_id=1, source_target_pairs={{0,24},{1,25},{2,26},{3,27},{4,28},{5,29},{6,30},{7,31},{8,0},{9,1... | collective-permute-start | bytes 589832 | tf_op jit(solution)/shard_map/ppermute | solution.py:46
  161.7 2.0 copy-start.8
  161.8 8.2 %collective-permute-start.4 = (bf16[64,1536]{1,0:T(8,128)(2,1)S(1)}, bf16[64,1536]{1,0:T(8,128)(2,1)S(1)}, u32[]{:S(2)}, u32[]{:S(2)}) collective-permute-start(bf16[64,1536]{1,0:T(8,128)(2,1)S(1)} %slice.489), channel_id=1, source_target_pairs={{0,8},{1,9},{2,10},{3,11},{4,12},{5,13},{6,14},{7,15},{8,16},{9,17... | collective-permute-start | bytes 589832 | tf_op jit(solution)/shard_map/ppermute | solution.py:46
  166.9 3.1 %copy-start.20 = (bf16[64,1536]{1,0:T(8,128)(2,1)}, bf16[64,1536]{1,0:T(8,128)(2,1)S(1)}, u32[]{:S(2)}) copy-start(bf16[64,1536]{1,0:T(8,128)(2,1)S(1)} %collective-permute-done.6.lower_ref.refs_16_) | copy-start | bytes 589828
  170.0 0.7 copy-start.21
  173.4 30.8 %copy-start.3 = (bf16[8,16,1664]{2,1,0:T(8,128)(2,1)}, bf16[8,16,1664]{2,1,0:T(8,128)(2,1)S(1)}, u32[]{:S(2)}) copy-start(bf16[8,16,1664]{2,1,0:T(8,128)(2,1)S(1)} %all-to-all-done.5) | copy-start | bytes 1277956
  173.4 36.0 %all-to-all-start.3 = ((bf16[16,32,384]{2,1,0:T(8,128)(2,1)}), bf16[16,32,384]{2,1,0:T(8,128)(2,1)S(1)}, u32[]{:S(2)}, u32[]{:S(2)}) async-start(bf16[16,32,384]{2,1,0:T(8,128)(2,1)} %shard_map.93), calls=%async_computation.3 | async-start | bytes 786432 | tf_op jit(solution)/shard_map/all_to_all | solution.py:275
  179.9 14.4 %collective-permute-start.11 = (bf16[128,1664]{1,0:T(8,128)(2,1)S(1)}, bf16[128,1664]{1,0:T(8,128)(2,1)S(1)}, u32[]{:S(2)}, u32[]{:S(2)}) collective-permute-start(bf16[128,1664]{1,0:T(8,128)(2,1)S(1)} %bitcast.171), channel_id=1, source_target_pairs={{0,8},{1,9},{2,10},{3,11},{4,12},{5,13},{6,14},{7,15},{8,16},{9,17... | collective-permute-start | bytes 1277960 | tf_op jit(solution)/shard_map/ppermute | solution.py:46
  181.8 14.4 %collective-permute-start.10 = (bf16[128,1664]{1,0:T(8,128)(2,1)S(1)}, bf16[128,1664]{1,0:T(8,128)(2,1)S(1)}, u32[]{:S(2)}, u32[]{:S(2)}) collective-permute-start(bf16[128,1664]{1,0:T(8,128)(2,1)S(1)} %bitcast.172), channel_id=1, source_target_pairs={{0,24},{1,25},{2,26},{3,27},{4,28},{5,29},{6,30},{7,31},{8,0},{9,1... | collective-permute-start | bytes 1277960 | tf_op jit(solution)/shard_map/ppermute | solution.py:46
  194.3 9.9 %copy-start.5 = (bf16[128,1664]{1,0:T(8,128)(2,1)}, bf16[128,1664]{1,0:T(8,128)(2,1)S(1)}, u32[]{:S(2)}) copy-start(bf16[128,1664]{1,0:T(8,128)(2,1)S(1)} %collective-permute-done.11.refs_4_.refs_12_) | copy-start | bytes 1277956
  194.3 8.9 %collective-permute-start.12 = (bf16[64,1664]{1,0:T(8,128)(2,1)S(1)}, bf16[64,1664]{1,0:T(8,128)(2,1)S(1)}, u32[]{:S(2)}, u32[]{:S(2)}) collective-permute-start(bf16[64,1664]{1,0:T(8,128)(2,1)S(1)} %slice.516), channel_id=1, source_target_pairs={{0,8},{1,9},{2,10},{3,11},{4,12},{5,13},{6,14},{7,15},{8,16},{9,17... | collective-permute-start | bytes 638984 | tf_op jit(solution)/shard_map/ppermute | solution.py:46
  196.2 8.0 %copy-start.6 = (bf16[128,1664]{1,0:T(8,128)(2,1)}, bf16[128,1664]{1,0:T(8,128)(2,1)S(1)}, u32[]{:S(2)}) copy-start(bf16[128,1664]{1,0:T(8,128)(2,1)S(1)} %collective-permute-done.10.refs_1_.refs_9_) | copy-start | bytes 1277956
  196.3 7.9 %collective-permute-start.13 = (bf16[64,1664]{1,0:T(8,128)(2,1)S(1)}, bf16[64,1664]{1,0:T(8,128)(2,1)S(1)}, u32[]{:S(2)}, u32[]{:S(2)}) collective-permute-start(bf16[64,1664]{1,0:T(8,128)(2,1)S(1)} %slice.517), channel_id=1, source_target_pairs={{0,24},{1,25},{2,26},{3,27},{4,28},{5,29},{6,30},{7,31},{8,0},{9,1... | collective-permute-start | bytes 638984 | tf_op jit(solution)/shard_map/ppermute | solution.py:46
  203.2 1.0 copy-start.18
  204.2 0.7 copy-start.19
  209.4 25.9 %all-to-all-start.6 = ((bf16[16,32,512]{2,1,0:T(8,128)(2,1)}), bf16[16,32,512]{2,1,0:T(8,128)(2,1)S(1)}, u32[]{:S(2)}, u32[]{:S(2)}) async-start(bf16[16,32,512]{2,1,0:T(8,128)(2,1)} %shard_map.94), calls=%async_computation.6 | async-start | bytes 1048576 | tf_op jit(solution)/shard_map/all_to_all | solution.py:270
  219.0 4.9 %copy-start.22 = (bf16[2,16,384]{2,1,0:T(8,128)(2,1)S(1)}, bf16[2,16,384]{2,1,0:T(8,128)(2,1)}, u32[]{:S(2)}) copy-start(bf16[2,16,384]{2,1,0:T(8,128)(2,1)} %param.5) | copy-start | bytes 73732
  223.8 12.1 %copy-start.23 = (bf16[2,16,384]{2,1,0:T(8,128)(2,1)S(1)}, bf16[2,16,384]{2,1,0:T(8,128)(2,1)}, u32[]{:S(2)}) copy-start(bf16[2,16,384]{2,1,0:T(8,128)(2,1)} %param.6) | copy-start | bytes 73732

commit v5 on v4

--- a/solution.py
+++ b/solution.py
@@ -67,12 +67,22 @@
     return high.astype(bf16), middle.astype(bf16), low.astype(bf16)
 
 
-def reduce_chunks(own, arrived):
-    total = own.astype(f32)
-    for part in arrived:
-        total = total + part.astype(f32)
-    pieces = total.astype(bf16).reshape(Z_COUNT, CHUNK // Z_COUNT, -1)
-    return lax.all_to_all(pieces, "tensor", 0, 0, tiled=True, axis_index_groups=Z_GROUPS)
+def exchange_z(total):
+    return lax.all_to_all(total, "tensor", 0, 0, tiled=True, axis_index_groups=Z_GROUPS)
+
+
+def add_kernel(own_ref, one_ref, two_ref, three_ref, out_ref):
+    total = own_ref[...].astype(f32) + one_ref[...].astype(f32)
+    total = total + two_ref[...].astype(f32) + three_ref[...].astype(f32)
+    out_ref[...] = total.astype(bf16).reshape(out_ref.shape)
+
+
+def product_add_kernel(rows_ref, down_ref, one_ref, two_ref, three_ref, out_ref):
+    total = lax.dot_general(
+        rows_ref[...], down_ref[...], (((1,), (1,)), ((), ())), preferred_element_type=f32
+    )
+    total = total + one_ref[...].astype(f32) + two_ref[...].astype(f32) + three_ref[...].astype(f32)
+    out_ref[...] = total.astype(bf16).reshape(out_ref.shape)
 
 
 def spread_z(value):
@@ -147,7 +157,7 @@
     place_output(out_ref, lax.rem(x_ref[0] + 2, X_COUNT), part)
 
 
-def weight_grads_kernel(x_ref, *refs):
+def weight_grads_kernel(*refs):
     normed = jnp.concatenate([ref[...] for ref in refs[:X_COUNT]], axis=0)
     grads = jnp.concatenate([ref[...] for ref in refs[X_COUNT : 2 * X_COUNT]], axis=0)
     refs = refs[2 * X_COUNT :]
@@ -163,20 +173,22 @@
     ).astype(bf16)
 
 
-def on_device(kernel, out_shape, x, *arrays):
+def on_device(kernel, out_shape, *arrays, scalars=0):
     vmem = pl.BlockSpec(memory_space=pltpu.VMEM)
+    smem = pl.BlockSpec(memory_space=pltpu.SMEM)
     return pl.pallas_call(
         kernel,
         out_shape=out_shape,
-        in_specs=[pl.BlockSpec(memory_space=pltpu.SMEM)] + [vmem] * len(arrays),
+        in_specs=[smem] * scalars + [vmem] * (len(arrays) - scalars),
         out_specs=jax.tree.map(lambda _: vmem, out_shape),
-    )(x.reshape(1).astype(jnp.int32), *arrays)
+    )(*arrays)
 
 
 def per_device(inputs, cotangent, up_weight, down_weight, norm_gain):
     width = inputs.shape[2]
     hid_width = up_weight.shape[1]
     x = lax.axis_index("tensor") // Z_COUNT
+    x_scalar = x.reshape(1).astype(jnp.int32)
     section = lax.axis_index("section")
     in_rows = inputs.reshape(32, width)
     grad_rows = cotangent.reshape(32, width)
@@ -213,12 +225,11 @@
     )
     dh_arrived = [shift_x(dh_parts[k], k) for k in (2, 1, 3)]
     summed = share(row_parts, "tensor")
-    dh_own = lax.optimization_barrier(grad_hidden_part(0))
     gain_up = summed[8:].reshape(hid_width)
     mean = (summed[:4] / D).reshape(ROWS)
     scale = lax.rsqrt((summed[4:8] / D).reshape(ROWS) - mean * mean + norm_eps)
     normed = ((a_all.astype(f32) - mean[:, None]) * scale[:, None] * norm_gain).astype(bf16)
-    normed_three, dh_own = lax.optimization_barrier((normed.reshape(SECTIONS, 32, width), dh_own))
+    normed_three, g_own = lax.optimization_barrier((normed.reshape(SECTIONS, 32, width), g_chunks[0]))
     line = lax.broadcasted_iota(jnp.int32, (ROWS, 128), 1)
     row_info = jnp.where(line == 0, mean[:, None], scale[:, None])
     normed_chunks = [chunk_of(normed_three, k, 0) for k in range(X_COUNT)]
@@ -228,8 +239,11 @@
 
     pre_arrived = [shift_x(pre_part(k), k) for k in (2, 1, 3)]
     pre_own = lax.optimization_barrier(pre_part(0))
-    grad_hidden = reduce_chunks(dh_own, dh_arrived)
-    pre = reduce_chunks(pre_own, pre_arrived)
+    sums = jax.ShapeDtypeStruct((Z_COUNT, CHUNK // Z_COUNT, hid_width), bf16)
+    dh_sum = on_device(product_add_kernel, sums, g_own, down_weight, *dh_arrived)
+    grad_hidden = exchange_z(dh_sum)
+    pre_sum = on_device(add_kernel, sums, pre_own, *pre_arrived)
+    pre = exchange_z(pre_sum)
     pre, row_info = lax.optimization_barrier((pre, row_info))
     grad_hidden = added(grad_hidden)
     pre = added(pre)
@@ -260,18 +274,19 @@
     dx_part = on_device(
         input_grad_kernel,
         jax.ShapeDtypeStruct((SECTIONS, 32, width + 128), bf16),
-        x,
+        x_scalar,
         *wide_chunks,
         up_weight,
         both,
         row_info,
         norm_gain.reshape(1, width),
+        scalars=1,
     )
     swapped = lax.all_to_all(dx_part, "section", 0, 0, tiled=True)
     own, after, upper, lower, before = hidden_chunks
     out_shape = jax.ShapeDtypeStruct((SECTIONS, 32, width), bf16)
-    near = on_device(near_output_kernel, out_shape, x, own, after, before, down_weight)
-    out_part = on_device(far_output_kernel, out_shape, x, upper, lower, near, down_weight)
+    near = on_device(near_output_kernel, out_shape, x_scalar, own, after, before, down_weight, scalars=1)
+    out_part = on_device(far_output_kernel, out_shape, x_scalar, upper, lower, near, down_weight, scalars=1)
     swapped_out = lax.all_to_all(out_part, "section", 0, 0, tiled=True)
 
     grad_up, grad_down = on_device(
@@ -280,7 +295,6 @@
             jax.ShapeDtypeStruct((width, hid_width), bf16),
             jax.ShapeDtypeStruct((hid_width, width), bf16),
         ),
-        x,
         *normed_chunks,
         *g_chunks,
         *wide_chunks,

time: 238 us -> 238 us (level)
  waiting for transfers between devices: 91.3 us -> 78.3 us
  starting transfers between devices: 84.4 us -> 95.6 us
  Pallas kernels: 15.2 us -> 20.4 us
  other arithmetic: 8.42 us -> 5.42 us
    all_to_all x2, waiting for transfers between devices: 27.2 us -> 9.82 us  [exchange_z(): lax.all_to_all(total, 'tensor', 0, 0, tiled=True, axis_index_groups=Z_GRO...]
    all_to_all x1, waiting for transfers between devices: 0.55 us -> 11.4 us  [share(): return added(lax.all_to_all(spread, axis, 0, 0, tiled=True))]
    all_to_all x1, starting transfers between devices: 6.53 us -> 16.1 us  [per_device(): swapped_out = lax.all_to_all(out_part, 'section', 0, 0, tiled=True)]
    pallas_call x4 -> x6, Pallas kernels: 15.2 us -> 20.4 us  [on_device(): pl.pallas_call(kernel, out_shape=out_shape, in_specs=[smem] * scalars + [...]
    all_to_all x2, waiting for transfers between devices: 14.9 us -> 10.5 us  [spread_z(): lax.all_to_all(copies, 'tensor', 0, 0, tiled=True, axis_index_groups=Z_GR...]
    convert_element_type x2 -> x0, other arithmetic: 3 us -> none  [reduce_chunks(): pieces = total.astype(bf16).reshape(Z_COUNT, CHUNK // Z_COUNT, -1)]
    all_to_all x2, starting transfers between devices: 8.75 us -> 11.6 us  [exchange_z(): lax.all_to_all(total, 'tensor', 0, 0, tiled=True, axis_index_groups=Z_GRO...]
    dot_general x4 -> x3, matrix products: 4.27 us -> 1.5 us  [grad_hidden_part(): lax.dot_general(g_chunks[k], down_weight, (((1,), (1,)), ((), ())), prefe...]
  transfers between devices with their start and end apart: 21 -> 21, of which waited for: 12 -> 12; matrix products, arithmetic and copies ran while one was open for 6% -> 3% of each run, Pallas kernels for 6% -> 9%
where the time goes in v5:
time: 238 us; the launch traced here: 237 us
  starting transfers between devices  95.6 us (40%)
  waiting for transfers between devices  78.3 us (33%)
  blocking collectives  23.5 us (10%)
  Pallas kernels  20.4 us (9%)
  local copies, waits for them, and re-layouts  8.02 us (3%)
  other arithmetic  5.42 us (2%)
  matrix products  4 us (2%)
    ppermute x14, starting transfers between devices, shift_x(): return lax.ppermute(value, 'tensor', pairs)  41.7 us
    ppermute x14, waiting for transfers between devices, shift_x(): return lax.ppermute(value, 'tensor', pairs)  35.9 us
    all_gather x1, blocking collectives, per_device(): lax.all_gather(jnp.concatenate([in_rows, grad_rows], axis=0), 'section',...  23.5 us
    pallas_call x6, Pallas kernels, on_device(): pl.pallas_call(kernel, out_shape=out_shape, in_specs=[smem] * scalars + [...  20.4 us
    all_to_all x1, starting transfers between devices, per_device(): swapped_out = lax.all_to_all(out_part, 'section', 0, 0, tiled=True)  16.1 us
    all_to_all x2, starting transfers between devices, exchange_z(): lax.all_to_all(total, 'tensor', 0, 0, tiled=True, axis_index_groups=Z_GRO...  11.6 us
    all_to_all x1, waiting for transfers between devices, share(): return added(lax.all_to_all(spread, axis, 0, 0, tiled=True))  11.4 us
    all_to_all x1, waiting for transfers between devices, per_device(): swapped = lax.all_to_all(dx_part, 'section', 0, 0, tiled=True)  10.7 us
  transfers between devices with their start and end apart: 21, of which 12 were waited for; matrix products, arithmetic and copies ran while one was open for 3% of the time, Pallas kernels for 9%

profile of v5, /device:TPU:1, one launch (start us, length us, event | category | flops | bytes accessed | tf_op | source)
XLA Modules:
  0.0 236.6 jit_solution(2159236945566282802)
XLA Ops:
  0.6 0.8 reduce-precision_convert_fusion.1
  1.4 0.8 pad_maximum_fusion.1
  2.2 23.5 %all_gather.3 = bf16[1024,384]{1,0:T(8,128)(2,1)S(1)} all-gather(bf16[64,384]{1,0:T(8,128)(2,1)S(1)} %pad_maximum_fusion.1), channel_id=1, replica_groups=mesh['section'=16,'tensor'=32] {'section'}, dimensions={0}, use_global_device_ids=true | all-gather | bytes 835584 | tf_op jit(solution)/shard_map/all_gather | solution.py:196
  26.4 0.8 broadcast_in_dim.79
  27.2 10.6 %all-to-all-start = ((f32[32,20,128]{2,1,0:T(8,128)}), f32[32,20,128]{2,1,0:T(8,128)S(1)}, u32[]{:S(2)}, u32[]{:S(2)}) async-start(f32[32,20,128]{2,1,0:T(8,128)} %broadcast_in_dim.79), calls=%async_computation | async-start | bytes 786432 | tf_op jit(solution)/shard_map/all_to_all | solution.py:52
  37.8 0.7 constant_dynamic-slice_fusion
  38.5 11.4 %all-to-all-done = f32[32,20,128]{2,1,0:T(8,128)S(1)} async-done(((f32[32,20,128]{2,1,0:T(8,128)}), f32[32,20,128]{2,1,0:T(8,128)S(1)}, u32[]{:S(2)}, u32[]{:S(2)}) %all-to-all-start) | async-done | bytes 327712 | tf_op jit(solution)/shard_map/all_to_all | solution.py:52
  50.4 0.4 convolution_convert_fusion.4
  50.8 0.4 convolution_convert_fusion.3
  51.2 0.4 convolution_convert_fusion.5
  51.6 4.1 %collective-permute-start = (bf16[128,1536]{1,0:T(8,128)(2,1)S(1)}, bf16[128,1536]{1,0:T(8,128)(2,1)S(1)}, u32[]{:S(2)}, u32[]{:S(2)}) collective-permute-start(bf16[128,1536]{1,0:T(8,128)(2,1)S(1)} %convolution_convert_fusion.5), channel_id=1, source_target_pairs={{0,16},{1,17},{2,18},{3,19},{4,20},{5,21},{6,22},{7,23},{8,24},{9,... | collective-permute-start | bytes 1179656 | tf_op jit(solution)/shard_map/ppermute | solution.py:46
  55.7 2.7 %collective-permute-start.2 = (bf16[128,1536]{1,0:T(8,128)(2,1)S(1)}, bf16[128,1536]{1,0:T(8,128)(2,1)S(1)}, u32[]{:S(2)}, u32[]{:S(2)}) collective-permute-start(bf16[128,1536]{1,0:T(8,128)(2,1)S(1)} %convolution_convert_fusion.3), channel_id=1, source_target_pairs={{0,24},{1,25},{2,26},{3,27},{4,28},{5,29},{6,30},{7,31},{8,0},{9,1... | collective-permute-start | bytes 1179656 | tf_op jit(solution)/shard_map/ppermute | solution.py:46
  58.5 2.5 %collective-permute-start.1 = (bf16[128,1536]{1,0:T(8,128)(2,1)S(1)}, bf16[128,1536]{1,0:T(8,128)(2,1)}, u32[]{:S(2)}, u32[]{:S(2)}) collective-permute-start(bf16[128,1536]{1,0:T(8,128)(2,1)S(1)} %convolution_convert_fusion.4), channel_id=1, source_target_pairs={{0,8},{1,9},{2,10},{3,11},{4,12},{5,13},{6,14},{7,15},{8,16},{9,17... | collective-permute-start | bytes 1179656 | tf_op jit(solution)/shard_map/ppermute | solution.py:46
  61.0 0.5 convolution_convert_fusion.2
  61.6 2.7 %collective-permute-start.7 = (bf16[128,1536]{1,0:T(8,128)(2,1)S(1)}, bf16[128,1536]{1,0:T(8,128)(2,1)}, u32[]{:S(2)}, u32[]{:S(2)}) collective-permute-start(bf16[128,1536]{1,0:T(8,128)(2,1)S(1)} %convolution_convert_fusion.2), channel_id=1, source_target_pairs={{0,16},{1,17},{2,18},{3,19},{4,20},{5,21},{6,22},{7,23},{8,24},{9,... | collective-permute-start | bytes 1179656 | tf_op jit(solution)/shard_map/ppermute | solution.py:46
  64.2 1.1 convolution_convert_fusion.6.own_ref
  65.4 9.5 %collective-permute-done.2.three_ref = bf16[128,1536]{1,0:T(8,128)(2,1)S(1)} collective-permute-done((bf16[128,1536]{1,0:T(8,128)(2,1)S(1)}, bf16[128,1536]{1,0:T(8,128)(2,1)S(1)}, u32[]{:S(2)}, u32[]{:S(2)}) %collective-permute-start.2) | collective-permute-done | bytes 393248 | tf_op jit(solution)/shard_map/ppermute | solution.py:46
  74.9 0.7 copy-done.22
  75.7 2.3 shard_map.92
  78.0 5.3 %all-to-all-start.1 = ((bf16[8,16,1536]{2,1,0:T(8,128)(2,1)}), bf16[8,16,1536]{2,1,0:T(8,128)(2,1)S(1)}, u32[]{:S(2)}, u32[]{:S(2)}) async-start(bf16[8,16,1536]{2,1,0:T(8,128)(2,1)} %shard_map.92), calls=%async_computation.1 | async-start | bytes 786432 | tf_op jit(solution)/shard_map/all_to_all | solution.py:71
  83.3 0.5 convolution_convert_fusion
  83.8 4.2 %collective-permute-start.9 = (bf16[128,1536]{1,0:T(8,128)(2,1)S(1)}, bf16[128,1536]{1,0:T(8,128)(2,1)S(1)}, u32[]{:S(2)}, u32[]{:S(2)}) collective-permute-start(bf16[128,1536]{1,0:T(8,128)(2,1)S(1)} %convolution_convert_fusion), channel_id=1, source_target_pairs={{0,24},{1,25},{2,26},{3,27},{4,28},{5,29},{6,30},{7,31},{8,0},{9,1... | collective-permute-start | bytes 1179656 | tf_op jit(solution)/shard_map/ppermute | solution.py:46
  88.0 0.5 convolution_convert_fusion.1
  88.5 1.9 collective-permute-start.8
  90.5 2.3 collective-permute-done.9.three_ref
  92.7 5.8 %collective-permute-done.8.two_ref = bf16[128,1536]{1,0:T(8,128)(2,1)S(1)} collective-permute-done((bf16[128,1536]{1,0:T(8,128)(2,1)S(1)}, bf16[128,1536]{1,0:T(8,128)(2,1)S(1)}, u32[]{:S(2)}, u32[]{:S(2)}) %collective-permute-start.8) | collective-permute-done | bytes 393248 | tf_op jit(solution)/shard_map/ppermute | solution.py:46
  98.5 0.7 copy-done.23
  99.3 2.9 %shard_map.95 = bf16[8,16,1536]{2,1,0:T(8,128)(2,1)} custom-call(bf16[128,384]{1,0:T(8,128)(2,1)} %bitcast.175, bf16[1536,384]{1,0:T(8,128)(2,1)} %down_ref.5, bf16[128,1536]{1,0:T(8,128)(2,1)} %collective-permute-done.7.one_ref, bf16[128,1536]{1,0:T(8,128)(2,1)} %copy-done.23, bf16[128,1536]{1,0:T(8,128)(2,1)} %copy-done.21), custom_call_target="tpu_custom_call" | custom-call | tf_op jit(solution)/shard_map/pallas_call | solution.py:179
  102.2 6.3 %all-to-all-start.4 = ((bf16[8,16,1536]{2,1,0:T(8,128)(2,1)}), bf16[8,16,1536]{2,1,0:T(8,128)(2,1)S(1)}, u32[]{:S(2)}, u32[]{:S(2)}) async-start(bf16[8,16,1536]{2,1,0:T(8,128)(2,1)} %shard_map.95), calls=%async_computation.4 | async-start | bytes 786432 | tf_op jit(solution)/shard_map/all_to_all | solution.py:71
  108.6 0.9 broadcast_select_fusion.refs_7_
  109.5 9.8 %all-to-all-done.4 = bf16[8,16,1536]{2,1,0:T(8,128)(2,1)S(1)} async-done(((bf16[8,16,1536]{2,1,0:T(8,128)(2,1)}), bf16[8,16,1536]{2,1,0:T(8,128)(2,1)S(1)}, u32[]{:S(2)}, u32[]{:S(2)}) %all-to-all-start.4) | async-done | bytes 393248 | tf_op jit(solution)/shard_map/all_to_all | solution.py:71
  119.3 0.3 fusion.4
  119.6 0.8 broadcast_in_dim.83
  120.4 3.5 %all-to-all-start.2 = ((bf16[8,16,1536]{2,1,0:T(8,128)(2,1)}), bf16[8,16,1536]{2,1,0:T(8,128)(2,1)S(1)}, u32[]{:S(2)}, u32[]{:S(2)}) async-start(bf16[8,16,1536]{2,1,0:T(8,128)(2,1)} %broadcast_in_dim.83), calls=%async_computation.2 | async-start | bytes 786432 | tf_op jit(solution)/shard_map/all_to_all | solution.py:90
  124.0 10.5 %all-to-all-done.2 = bf16[8,16,1536]{2,1,0:T(8,128)(2,1)S(1)} async-done(((bf16[8,16,1536]{2,1,0:T(8,128)(2,1)}), bf16[8,16,1536]{2,1,0:T(8,128)(2,1)S(1)}, u32[]{:S(2)}, u32[]{:S(2)}) %all-to-all-start.2) | async-done | bytes 393248 | tf_op jit(solution)/shard_map/all_to_all | solution.py:90
  134.5 0.8 broadcast_in_dim.91
  135.3 3.5 %all-to-all-start.5 = ((bf16[8,16,1664]{2,1,0:T(8,128)(2,1)}), bf16[8,16,1664]{2,1,0:T(8,128)(2,1)S(1)}, u32[]{:S(2)}, u32[]{:S(2)}) async-start(bf16[8,16,1664]{2,1,0:T(8,128)(2,1)} %broadcast_in_dim.91), calls=%async_computation.5 | async-start | bytes 851968 | tf_op jit(solution)/shard_map/all_to_all | solution.py:90
  138.8 1.9 collective-permute-start.5
  140.7 3.4 %collective-permute-start.3 = (bf16[128,1536]{1,0:T(8,128)(2,1)S(1)}, bf16[128,1536]{1,0:T(8,128)(2,1)S(1)}, u32[]{:S(2)}, u32[]{:S(2)}) collective-permute-start(bf16[128,1536]{1,0:T(8,128)(2,1)S(1)} %bitcast.172), channel_id=1, source_target_pairs={{0,8},{1,9},{2,10},{3,11},{4,12},{5,13},{6,14},{7,15},{8,16},{9,17... | collective-permute-start | bytes 1179656 | tf_op jit(solution)/shard_map/ppermute | solution.py:46
  144.1 3.2 %collective-permute-done.5.after_ref.refs_14_ = bf16[128,1536]{1,0:T(8,128)(2,1)S(1)} collective-permute-done((bf16[128,1536]{1,0:T(8,128)(2,1)S(1)}, bf16[128,1536]{1,0:T(8,128)(2,1)S(1)}, u32[]{:S(2)}, u32[]{:S(2)}) %collective-permute-start.5) | collective-permute-done | bytes 393248 | tf_op jit(solution)/shard_map/ppermute | solution.py:46
  147.3 3.1 %collective-permute-start.6 = (bf16[64,1536]{1,0:T(8,128)(2,1)S(1)}, bf16[64,1536]{1,0:T(8,128)(2,1)S(1)}, u32[]{:S(2)}, u32[]{:S(2)}) collective-permute-start(bf16[64,1536]{1,0:T(8,128)(2,1)S(1)} %slice.490), channel_id=1, source_target_pairs={{0,24},{1,25},{2,26},{3,27},{4,28},{5,29},{6,30},{7,31},{8,0},{9,1... | collective-permute-start | bytes 589832 | tf_op jit(solution)/shard_map/ppermute | solution.py:46
  150.5 2.2 collective-permute-start.4
  152.7 3.2 %shard_map.93.near_ref = bf16[16,32,384]{2,1,0:T(8,128)(2,1)} custom-call(s32[1]{0:T(128)} %bitcast.x_ref, bf16[128,1536]{1,0:T(8,128)(2,1)} %bitcast.173, bf16[128,1536]{1,0:T(8,128)(2,1)} %copy-done.7, bf16[128,1536]{1,0:T(8,128)(2,1)} %copy-done.8, bf16[1536,384]{1,0:T(8,128)(2,1)} %down_ref.5), custom_call_target="tpu_custom_call" | custom-call | tf_op jit(solution)/shard_map/pallas_call | solution.py:179
  155.9 4.4 %collective-permute-done.4.upper_ref.refs_15_ = bf16[64,1536]{1,0:T(8,128)(2,1)S(1)} collective-permute-done((bf16[64,1536]{1,0:T(8,128)(2,1)S(1)}, bf16[64,1536]{1,0:T(8,128)(2,1)S(1)}, u32[]{:S(2)}, u32[]{:S(2)}) %collective-permute-start.4) | collective-permute-done | bytes 196640 | tf_op jit(solution)/shard_map/ppermute | solution.py:46
  160.3 0.7 copy-done.19
  161.0 2.7 %shard_map.94 = bf16[16,32,384]{2,1,0:T(8,128)(2,1)} custom-call(s32[1]{0:T(128)} %bitcast.x_ref, bf16[64,1536]{1,0:T(8,128)(2,1)} %copy-done.19, bf16[64,1536]{1,0:T(8,128)(2,1)} %copy-done.18, bf16[16,32,384]{2,1,0:T(8,128)(2,1)} %shard_map.93.near_ref, bf16[1536,384]{1,0:T(8,128)(2,1)} %down_ref.5), custom_call_target="tpu_custom_call" | custom-call | tf_op jit(solution)/shard_map/pallas_call | solution.py:179
  163.7 16.1 %all-to-all-start.3 = ((bf16[16,32,384]{2,1,0:T(8,128)(2,1)}), bf16[16,32,384]{2,1,0:T(8,128)(2,1)S(1)}, u32[]{:S(2)}, u32[]{:S(2)}) async-start(bf16[16,32,384]{2,1,0:T(8,128)(2,1)} %shard_map.94), calls=%async_computation.3 | async-start | bytes 786432 | tf_op jit(solution)/shard_map/all_to_all | solution.py:290
  179.9 1.9 collective-permute-start.11
  181.8 4.6 %collective-permute-start.10 = (bf16[128,1664]{1,0:T(8,128)(2,1)S(1)}, bf16[128,1664]{1,0:T(8,128)(2,1)S(1)}, u32[]{:S(2)}, u32[]{:S(2)}) collective-permute-start(bf16[128,1664]{1,0:T(8,128)(2,1)S(1)} %bitcast.168), channel_id=1, source_target_pairs={{0,24},{1,25},{2,26},{3,27},{4,28},{5,29},{6,30},{7,31},{8,0},{9,1... | collective-permute-start | bytes 1277960 | tf_op jit(solution)/shard_map/ppermute | solution.py:46
  186.4 7.9 %collective-permute-done.11.refs_4_.refs_12_ = bf16[128,1664]{1,0:T(8,128)(2,1)S(1)} collective-permute-done((bf16[128,1664]{1,0:T(8,128)(2,1)S(1)}, bf16[128,1664]{1,0:T(8,128)(2,1)S(1)}, u32[]{:S(2)}, u32[]{:S(2)}) %collective-permute-start.11) | collective-permute-done | bytes 426016 | tf_op jit(solution)/shard_map/ppermute | solution.py:46
  194.2 1.9 collective-permute-start.12
  196.2 4.6 %collective-permute-start.13 = (bf16[64,1664]{1,0:T(8,128)(2,1)S(1)}, bf16[64,1664]{1,0:T(8,128)(2,1)S(1)}, u32[]{:S(2)}, u32[]{:S(2)}) collective-permute-start(bf16[64,1664]{1,0:T(8,128)(2,1)S(1)} %slice.517), channel_id=1, source_target_pairs={{0,24},{1,25},{2,26},{3,27},{4,28},{5,29},{6,30},{7,31},{8,0},{9,1... | collective-permute-start | bytes 638984 | tf_op jit(solution)/shard_map/ppermute | solution.py:46
  200.8 0.6 broadcast_in_dim.92.refs_8_
  201.4 1.8 collective-permute-done.12.refs_2_.refs_10_
  203.2 0.9 collective-permute-done.13.refs_3_.refs_11_
  204.2 0.7 copy-done.17
  204.9 4.5 %shard_map.96 = bf16[16,32,512]{2,1,0:T(8,128)(2,1)} custom-call(s32[1]{0:T(128)} %bitcast.x_ref, bf16[128,1664]{1,0:T(8,128)(2,1)} %bitcast.169, bf16[128,1664]{1,0:T(8,128)(2,1)} %copy-done.6, bf16[64,1664]{1,0:T(8,128)(2,1)} %copy-done.16, bf16[64,1664]{1,0:T(8,128)(2,1)} %copy-done.17, bf16[128,1664]{1,0:T(8,128)(2,1)} %copy-done.5, ...), custom_call_target="tpu_custom_call" | custom-call | tf_op jit(solution)/shard_map/pallas_call | solution.py:179
  209.3 8.7 %all-to-all-start.6 = ((bf16[16,32,512]{2,1,0:T(8,128)(2,1)}), bf16[16,32,512]{2,1,0:T(8,128)(2,1)S(1)}, u32[]{:S(2)}, u32[]{:S(2)}) async-start(bf16[16,32,512]{2,1,0:T(8,128)(2,1)} %shard_map.96), calls=%async_computation.6 | async-start | bytes 1048576 | tf_op jit(solution)/shard_map/all_to_all | solution.py:285
  218.0 0.9 dynamic-slice_reduce_fusion
  219.0 4.8 %shard_map.97 = (bf16[384,1536]{1,0:T(8,128)(2,1)}, bf16[1536,384]{1,0:T(8,128)(2,1)}) custom-call(bf16[128,384]{1,0:T(8,128)(2,1)} %bitcast.190, bf16[128,384]{1,0:T(8,128)(2,1)} %bitcast.186, bf16[128,384]{1,0:T(8,128)(2,1)} %bitcast.188, bf16[128,384]{1,0:T(8,128)(2,1)} %bitcast.184, bf16[128,384]{1,0:T(8,128)(2,1)} %bitcast.176, ...), custom_call_target="tpu_custom_call" | custom-call | tf_op jit(solution)/shard_map/pallas_call | solution.py:179
  223.9 0.6 fusion.24
  224.5 10.7 %all-to-all-done.6 = bf16[16,32,512]{2,1,0:T(8,128)(2,1)S(1)} async-done(((bf16[16,32,512]{2,1,0:T(8,128)(2,1)}), bf16[16,32,512]{2,1,0:T(8,128)(2,1)S(1)}, u32[]{:S(2)}, u32[]{:S(2)}) %all-to-all-start.6) | async-done | bytes 524320 | tf_op jit(solution)/shard_map/all_to_all | solution.py:285
  235.3 0.6 reduce_sum.59
  235.9 0.7 fusion.22
  (97 shorter events, 1.7 us)
Async XLA Ops:
  0.6 25.5 %copy-start.1 = (bf16[384,1536]{1,0:T(8,128)(2,1)S(1)}, bf16[384,1536]{1,0:T(8,128)(2,1)}, u32[]{:S(2)}) copy-start(bf16[384,1536]{1,0:T(8,128)(2,1)} %refs_5_.1) | copy-start | bytes 3538948
  25.7 24.4 %copy-start.2 = (bf16[1024,384]{1,0:T(8,128)(2,1)}, bf16[1024,384]{1,0:T(8,128)(2,1)S(1)}, u32[]{:S(2)}) copy-start(bf16[1024,384]{1,0:T(8,128)(2,1)S(1)} %all_gather.3) | copy-start | bytes 2359300
  27.1 23.0 %copy-start.26 = (f32[384]{0:T(512)S(1)}, f32[384]{0:T(512)}, u32[]{:S(2)}) copy-start(f32[384]{0:T(512)} %param.9) | copy-start | bytes 4612
  27.2 22.7 %all-to-all-start = ((f32[32,20,128]{2,1,0:T(8,128)}), f32[32,20,128]{2,1,0:T(8,128)S(1)}, u32[]{:S(2)}, u32[]{:S(2)}) async-start(f32[32,20,128]{2,1,0:T(8,128)} %broadcast_in_dim.79), calls=%async_computation | async-start | bytes 786432 | tf_op jit(solution)/shard_map/all_to_all | solution.py:52
  38.5 22.5 %copy-start.11 = (bf16[4,32,384]{2,1,0:T(8,128)(2,1)}, bf16[4,32,384]{2,1,0:T(8,128)(2,1)S(1)}, u32[]{:S(2)}) copy-start(bf16[4,32,384]{2,1,0:T(8,128)(2,1)S(1)} %get-tuple-element.25) | copy-start | bytes 294916
  38.5 44.7 %copy-start.9 = (bf16[4,32,384]{2,1,0:T(8,128)(2,1)}, bf16[4,32,384]{2,1,0:T(8,128)(2,1)S(1)}, u32[]{:S(2)}) copy-start(bf16[4,32,384]{2,1,0:T(8,128)(2,1)S(1)} %get-tuple-element.23) | copy-start | bytes 294916
  38.5 49.5 %copy-start.10 = (bf16[4,32,384]{2,1,0:T(8,128)(2,1)}, bf16[4,32,384]{2,1,0:T(8,128)(2,1)S(1)}, u32[]{:S(2)}) copy-start(bf16[4,32,384]{2,1,0:T(8,128)(2,1)S(1)} %get-tuple-element.24) | copy-start | bytes 294916
  50.4 0.8 copy-start.12
  50.4 0.8 copy-start.13
  50.4 0.8 copy-start.14
  50.4 13.8 %copy-start.15 = (bf16[4,32,384]{2,1,0:T(8,128)(2,1)}, bf16[4,32,384]{2,1,0:T(8,128)(2,1)S(1)}, u32[]{:S(2)}) copy-start(bf16[4,32,384]{2,1,0:T(8,128)(2,1)S(1)} %get-tuple-element.30) | copy-start | bytes 294916
  51.2 9.8 %copy-start = (bf16[1536,384]{1,0:T(8,128)(2,1)S(1)}, bf16[1536,384]{1,0:T(8,128)(2,1)}, u32[]{:S(2)}) copy-start(bf16[1536,384]{1,0:T(8,128)(2,1)} %down_ref.5) | copy-start | bytes 3538948
  51.6 13.8 %collective-permute-start = (bf16[128,1536]{1,0:T(8,128)(2,1)S(1)}, bf16[128,1536]{1,0:T(8,128)(2,1)S(1)}, u32[]{:S(2)}, u32[]{:S(2)}) collective-permute-start(bf16[128,1536]{1,0:T(8,128)(2,1)S(1)} %convolution_convert_fusion.5), channel_id=1, source_target_pairs={{0,16},{1,17},{2,18},{3,19},{4,20},{5,21},{6,22},{7,23},{8,24},{9,... | collective-permute-start | bytes 1179656 | tf_op jit(solution)/shard_map/ppermute | solution.py:46
  55.7 19.2 %collective-permute-start.2 = (bf16[128,1536]{1,0:T(8,128)(2,1)S(1)}, bf16[128,1536]{1,0:T(8,128)(2,1)S(1)}, u32[]{:S(2)}, u32[]{:S(2)}) collective-permute-start(bf16[128,1536]{1,0:T(8,128)(2,1)S(1)} %convolution_convert_fusion.3), channel_id=1, source_target_pairs={{0,24},{1,25},{2,26},{3,27},{4,28},{5,29},{6,30},{7,31},{8,0},{9,1... | collective-permute-start | bytes 1179656 | tf_op jit(solution)/shard_map/ppermute | solution.py:46
  58.5 17.2 %collective-permute-start.1 = (bf16[128,1536]{1,0:T(8,128)(2,1)S(1)}, bf16[128,1536]{1,0:T(8,128)(2,1)}, u32[]{:S(2)}, u32[]{:S(2)}) collective-permute-start(bf16[128,1536]{1,0:T(8,128)(2,1)S(1)} %convolution_convert_fusion.4), channel_id=1, source_target_pairs={{0,8},{1,9},{2,10},{3,11},{4,12},{5,13},{6,14},{7,15},{8,16},{9,17... | collective-permute-start | bytes 1179656 | tf_op jit(solution)/shard_map/ppermute | solution.py:46
  61.6 28.9 %collective-permute-start.7 = (bf16[128,1536]{1,0:T(8,128)(2,1)S(1)}, bf16[128,1536]{1,0:T(8,128)(2,1)}, u32[]{:S(2)}, u32[]{:S(2)}) collective-permute-start(bf16[128,1536]{1,0:T(8,128)(2,1)S(1)} %convolution_convert_fusion.2), channel_id=1, source_target_pairs={{0,16},{1,17},{2,18},{3,19},{4,20},{5,21},{6,22},{7,23},{8,24},{9,... | collective-permute-start | bytes 1179656 | tf_op jit(solution)/shard_map/ppermute | solution.py:46
  65.4 9.6 %copy-start.20 = (bf16[128,1536]{1,0:T(8,128)(2,1)}, bf16[128,1536]{1,0:T(8,128)(2,1)S(1)}, u32[]{:S(2)}) copy-start(bf16[128,1536]{1,0:T(8,128)(2,1)S(1)} %collective-permute-done.one_ref) | copy-start | bytes 1179652
  74.9 0.7 copy-start.22
  78.0 24.2 %all-to-all-start.1 = ((bf16[8,16,1536]{2,1,0:T(8,128)(2,1)}), bf16[8,16,1536]{2,1,0:T(8,128)(2,1)S(1)}, u32[]{:S(2)}, u32[]{:S(2)}) async-start(bf16[8,16,1536]{2,1,0:T(8,128)(2,1)} %shard_map.92), calls=%async_computation.1 | async-start | bytes 786432 | tf_op jit(solution)/shard_map/all_to_all | solution.py:71
  83.8 9.0 %collective-permute-start.9 = (bf16[128,1536]{1,0:T(8,128)(2,1)S(1)}, bf16[128,1536]{1,0:T(8,128)(2,1)S(1)}, u32[]{:S(2)}, u32[]{:S(2)}) collective-permute-start(bf16[128,1536]{1,0:T(8,128)(2,1)S(1)} %convolution_convert_fusion), channel_id=1, source_target_pairs={{0,24},{1,25},{2,26},{3,27},{4,28},{5,29},{6,30},{7,31},{8,0},{9,1... | collective-permute-start | bytes 1179656 | tf_op jit(solution)/shard_map/ppermute | solution.py:46
  88.5 10.0 %collective-permute-start.8 = (bf16[128,1536]{1,0:T(8,128)(2,1)S(1)}, bf16[128,1536]{1,0:T(8,128)(2,1)S(1)}, u32[]{:S(2)}, u32[]{:S(2)}) collective-permute-start(bf16[128,1536]{1,0:T(8,128)(2,1)S(1)} %convolution_convert_fusion.1), channel_id=1, source_target_pairs={{0,8},{1,9},{2,10},{3,11},{4,12},{5,13},{6,14},{7,15},{8,16},{9,17... | collective-permute-start | bytes 1179656 | tf_op jit(solution)/shard_map/ppermute | solution.py:46
  92.7 5.8 %copy-start.21 = (bf16[128,1536]{1,0:T(8,128)(2,1)}, bf16[128,1536]{1,0:T(8,128)(2,1)S(1)}, u32[]{:S(2)}) copy-start(bf16[128,1536]{1,0:T(8,128)(2,1)S(1)} %collective-permute-done.9.three_ref) | copy-start | bytes 1179652
  98.5 0.7 copy-start.23
  102.2 17.1 %all-to-all-start.4 = ((bf16[8,16,1536]{2,1,0:T(8,128)(2,1)}), bf16[8,16,1536]{2,1,0:T(8,128)(2,1)S(1)}, u32[]{:S(2)}, u32[]{:S(2)}) async-start(bf16[8,16,1536]{2,1,0:T(8,128)(2,1)} %shard_map.95), calls=%async_computation.4 | async-start | bytes 786432 | tf_op jit(solution)/shard_map/all_to_all | solution.py:71
  120.4 14.1 %all-to-all-start.2 = ((bf16[8,16,1536]{2,1,0:T(8,128)(2,1)}), bf16[8,16,1536]{2,1,0:T(8,128)(2,1)S(1)}, u32[]{:S(2)}, u32[]{:S(2)}) async-start(bf16[8,16,1536]{2,1,0:T(8,128)(2,1)} %broadcast_in_dim.83), calls=%async_computation.2 | async-start | bytes 786432 | tf_op jit(solution)/shard_map/all_to_all | solution.py:90
  134.5 18.2 %copy-start.4 = (bf16[8,16,1536]{2,1,0:T(8,128)(2,1)}, bf16[8,16,1536]{2,1,0:T(8,128)(2,1)S(1)}, u32[]{:S(2)}) copy-start(bf16[8,16,1536]{2,1,0:T(8,128)(2,1)S(1)} %all-to-all-done.2) | copy-start | bytes 1179652
  135.3 28.4 %all-to-all-start.5 = ((bf16[8,16,1664]{2,1,0:T(8,128)(2,1)}), bf16[8,16,1664]{2,1,0:T(8,128)(2,1)S(1)}, u32[]{:S(2)}, u32[]{:S(2)}) async-start(bf16[8,16,1664]{2,1,0:T(8,128)(2,1)} %broadcast_in_dim.91), calls=%async_computation.5 | async-start | bytes 851968 | tf_op jit(solution)/shard_map/all_to_all | solution.py:90
  138.8 8.5 %collective-permute-start.5 = (bf16[128,1536]{1,0:T(8,128)(2,1)S(1)}, bf16[128,1536]{1,0:T(8,128)(2,1)S(1)}, u32[]{:S(2)}, u32[]{:S(2)}) collective-permute-start(bf16[128,1536]{1,0:T(8,128)(2,1)S(1)} %bitcast.171), channel_id=1, source_target_pairs={{0,24},{1,25},{2,26},{3,27},{4,28},{5,29},{6,30},{7,31},{8,0},{9,1... | collective-permute-start | bytes 1179656 | tf_op jit(solution)/shard_map/ppermute | solution.py:46
  140.7 9.8 %collective-permute-start.3 = (bf16[128,1536]{1,0:T(8,128)(2,1)S(1)}, bf16[128,1536]{1,0:T(8,128)(2,1)S(1)}, u32[]{:S(2)}, u32[]{:S(2)}) collective-permute-start(bf16[128,1536]{1,0:T(8,128)(2,1)S(1)} %bitcast.172), channel_id=1, source_target_pairs={{0,8},{1,9},{2,10},{3,11},{4,12},{5,13},{6,14},{7,15},{8,16},{9,17... | collective-permute-start | bytes 1179656 | tf_op jit(solution)/shard_map/ppermute | solution.py:46
  147.3 5.4 %copy-start.7 = (bf16[128,1536]{1,0:T(8,128)(2,1)}, bf16[128,1536]{1,0:T(8,128)(2,1)S(1)}, u32[]{:S(2)}) copy-start(bf16[128,1536]{1,0:T(8,128)(2,1)S(1)} %collective-permute-done.5.after_ref.refs_14_) | copy-start | bytes 1179652
  147.3 8.5 %collective-permute-start.6 = (bf16[64,1536]{1,0:T(8,128)(2,1)S(1)}, bf16[64,1536]{1,0:T(8,128)(2,1)S(1)}, u32[]{:S(2)}, u32[]{:S(2)}) collective-permute-start(bf16[64,1536]{1,0:T(8,128)(2,1)S(1)} %slice.490), channel_id=1, source_target_pairs={{0,24},{1,25},{2,26},{3,27},{4,28},{5,29},{6,30},{7,31},{8,0},{9,1... | collective-permute-start | bytes 589832 | tf_op jit(solution)/shard_map/ppermute | solution.py:46
  150.5 2.2 copy-start.8
  150.5 9.8 %collective-permute-start.4 = (bf16[64,1536]{1,0:T(8,128)(2,1)S(1)}, bf16[64,1536]{1,0:T(8,128)(2,1)S(1)}, u32[]{:S(2)}, u32[]{:S(2)}) collective-permute-start(bf16[64,1536]{1,0:T(8,128)(2,1)S(1)} %slice.489), channel_id=1, source_target_pairs={{0,8},{1,9},{2,10},{3,11},{4,12},{5,13},{6,14},{7,15},{8,16},{9,17... | collective-permute-start | bytes 589832 | tf_op jit(solution)/shard_map/ppermute | solution.py:46
  155.9 4.5 %copy-start.18 = (bf16[64,1536]{1,0:T(8,128)(2,1)}, bf16[64,1536]{1,0:T(8,128)(2,1)S(1)}, u32[]{:S(2)}) copy-start(bf16[64,1536]{1,0:T(8,128)(2,1)S(1)} %collective-permute-done.6.lower_ref.refs_16_) | copy-start | bytes 589828
  160.3 0.7 copy-start.19
  163.7 40.4 %copy-start.3 = (bf16[8,16,1664]{2,1,0:T(8,128)(2,1)}, bf16[8,16,1664]{2,1,0:T(8,128)(2,1)S(1)}, u32[]{:S(2)}) copy-start(bf16[8,16,1664]{2,1,0:T(8,128)(2,1)S(1)} %all-to-all-done.5) | copy-start | bytes 1277956
  163.7 45.6 %all-to-all-start.3 = ((bf16[16,32,384]{2,1,0:T(8,128)(2,1)}), bf16[16,32,384]{2,1,0:T(8,128)(2,1)S(1)}, u32[]{:S(2)}, u32[]{:S(2)}) async-start(bf16[16,32,384]{2,1,0:T(8,128)(2,1)} %shard_map.94), calls=%async_computation.3 | async-start | bytes 786432 | tf_op jit(solution)/shard_map/all_to_all | solution.py:290
  179.9 14.4 %collective-permute-start.11 = (bf16[128,1664]{1,0:T(8,128)(2,1)S(1)}, bf16[128,1664]{1,0:T(8,128)(2,1)S(1)}, u32[]{:S(2)}, u32[]{:S(2)}) collective-permute-start(bf16[128,1664]{1,0:T(8,128)(2,1)S(1)} %bitcast.167), channel_id=1, source_target_pairs={{0,8},{1,9},{2,10},{3,11},{4,12},{5,13},{6,14},{7,15},{8,16},{9,17... | collective-permute-start | bytes 1277960 | tf_op jit(solution)/shard_map/ppermute | solution.py:46
  181.8 14.4 %collective-permute-start.10 = (bf16[128,1664]{1,0:T(8,128)(2,1)S(1)}, bf16[128,1664]{1,0:T(8,128)(2,1)S(1)}, u32[]{:S(2)}, u32[]{:S(2)}) collective-permute-start(bf16[128,1664]{1,0:T(8,128)(2,1)S(1)} %bitcast.168), channel_id=1, source_target_pairs={{0,24},{1,25},{2,26},{3,27},{4,28},{5,29},{6,30},{7,31},{8,0},{9,1... | collective-permute-start | bytes 1277960 | tf_op jit(solution)/shard_map/ppermute | solution.py:46
  194.2 9.9 %copy-start.5 = (bf16[128,1664]{1,0:T(8,128)(2,1)}, bf16[128,1664]{1,0:T(8,128)(2,1)S(1)}, u32[]{:S(2)}) copy-start(bf16[128,1664]{1,0:T(8,128)(2,1)S(1)} %collective-permute-done.11.refs_4_.refs_12_) | copy-start | bytes 1277956
  194.2 8.9 %collective-permute-start.12 = (bf16[64,1664]{1,0:T(8,128)(2,1)S(1)}, bf16[64,1664]{1,0:T(8,128)(2,1)S(1)}, u32[]{:S(2)}, u32[]{:S(2)}) collective-permute-start(bf16[64,1664]{1,0:T(8,128)(2,1)S(1)} %slice.516), channel_id=1, source_target_pairs={{0,8},{1,9},{2,10},{3,11},{4,12},{5,13},{6,14},{7,15},{8,16},{9,17... | collective-permute-start | bytes 638984 | tf_op jit(solution)/shard_map/ppermute | solution.py:46
  196.2 8.0 %copy-start.6 = (bf16[128,1664]{1,0:T(8,128)(2,1)}, bf16[128,1664]{1,0:T(8,128)(2,1)S(1)}, u32[]{:S(2)}) copy-start(bf16[128,1664]{1,0:T(8,128)(2,1)S(1)} %collective-permute-done.10.refs_1_.refs_9_) | copy-start | bytes 1277956
  196.2 7.9 %collective-permute-start.13 = (bf16[64,1664]{1,0:T(8,128)(2,1)S(1)}, bf16[64,1664]{1,0:T(8,128)(2,1)S(1)}, u32[]{:S(2)}, u32[]{:S(2)}) collective-permute-start(bf16[64,1664]{1,0:T(8,128)(2,1)S(1)} %slice.517), channel_id=1, source_target_pairs={{0,24},{1,25},{2,26},{3,27},{4,28},{5,29},{6,30},{7,31},{8,0},{9,1... | collective-permute-start | bytes 638984 | tf_op jit(solution)/shard_map/ppermute | solution.py:46
  203.2 1.0 copy-start.16
  204.1 0.7 copy-start.17
  209.3 25.9 %all-to-all-start.6 = ((bf16[16,32,512]{2,1,0:T(8,128)(2,1)}), bf16[16,32,512]{2,1,0:T(8,128)(2,1)S(1)}, u32[]{:S(2)}, u32[]{:S(2)}) async-start(bf16[16,32,512]{2,1,0:T(8,128)(2,1)} %shard_map.96), calls=%async_computation.6 | async-start | bytes 1048576 | tf_op jit(solution)/shard_map/all_to_all | solution.py:285
  219.0 4.9 %copy-start.24 = (bf16[2,16,384]{2,1,0:T(8,128)(2,1)S(1)}, bf16[2,16,384]{2,1,0:T(8,128)(2,1)}, u32[]{:S(2)}) copy-start(bf16[2,16,384]{2,1,0:T(8,128)(2,1)} %param.5) | copy-start | bytes 73732
  223.8 12.1 %copy-start.25 = (bf16[2,16,384]{2,1,0:T(8,128)(2,1)S(1)}, bf16[2,16,384]{2,1,0:T(8,128)(2,1)}, u32[]{:S(2)}) copy-start(bf16[2,16,384]{2,1,0:T(8,128)(2,1)} %param.6) | copy-start | bytes 73732

commit v6 on v4

--- a/solution.py
+++ b/solution.py
@@ -213,12 +213,11 @@
     )
     dh_arrived = [shift_x(dh_parts[k], k) for k in (2, 1, 3)]
     summed = share(row_parts, "tensor")
-    dh_own = lax.optimization_barrier(grad_hidden_part(0))
     gain_up = summed[8:].reshape(hid_width)
     mean = (summed[:4] / D).reshape(ROWS)
     scale = lax.rsqrt((summed[4:8] / D).reshape(ROWS) - mean * mean + norm_eps)
     normed = ((a_all.astype(f32) - mean[:, None]) * scale[:, None] * norm_gain).astype(bf16)
-    normed_three, dh_own = lax.optimization_barrier((normed.reshape(SECTIONS, 32, width), dh_own))
+    normed_three, g_chunks[0] = lax.optimization_barrier((normed.reshape(SECTIONS, 32, width), g_chunks[0]))
     line = lax.broadcasted_iota(jnp.int32, (ROWS, 128), 1)
     row_info = jnp.where(line == 0, mean[:, None], scale[:, None])
     normed_chunks = [chunk_of(normed_three, k, 0) for k in range(X_COUNT)]
@@ -228,7 +227,7 @@
 
     pre_arrived = [shift_x(pre_part(k), k) for k in (2, 1, 3)]
     pre_own = lax.optimization_barrier(pre_part(0))
-    grad_hidden = reduce_chunks(dh_own, dh_arrived)
+    grad_hidden = reduce_chunks(grad_hidden_part(0), dh_arrived)
     pre = reduce_chunks(pre_own, pre_arrived)
     pre, row_info = lax.optimization_barrier((pre, row_info))
     grad_hidden = added(grad_hidden)

time: 238 us -> 239 us (level)
  transfers between devices with their start and end apart: 21 -> 21, of which waited for: 12 -> 12; matrix products, arithmetic and copies ran while one was open for 6% -> 5% of each run, Pallas kernels for 6% -> 6%
where the time goes in v6:
time: 239 us; the launch traced here: 237 us
  waiting for transfers between devices  92.1 us (39%)
  starting transfers between devices  84.8 us (35%)
  blocking collectives  23.5 us (10%)
  Pallas kernels  15.2 us (6%)
  matrix products  7.15 us (3%)
  local copies, waits for them, and re-layouts  6.56 us (3%)
  other arithmetic  6.36 us (3%)
    ppermute x14, starting transfers between devices, shift_x(): return lax.ppermute(value, 'tensor', pairs)  43.7 us
    ppermute x14, waiting for transfers between devices, shift_x(): return lax.ppermute(value, 'tensor', pairs)  38.6 us
    all_to_all x2, waiting for transfers between devices, reduce_chunks(): lax.all_to_all(pieces, 'tensor', 0, 0, tiled=True, axis_index_groups=Z_GR...  26.7 us
    all_gather x1, blocking collectives, per_device(): lax.all_gather(jnp.concatenate([in_rows, grad_rows], axis=0), 'section',...  23.5 us
    pallas_call x4, Pallas kernels, on_device(): pl.pallas_call(kernel, out_shape=out_shape, in_specs=[pl.BlockSpec(memory...  15.2 us
    all_to_all x2, waiting for transfers between devices, spread_z(): lax.all_to_all(copies, 'tensor', 0, 0, tiled=True, axis_index_groups=Z_GR...  14.9 us
    all_to_all x1, waiting for transfers between devices, per_device(): swapped = lax.all_to_all(dx_part, 'section', 0, 0, tiled=True)  10.7 us
    all_to_all x1, starting transfers between devices, share(): return added(lax.all_to_all(spread, axis, 0, 0, tiled=True))  10.5 us
  transfers between devices with their start and end apart: 21, of which 12 were waited for; matrix products, arithmetic and copies ran while one was open for 5% of the time, Pallas kernels for 6%

profile of v6, /device:TPU:1, one launch (start us, length us, event | category | flops | bytes accessed | tf_op | source)
XLA Modules:
  0.0 237.0 jit_solution(13550340666671301586)
XLA Ops:
  0.6 0.8 reduce-precision_convert_fusion.1
  1.4 0.8 pad_maximum_fusion.1
  2.2 23.5 %all_gather.3 = bf16[1024,384]{1,0:T(8,128)(2,1)S(1)} all-gather(bf16[64,384]{1,0:T(8,128)(2,1)S(1)} %pad_maximum_fusion.1), channel_id=1, replica_groups=mesh['section'=16,'tensor'=32] {'section'}, dimensions={0}, use_global_device_ids=true | all-gather | bytes 835584 | tf_op jit(solution)/shard_map/all_gather | solution.py:184
  25.7 0.2 convert_reduce_fusion
  26.1 0.3 convolution_reduce_fusion
  26.4 0.8 broadcast_in_dim.79
  27.2 10.5 %all-to-all-start = ((f32[32,20,128]{2,1,0:T(8,128)}), f32[32,20,128]{2,1,0:T(8,128)S(1)}, u32[]{:S(2)}, u32[]{:S(2)}) async-start(f32[32,20,128]{2,1,0:T(8,128)} %broadcast_in_dim.79), calls=%async_computation | async-start | bytes 786432 | tf_op jit(solution)/shard_map/all_to_all | solution.py:52
  37.7 0.7 constant_dynamic-slice_fusion.2
  38.5 1.3 convolution_convert_fusion.1
  39.7 3.3 %collective-permute-start.8 = (bf16[128,1536]{1,0:T(8,128)(2,1)}, bf16[128,1536]{1,0:T(8,128)(2,1)}, u32[]{:S(2)}, u32[]{:S(2)}) collective-permute-start(bf16[128,1536]{1,0:T(8,128)(2,1)} %convolution_convert_fusion.1), channel_id=1, source_target_pairs={{0,8},{1,9},{2,10},{3,11},{4,12},{5,13},{6,14},{7,15},{8,16},{9,17... | collective-permute-start | bytes 1179656 | tf_op jit(solution)/shard_map/ppermute | solution.py:46
  43.0 1.3 convolution_convert_fusion.2
  44.3 4.3 %collective-permute-start.7 = (bf16[128,1536]{1,0:T(8,128)(2,1)}, bf16[128,1536]{1,0:T(8,128)(2,1)}, u32[]{:S(2)}, u32[]{:S(2)}) collective-permute-start(bf16[128,1536]{1,0:T(8,128)(2,1)} %convolution_convert_fusion.2), channel_id=1, source_target_pairs={{0,16},{1,17},{2,18},{3,19},{4,20},{5,21},{6,22},{7,23},{8,24},{9,... | collective-permute-start | bytes 1179656 | tf_op jit(solution)/shard_map/ppermute | solution.py:46
  48.6 1.2 all-to-all-done
  50.3 0.4 convolution_convert_fusion.4
  50.7 0.4 convolution_convert_fusion.5
  51.1 0.4 convolution_convert_fusion.6
  51.5 4.1 %collective-permute-start = (bf16[128,1536]{1,0:T(8,128)(2,1)S(1)}, bf16[128,1536]{1,0:T(8,128)(2,1)S(1)}, u32[]{:S(2)}, u32[]{:S(2)}) collective-permute-start(bf16[128,1536]{1,0:T(8,128)(2,1)S(1)} %convolution_convert_fusion.6), channel_id=1, source_target_pairs={{0,16},{1,17},{2,18},{3,19},{4,20},{5,21},{6,22},{7,23},{8,24},{9,... | collective-permute-start | bytes 1179656 | tf_op jit(solution)/shard_map/ppermute | solution.py:46
  55.6 2.3 collective-permute-start.1
  57.9 4.2 %collective-permute-start.2 = (bf16[128,1536]{1,0:T(8,128)(2,1)S(1)}, bf16[128,1536]{1,0:T(8,128)(2,1)S(1)}, u32[]{:S(2)}, u32[]{:S(2)}) collective-permute-start(bf16[128,1536]{1,0:T(8,128)(2,1)S(1)} %convolution_convert_fusion.4), channel_id=1, source_target_pairs={{0,24},{1,25},{2,26},{3,27},{4,28},{5,29},{6,30},{7,31},{8,0},{9,1... | collective-permute-start | bytes 1179656 | tf_op jit(solution)/shard_map/ppermute | solution.py:46
  62.1 0.5 convolution_convert_fusion
  62.6 0.4 convolution_convert_fusion.7
  63.0 11.2 %collective-permute-done = bf16[128,1536]{1,0:T(8,128)(2,1)S(1)} collective-permute-done((bf16[128,1536]{1,0:T(8,128)(2,1)S(1)}, bf16[128,1536]{1,0:T(8,128)(2,1)S(1)}, u32[]{:S(2)}, u32[]{:S(2)}) %collective-permute-start) | collective-permute-done | bytes 393248 | tf_op jit(solution)/shard_map/ppermute | solution.py:46
  74.2 1.9 collective-permute-start.9
  76.1 6.9 %collective-permute-done.1 = bf16[128,1536]{1,0:T(8,128)(2,1)S(1)} collective-permute-done((bf16[128,1536]{1,0:T(8,128)(2,1)S(1)}, bf16[128,1536]{1,0:T(8,128)(2,1)S(1)}, u32[]{:S(2)}, u32[]{:S(2)}) %collective-permute-start.1) | collective-permute-done | bytes 393248 | tf_op jit(solution)/shard_map/ppermute | solution.py:46
  83.0 0.9 add_convert_fusion.1
  83.9 5.1 %all-to-all-start.1 = ((bf16[8,16,1536]{2,1,0:T(8,128)(2,1)}), bf16[8,16,1536]{2,1,0:T(8,128)(2,1)S(1)}, u32[]{:S(2)}, u32[]{:S(2)}) async-start(bf16[8,16,1536]{2,1,0:T(8,128)(2,1)} %bitcast.26), calls=%async_computation.1 | async-start | bytes 786432 | tf_op jit(solution)/shard_map/all_to_all | solution.py:75
  89.1 2.4 %add_convert_fusion = bf16[128,1536]{1,0:T(8,128)(2,1)} fusion(bf16[128,1536]{1,0:T(8,128)(2,1)S(1)} %collective-permute-done.9, bf16[128,1536]{1,0:T(8,128)(2,1)} %collective-permute-done.8, bf16[128,1536]{1,0:T(8,128)(2,1)} %collective-permute-done.7, bf16[128,384]{1,0:T(8,128)(2,1)S(1)} %bitcast.180, bf16[1536,384]{1,0:T(8,128)(2,1)S(1)} %copy-done), kind=kOutput, calls=%fused_computation.17 | convolution fusion | flops 152764416 | bytes 2850816 | tf_op jit(solution)/shard_map/dot_general | solution.py:196
  91.5 12.6 %all-to-all-done.1 = bf16[8,16,1536]{2,1,0:T(8,128)(2,1)S(1)} async-done(((bf16[8,16,1536]{2,1,0:T(8,128)(2,1)}), bf16[8,16,1536]{2,1,0:T(8,128)(2,1)S(1)}, u32[]{:S(2)}, u32[]{:S(2)}) %all-to-all-start.1) | async-done | bytes 393248 | tf_op jit(solution)/shard_map/all_to_all | solution.py:75
  104.1 3.5 %all-to-all-start.4 = ((bf16[8,16,1536]{2,1,0:T(8,128)(2,1)}), bf16[8,16,1536]{2,1,0:T(8,128)(2,1)S(1)}, u32[]{:S(2)}, u32[]{:S(2)}) async-start(bf16[8,16,1536]{2,1,0:T(8,128)(2,1)} %bitcast.36), calls=%async_computation.4 | async-start | bytes 786432 | tf_op jit(solution)/shard_map/all_to_all | solution.py:75
  107.6 0.9 broadcast_select_fusion.refs_7_
  108.5 14.1 %all-to-all-done.4 = bf16[8,16,1536]{2,1,0:T(8,128)(2,1)S(1)} async-done(((bf16[8,16,1536]{2,1,0:T(8,128)(2,1)}), bf16[8,16,1536]{2,1,0:T(8,128)(2,1)S(1)}, u32[]{:S(2)}, u32[]{:S(2)}) %all-to-all-start.4) | async-done | bytes 393248 | tf_op jit(solution)/shard_map/all_to_all | solution.py:75
  122.7 0.3 fusion.5
  123.0 0.8 broadcast_in_dim.83
  123.8 3.5 %all-to-all-start.2 = ((bf16[8,16,1536]{2,1,0:T(8,128)(2,1)}), bf16[8,16,1536]{2,1,0:T(8,128)(2,1)S(1)}, u32[]{:S(2)}, u32[]{:S(2)}) async-start(bf16[8,16,1536]{2,1,0:T(8,128)(2,1)} %broadcast_in_dim.83), calls=%async_computation.2 | async-start | bytes 786432 | tf_op jit(solution)/shard_map/all_to_all | solution.py:80
  127.4 14.9 %all-to-all-done.2 = bf16[8,16,1536]{2,1,0:T(8,128)(2,1)S(1)} async-done(((bf16[8,16,1536]{2,1,0:T(8,128)(2,1)}), bf16[8,16,1536]{2,1,0:T(8,128)(2,1)S(1)}, u32[]{:S(2)}, u32[]{:S(2)}) %all-to-all-start.2) | async-done | bytes 393248 | tf_op jit(solution)/shard_map/all_to_all | solution.py:80
  142.3 0.8 broadcast_in_dim.91
  143.1 3.5 %all-to-all-start.5 = ((bf16[8,16,1664]{2,1,0:T(8,128)(2,1)}), bf16[8,16,1664]{2,1,0:T(8,128)(2,1)S(1)}, u32[]{:S(2)}, u32[]{:S(2)}) async-start(bf16[8,16,1664]{2,1,0:T(8,128)(2,1)} %broadcast_in_dim.91), calls=%async_computation.5 | async-start | bytes 851968 | tf_op jit(solution)/shard_map/all_to_all | solution.py:80
  146.6 1.9 collective-permute-start.5
  148.5 3.4 %collective-permute-start.3 = (bf16[128,1536]{1,0:T(8,128)(2,1)S(1)}, bf16[128,1536]{1,0:T(8,128)(2,1)S(1)}, u32[]{:S(2)}, u32[]{:S(2)}) collective-permute-start(bf16[128,1536]{1,0:T(8,128)(2,1)S(1)} %bitcast.176), channel_id=1, source_target_pairs={{0,8},{1,9},{2,10},{3,11},{4,12},{5,13},{6,14},{7,15},{8,16},{9,17... | collective-permute-start | bytes 1179656 | tf_op jit(solution)/shard_map/ppermute | solution.py:46
  151.9 6.8 %collective-permute-done.5.after_ref.refs_14_ = bf16[128,1536]{1,0:T(8,128)(2,1)S(1)} collective-permute-done((bf16[128,1536]{1,0:T(8,128)(2,1)S(1)}, bf16[128,1536]{1,0:T(8,128)(2,1)S(1)}, u32[]{:S(2)}, u32[]{:S(2)}) %collective-permute-start.5) | collective-permute-done | bytes 393248 | tf_op jit(solution)/shard_map/ppermute | solution.py:46
  158.7 3.4 %collective-permute-start.6 = (bf16[64,1536]{1,0:T(8,128)(2,1)S(1)}, bf16[64,1536]{1,0:T(8,128)(2,1)S(1)}, u32[]{:S(2)}, u32[]{:S(2)}) collective-permute-start(bf16[64,1536]{1,0:T(8,128)(2,1)S(1)} %slice.490), channel_id=1, source_target_pairs={{0,24},{1,25},{2,26},{3,27},{4,28},{5,29},{6,30},{7,31},{8,0},{9,1... | collective-permute-start | bytes 589832 | tf_op jit(solution)/shard_map/ppermute | solution.py:46
  162.1 1.9 collective-permute-start.4
  164.1 3.2 %shard_map.92.near_ref = bf16[16,32,384]{2,1,0:T(8,128)(2,1)} custom-call(s32[1]{0:T(128)} %bitcast.x_ref, bf16[128,1536]{1,0:T(8,128)(2,1)} %bitcast.177, bf16[128,1536]{1,0:T(8,128)(2,1)} %copy-done.7, bf16[128,1536]{1,0:T(8,128)(2,1)} %copy-done.8, bf16[1536,384]{1,0:T(8,128)(2,1)} %down_ref.3), custom_call_target="tpu_custom_call" | custom-call | tf_op jit(solution)/shard_map/pallas_call | solution.py:168
  167.3 3.1 %collective-permute-done.4.upper_ref.refs_15_ = bf16[64,1536]{1,0:T(8,128)(2,1)S(1)} collective-permute-done((bf16[64,1536]{1,0:T(8,128)(2,1)S(1)}, bf16[64,1536]{1,0:T(8,128)(2,1)S(1)}, u32[]{:S(2)}, u32[]{:S(2)}) %collective-permute-start.4) | collective-permute-done | bytes 196640 | tf_op jit(solution)/shard_map/ppermute | solution.py:46
  170.4 0.7 copy-done.20
  171.0 2.7 %shard_map.93 = bf16[16,32,384]{2,1,0:T(8,128)(2,1)} custom-call(s32[1]{0:T(128)} %bitcast.x_ref, bf16[64,1536]{1,0:T(8,128)(2,1)} %copy-done.20, bf16[64,1536]{1,0:T(8,128)(2,1)} %copy-done.19, bf16[16,32,384]{2,1,0:T(8,128)(2,1)} %shard_map.92.near_ref, bf16[1536,384]{1,0:T(8,128)(2,1)} %down_ref.3), custom_call_target="tpu_custom_call" | custom-call | tf_op jit(solution)/shard_map/pallas_call | solution.py:168
  173.8 6.5 %all-to-all-start.3 = ((bf16[16,32,384]{2,1,0:T(8,128)(2,1)}), bf16[16,32,384]{2,1,0:T(8,128)(2,1)S(1)}, u32[]{:S(2)}, u32[]{:S(2)}) async-start(bf16[16,32,384]{2,1,0:T(8,128)(2,1)} %shard_map.93), calls=%async_computation.3 | async-start | bytes 786432 | tf_op jit(solution)/shard_map/all_to_all | solution.py:274
  180.3 1.9 collective-permute-start.11
  182.2 4.6 %collective-permute-start.10 = (bf16[128,1664]{1,0:T(8,128)(2,1)S(1)}, bf16[128,1664]{1,0:T(8,128)(2,1)S(1)}, u32[]{:S(2)}, u32[]{:S(2)}) collective-permute-start(bf16[128,1664]{1,0:T(8,128)(2,1)S(1)} %bitcast.172), channel_id=1, source_target_pairs={{0,24},{1,25},{2,26},{3,27},{4,28},{5,29},{6,30},{7,31},{8,0},{9,1... | collective-permute-start | bytes 1277960 | tf_op jit(solution)/shard_map/ppermute | solution.py:46
  186.8 7.9 %collective-permute-done.11.refs_4_.refs_12_ = bf16[128,1664]{1,0:T(8,128)(2,1)S(1)} collective-permute-done((bf16[128,1664]{1,0:T(8,128)(2,1)S(1)}, bf16[128,1664]{1,0:T(8,128)(2,1)S(1)}, u32[]{:S(2)}, u32[]{:S(2)}) %collective-permute-start.11) | collective-permute-done | bytes 426016 | tf_op jit(solution)/shard_map/ppermute | solution.py:46
  194.7 1.9 collective-permute-start.12
  196.6 4.6 %collective-permute-start.13 = (bf16[64,1664]{1,0:T(8,128)(2,1)S(1)}, bf16[64,1664]{1,0:T(8,128)(2,1)S(1)}, u32[]{:S(2)}, u32[]{:S(2)}) collective-permute-start(bf16[64,1664]{1,0:T(8,128)(2,1)S(1)} %slice.517), channel_id=1, source_target_pairs={{0,24},{1,25},{2,26},{3,27},{4,28},{5,29},{6,30},{7,31},{8,0},{9,1... | collective-permute-start | bytes 638984 | tf_op jit(solution)/shard_map/ppermute | solution.py:46
  201.2 0.6 broadcast_in_dim.92.refs_8_
  201.8 1.8 collective-permute-done.12.refs_2_.refs_10_
  203.6 0.9 collective-permute-done.13.refs_3_.refs_11_
  204.6 0.7 copy-done.18
  205.3 4.5 %shard_map.94 = bf16[16,32,512]{2,1,0:T(8,128)(2,1)} custom-call(s32[1]{0:T(128)} %bitcast.x_ref, bf16[128,1664]{1,0:T(8,128)(2,1)} %bitcast.173, bf16[128,1664]{1,0:T(8,128)(2,1)} %copy-done.6, bf16[64,1664]{1,0:T(8,128)(2,1)} %copy-done.17, bf16[64,1664]{1,0:T(8,128)(2,1)} %copy-done.18, bf16[128,1664]{1,0:T(8,128)(2,1)} %copy-done.5, ...), custom_call_target="tpu_custom_call" | custom-call | tf_op jit(solution)/shard_map/pallas_call | solution.py:168
  209.7 8.7 %all-to-all-start.6 = ((bf16[16,32,512]{2,1,0:T(8,128)(2,1)}), bf16[16,32,512]{2,1,0:T(8,128)(2,1)S(1)}, u32[]{:S(2)}, u32[]{:S(2)}) async-start(bf16[16,32,512]{2,1,0:T(8,128)(2,1)} %shard_map.94), calls=%async_computation.6 | async-start | bytes 1048576 | tf_op jit(solution)/shard_map/all_to_all | solution.py:269
  218.4 0.9 dynamic-slice_reduce_fusion
  219.4 4.8 %shard_map.95 = (bf16[384,1536]{1,0:T(8,128)(2,1)}, bf16[1536,384]{1,0:T(8,128)(2,1)}) custom-call(s32[1]{0:T(128)} %bitcast.x_ref, bf16[128,384]{1,0:T(8,128)(2,1)} %bitcast.188, bf16[128,384]{1,0:T(8,128)(2,1)} %bitcast.192, bf16[128,384]{1,0:T(8,128)(2,1)} %bitcast.194, bf16[128,384]{1,0:T(8,128)(2,1)} %bitcast.190, bf16[128,384]{1,0:T(8,128)(2,1)} %bitcast.179, ...), custom_call_target="tpu_custom_call" | custom-call | tf_op jit(solution)/shard_map/pallas_call | solution.py:168
  224.3 0.6 fusion.25
  224.9 10.7 %all-to-all-done.6 = bf16[16,32,512]{2,1,0:T(8,128)(2,1)S(1)} async-done(((bf16[16,32,512]{2,1,0:T(8,128)(2,1)}), bf16[16,32,512]{2,1,0:T(8,128)(2,1)S(1)}, u32[]{:S(2)}, u32[]{:S(2)}) %all-to-all-start.6) | async-done | bytes 524320 | tf_op jit(solution)/shard_map/all_to_all | solution.py:269
  235.6 0.6 reduce_sum.59
  236.3 0.7 fusion.23
  (91 shorter events, 1.2 us)
Async XLA Ops:
  0.6 25.5 %copy-start.1 = (bf16[384,1536]{1,0:T(8,128)(2,1)S(1)}, bf16[384,1536]{1,0:T(8,128)(2,1)}, u32[]{:S(2)}) copy-start(bf16[384,1536]{1,0:T(8,128)(2,1)} %refs_5_.1) | copy-start | bytes 3538948
  25.7 24.3 %copy-start.2 = (bf16[1024,384]{1,0:T(8,128)(2,1)}, bf16[1024,384]{1,0:T(8,128)(2,1)S(1)}, u32[]{:S(2)}) copy-start(bf16[1024,384]{1,0:T(8,128)(2,1)S(1)} %all_gather.3) | copy-start | bytes 2359300
  26.4 12.1 %copy-start = (bf16[1536,384]{1,0:T(8,128)(2,1)S(1)}, bf16[1536,384]{1,0:T(8,128)(2,1)}, u32[]{:S(2)}) copy-start(bf16[1536,384]{1,0:T(8,128)(2,1)} %down_ref.3) | copy-start | bytes 3538948
  27.2 22.6 %all-to-all-start = ((f32[32,20,128]{2,1,0:T(8,128)}), f32[32,20,128]{2,1,0:T(8,128)S(1)}, u32[]{:S(2)}, u32[]{:S(2)}) async-start(f32[32,20,128]{2,1,0:T(8,128)} %broadcast_in_dim.79), calls=%async_computation | async-start | bytes 786432 | tf_op jit(solution)/shard_map/all_to_all | solution.py:52
  38.5 5.8 %copy-start.10 = (bf16[4,32,384]{2,1,0:T(8,128)(2,1)}, bf16[4,32,384]{2,1,0:T(8,128)(2,1)S(1)}, u32[]{:S(2)}) copy-start(bf16[4,32,384]{2,1,0:T(8,128)(2,1)S(1)} %get-tuple-element.23) | copy-start | bytes 294916
  38.5 5.8 %copy-start.12 = (bf16[4,32,384]{2,1,0:T(8,128)(2,1)}, bf16[4,32,384]{2,1,0:T(8,128)(2,1)S(1)}, u32[]{:S(2)}) copy-start(bf16[4,32,384]{2,1,0:T(8,128)(2,1)S(1)} %get-tuple-element.25) | copy-start | bytes 294916
  39.7 10.3 %copy-start.23 = (f32[384]{0:T(512)S(1)}, f32[384]{0:T(512)}, u32[]{:S(2)}) copy-start(f32[384]{0:T(512)} %param.9) | copy-start | bytes 4612
  39.7 49.4 %collective-permute-start.8 = (bf16[128,1536]{1,0:T(8,128)(2,1)}, bf16[128,1536]{1,0:T(8,128)(2,1)}, u32[]{:S(2)}, u32[]{:S(2)}) collective-permute-start(bf16[128,1536]{1,0:T(8,128)(2,1)} %convolution_convert_fusion.1), channel_id=1, source_target_pairs={{0,8},{1,9},{2,10},{3,11},{4,12},{5,13},{6,14},{7,15},{8,16},{9,17... | collective-permute-start | bytes 1179656 | tf_op jit(solution)/shard_map/ppermute | solution.py:46
  44.3 44.8 %collective-permute-start.7 = (bf16[128,1536]{1,0:T(8,128)(2,1)}, bf16[128,1536]{1,0:T(8,128)(2,1)}, u32[]{:S(2)}, u32[]{:S(2)}) collective-permute-start(bf16[128,1536]{1,0:T(8,128)(2,1)} %convolution_convert_fusion.2), channel_id=1, source_target_pairs={{0,16},{1,17},{2,18},{3,19},{4,20},{5,21},{6,22},{7,23},{8,24},{9,... | collective-permute-start | bytes 1179656 | tf_op jit(solution)/shard_map/ppermute | solution.py:46
  50.3 0.8 copy-start.14
  50.3 0.8 copy-start.15
  50.3 0.8 copy-start.16
  50.3 12.3 %copy-start.13 = (bf16[4,32,384]{2,1,0:T(8,128)(2,1)}, bf16[4,32,384]{2,1,0:T(8,128)(2,1)S(1)}, u32[]{:S(2)}) copy-start(bf16[4,32,384]{2,1,0:T(8,128)(2,1)S(1)} %get-tuple-element.27) | copy-start | bytes 294916
  51.1 11.0 %copy-start.11 = (bf16[4,32,384]{2,1,0:T(8,128)(2,1)S(1)}, bf16[4,32,384]{2,1,0:T(8,128)(2,1)}, u32[]{:S(2)}) copy-start(bf16[4,32,384]{2,1,0:T(8,128)(2,1)} %get-tuple-element.24) | copy-start | bytes 294916
  51.5 22.7 %collective-permute-start = (bf16[128,1536]{1,0:T(8,128)(2,1)S(1)}, bf16[128,1536]{1,0:T(8,128)(2,1)S(1)}, u32[]{:S(2)}, u32[]{:S(2)}) collective-permute-start(bf16[128,1536]{1,0:T(8,128)(2,1)S(1)} %convolution_convert_fusion.6), channel_id=1, source_target_pairs={{0,16},{1,17},{2,18},{3,19},{4,20},{5,21},{6,22},{7,23},{8,24},{9,... | collective-permute-start | bytes 1179656 | tf_op jit(solution)/shard_map/ppermute | solution.py:46
  55.6 27.4 %collective-permute-start.1 = (bf16[128,1536]{1,0:T(8,128)(2,1)S(1)}, bf16[128,1536]{1,0:T(8,128)(2,1)S(1)}, u32[]{:S(2)}, u32[]{:S(2)}) collective-permute-start(bf16[128,1536]{1,0:T(8,128)(2,1)S(1)} %convolution_convert_fusion.5), channel_id=1, source_target_pairs={{0,8},{1,9},{2,10},{3,11},{4,12},{5,13},{6,14},{7,15},{8,16},{9,17... | collective-permute-start | bytes 1179656 | tf_op jit(solution)/shard_map/ppermute | solution.py:46
  57.9 25.1 %collective-permute-start.2 = (bf16[128,1536]{1,0:T(8,128)(2,1)S(1)}, bf16[128,1536]{1,0:T(8,128)(2,1)S(1)}, u32[]{:S(2)}, u32[]{:S(2)}) collective-permute-start(bf16[128,1536]{1,0:T(8,128)(2,1)S(1)} %convolution_convert_fusion.4), channel_id=1, source_target_pairs={{0,24},{1,25},{2,26},{3,27},{4,28},{5,29},{6,30},{7,31},{8,0},{9,1... | collective-permute-start | bytes 1179656 | tf_op jit(solution)/shard_map/ppermute | solution.py:46
  63.0 26.1 %copy-start.9 = (bf16[4,32,384]{2,1,0:T(8,128)(2,1)S(1)}, bf16[4,32,384]{2,1,0:T(8,128)(2,1)}, u32[]{:S(2)}) copy-start(bf16[4,32,384]{2,1,0:T(8,128)(2,1)} %get-tuple-element.26) | copy-start | bytes 294916
  74.2 14.9 %collective-permute-start.9 = (bf16[128,1536]{1,0:T(8,128)(2,1)S(1)}, bf16[128,1536]{1,0:T(8,128)(2,1)S(1)}, u32[]{:S(2)}, u32[]{:S(2)}) collective-permute-start(bf16[128,1536]{1,0:T(8,128)(2,1)S(1)} %convolution_convert_fusion), channel_id=1, source_target_pairs={{0,24},{1,25},{2,26},{3,27},{4,28},{5,29},{6,30},{7,31},{8,0},{9,1... | collective-permute-start | bytes 1179656 | tf_op jit(solution)/shard_map/ppermute | solution.py:46
  83.9 20.2 %all-to-all-start.1 = ((bf16[8,16,1536]{2,1,0:T(8,128)(2,1)}), bf16[8,16,1536]{2,1,0:T(8,128)(2,1)S(1)}, u32[]{:S(2)}, u32[]{:S(2)}) async-start(bf16[8,16,1536]{2,1,0:T(8,128)(2,1)} %bitcast.26), calls=%async_computation.1 | async-start | bytes 786432 | tf_op jit(solution)/shard_map/all_to_all | solution.py:75
  104.1 18.5 %all-to-all-start.4 = ((bf16[8,16,1536]{2,1,0:T(8,128)(2,1)}), bf16[8,16,1536]{2,1,0:T(8,128)(2,1)S(1)}, u32[]{:S(2)}, u32[]{:S(2)}) async-start(bf16[8,16,1536]{2,1,0:T(8,128)(2,1)} %bitcast.36), calls=%async_computation.4 | async-start | bytes 786432 | tf_op jit(solution)/shard_map/all_to_all | solution.py:75
  123.8 18.5 %all-to-all-start.2 = ((bf16[8,16,1536]{2,1,0:T(8,128)(2,1)}), bf16[8,16,1536]{2,1,0:T(8,128)(2,1)S(1)}, u32[]{:S(2)}, u32[]{:S(2)}) async-start(bf16[8,16,1536]{2,1,0:T(8,128)(2,1)} %broadcast_in_dim.83), calls=%async_computation.2 | async-start | bytes 786432 | tf_op jit(solution)/shard_map/all_to_all | solution.py:80
  142.3 21.8 %copy-start.4 = (bf16[8,16,1536]{2,1,0:T(8,128)(2,1)}, bf16[8,16,1536]{2,1,0:T(8,128)(2,1)S(1)}, u32[]{:S(2)}) copy-start(bf16[8,16,1536]{2,1,0:T(8,128)(2,1)S(1)} %all-to-all-done.2) | copy-start | bytes 1179652
  143.1 30.6 %all-to-all-start.5 = ((bf16[8,16,1664]{2,1,0:T(8,128)(2,1)}), bf16[8,16,1664]{2,1,0:T(8,128)(2,1)S(1)}, u32[]{:S(2)}, u32[]{:S(2)}) async-start(bf16[8,16,1664]{2,1,0:T(8,128)(2,1)} %broadcast_in_dim.91), calls=%async_computation.5 | async-start | bytes 851968 | tf_op jit(solution)/shard_map/all_to_all | solution.py:80
  146.6 12.1 %collective-permute-start.5 = (bf16[128,1536]{1,0:T(8,128)(2,1)S(1)}, bf16[128,1536]{1,0:T(8,128)(2,1)S(1)}, u32[]{:S(2)}, u32[]{:S(2)}) collective-permute-start(bf16[128,1536]{1,0:T(8,128)(2,1)S(1)} %bitcast.175), channel_id=1, source_target_pairs={{0,24},{1,25},{2,26},{3,27},{4,28},{5,29},{6,30},{7,31},{8,0},{9,1... | collective-permute-start | bytes 1179656 | tf_op jit(solution)/shard_map/ppermute | solution.py:46
  148.5 13.6 %collective-permute-start.3 = (bf16[128,1536]{1,0:T(8,128)(2,1)S(1)}, bf16[128,1536]{1,0:T(8,128)(2,1)S(1)}, u32[]{:S(2)}, u32[]{:S(2)}) collective-permute-start(bf16[128,1536]{1,0:T(8,128)(2,1)S(1)} %bitcast.176), channel_id=1, source_target_pairs={{0,8},{1,9},{2,10},{3,11},{4,12},{5,13},{6,14},{7,15},{8,16},{9,17... | collective-permute-start | bytes 1179656 | tf_op jit(solution)/shard_map/ppermute | solution.py:46
  158.7 5.4 %copy-start.7 = (bf16[128,1536]{1,0:T(8,128)(2,1)}, bf16[128,1536]{1,0:T(8,128)(2,1)S(1)}, u32[]{:S(2)}) copy-start(bf16[128,1536]{1,0:T(8,128)(2,1)S(1)} %collective-permute-done.5.after_ref.refs_14_) | copy-start | bytes 1179652
  158.7 8.6 %collective-permute-start.6 = (bf16[64,1536]{1,0:T(8,128)(2,1)S(1)}, bf16[64,1536]{1,0:T(8,128)(2,1)S(1)}, u32[]{:S(2)}, u32[]{:S(2)}) collective-permute-start(bf16[64,1536]{1,0:T(8,128)(2,1)S(1)} %slice.490), channel_id=1, source_target_pairs={{0,24},{1,25},{2,26},{3,27},{4,28},{5,29},{6,30},{7,31},{8,0},{9,1... | collective-permute-start | bytes 589832 | tf_op jit(solution)/shard_map/ppermute | solution.py:46
  162.1 2.0 copy-start.8
  162.1 8.2 %collective-permute-start.4 = (bf16[64,1536]{1,0:T(8,128)(2,1)S(1)}, bf16[64,1536]{1,0:T(8,128)(2,1)S(1)}, u32[]{:S(2)}, u32[]{:S(2)}) collective-permute-start(bf16[64,1536]{1,0:T(8,128)(2,1)S(1)} %slice.489), channel_id=1, source_target_pairs={{0,8},{1,9},{2,10},{3,11},{4,12},{5,13},{6,14},{7,15},{8,16},{9,17... | collective-permute-start | bytes 589832 | tf_op jit(solution)/shard_map/ppermute | solution.py:46
  167.3 3.1 %copy-start.19 = (bf16[64,1536]{1,0:T(8,128)(2,1)}, bf16[64,1536]{1,0:T(8,128)(2,1)S(1)}, u32[]{:S(2)}) copy-start(bf16[64,1536]{1,0:T(8,128)(2,1)S(1)} %collective-permute-done.6.lower_ref.refs_16_) | copy-start | bytes 589828
  170.4 0.7 copy-start.20
  173.8 30.8 %copy-start.3 = (bf16[8,16,1664]{2,1,0:T(8,128)(2,1)}, bf16[8,16,1664]{2,1,0:T(8,128)(2,1)S(1)}, u32[]{:S(2)}) copy-start(bf16[8,16,1664]{2,1,0:T(8,128)(2,1)S(1)} %all-to-all-done.5) | copy-start | bytes 1277956
  173.8 36.0 %all-to-all-start.3 = ((bf16[16,32,384]{2,1,0:T(8,128)(2,1)}), bf16[16,32,384]{2,1,0:T(8,128)(2,1)S(1)}, u32[]{:S(2)}, u32[]{:S(2)}) async-start(bf16[16,32,384]{2,1,0:T(8,128)(2,1)} %shard_map.93), calls=%async_computation.3 | async-start | bytes 786432 | tf_op jit(solution)/shard_map/all_to_all | solution.py:274
  180.3 14.4 %collective-permute-start.11 = (bf16[128,1664]{1,0:T(8,128)(2,1)S(1)}, bf16[128,1664]{1,0:T(8,128)(2,1)S(1)}, u32[]{:S(2)}, u32[]{:S(2)}) collective-permute-start(bf16[128,1664]{1,0:T(8,128)(2,1)S(1)} %bitcast.171), channel_id=1, source_target_pairs={{0,8},{1,9},{2,10},{3,11},{4,12},{5,13},{6,14},{7,15},{8,16},{9,17... | collective-permute-start | bytes 1277960 | tf_op jit(solution)/shard_map/ppermute | solution.py:46
  182.2 14.4 %collective-permute-start.10 = (bf16[128,1664]{1,0:T(8,128)(2,1)S(1)}, bf16[128,1664]{1,0:T(8,128)(2,1)S(1)}, u32[]{:S(2)}, u32[]{:S(2)}) collective-permute-start(bf16[128,1664]{1,0:T(8,128)(2,1)S(1)} %bitcast.172), channel_id=1, source_target_pairs={{0,24},{1,25},{2,26},{3,27},{4,28},{5,29},{6,30},{7,31},{8,0},{9,1... | collective-permute-start | bytes 1277960 | tf_op jit(solution)/shard_map/ppermute | solution.py:46
  194.6 9.9 %copy-start.5 = (bf16[128,1664]{1,0:T(8,128)(2,1)}, bf16[128,1664]{1,0:T(8,128)(2,1)S(1)}, u32[]{:S(2)}) copy-start(bf16[128,1664]{1,0:T(8,128)(2,1)S(1)} %collective-permute-done.11.refs_4_.refs_12_) | copy-start | bytes 1277956
  194.7 8.9 %collective-permute-start.12 = (bf16[64,1664]{1,0:T(8,128)(2,1)S(1)}, bf16[64,1664]{1,0:T(8,128)(2,1)S(1)}, u32[]{:S(2)}, u32[]{:S(2)}) collective-permute-start(bf16[64,1664]{1,0:T(8,128)(2,1)S(1)} %slice.516), channel_id=1, source_target_pairs={{0,8},{1,9},{2,10},{3,11},{4,12},{5,13},{6,14},{7,15},{8,16},{9,17... | collective-permute-start | bytes 638984 | tf_op jit(solution)/shard_map/ppermute | solution.py:46
  196.6 8.0 %copy-start.6 = (bf16[128,1664]{1,0:T(8,128)(2,1)}, bf16[128,1664]{1,0:T(8,128)(2,1)S(1)}, u32[]{:S(2)}) copy-start(bf16[128,1664]{1,0:T(8,128)(2,1)S(1)} %collective-permute-done.10.refs_1_.refs_9_) | copy-start | bytes 1277956
  196.6 7.9 %collective-permute-start.13 = (bf16[64,1664]{1,0:T(8,128)(2,1)S(1)}, bf16[64,1664]{1,0:T(8,128)(2,1)S(1)}, u32[]{:S(2)}, u32[]{:S(2)}) collective-permute-start(bf16[64,1664]{1,0:T(8,128)(2,1)S(1)} %slice.517), channel_id=1, source_target_pairs={{0,24},{1,25},{2,26},{3,27},{4,28},{5,29},{6,30},{7,31},{8,0},{9,1... | collective-permute-start | bytes 638984 | tf_op jit(solution)/shard_map/ppermute | solution.py:46
  203.6 1.0 copy-start.17
  204.6 0.7 copy-start.18
  209.7 25.9 %all-to-all-start.6 = ((bf16[16,32,512]{2,1,0:T(8,128)(2,1)}), bf16[16,32,512]{2,1,0:T(8,128)(2,1)S(1)}, u32[]{:S(2)}, u32[]{:S(2)}) async-start(bf16[16,32,512]{2,1,0:T(8,128)(2,1)} %shard_map.94), calls=%async_computation.6 | async-start | bytes 1048576 | tf_op jit(solution)/shard_map/all_to_all | solution.py:269
  219.4 4.9 %copy-start.21 = (bf16[2,16,384]{2,1,0:T(8,128)(2,1)S(1)}, bf16[2,16,384]{2,1,0:T(8,128)(2,1)}, u32[]{:S(2)}) copy-start(bf16[2,16,384]{2,1,0:T(8,128)(2,1)} %param.5) | copy-start | bytes 73732
  224.2 12.1 %copy-start.22 = (bf16[2,16,384]{2,1,0:T(8,128)(2,1)S(1)}, bf16[2,16,384]{2,1,0:T(8,128)(2,1)}, u32[]{:S(2)}) copy-start(bf16[2,16,384]{2,1,0:T(8,128)(2,1)} %param.6) | copy-start | bytes 73732
